TPU v7x, 32 devices: a whole 2x2x4 slice. The times are simulated.
32 devices in a mesh: ty: 4 (over x, core), tx: 8 (over z, y).
Axes of the slice: x: 2, y: 2, z: 4, core: 2. Of those that a mesh axis runs over, the one named last changes fastest.
Arguments:
- velocity: float32 [2, 3, 512, 1024], P(None, None, 'ty', 'tx'), may hold values from -6 to 6
- start_position: float32 [2, 16384], P(None, ('ty', 'tx')), may hold values from 0 to 128, as said below
- cells: int32 [2, 4, 2, 16384], P(None, None, None, ('ty', 'tx')), may hold values from -1 to 127, as said below
- history: float32 [2, 71, 16384], P(None, None, ('ty', 'tx')), may hold values from -6 to 6
- leavers: int32 [1, 8], replicated, may hold values from 1 to 16, as said below
- owner: int32 [16384, 1], P(('ty', 'tx')), may hold values from 0 to 31; in each aligned block of 512 rows (0 to 511, 512 to 1023, ...) at most 64 rows name the same one
- filter_matrix: float32 [73, 73], replicated, may hold values from -0.75 to 0.75
Outputs:
- filtered: float32 [2, 73, 65536], P(None, None, ('ty', 'tx'))
Inputs may be any that keep to these rules, and one draw needn't show every extreme that they name: `start_position`: coordinates in cell units of the particle's tile. First coordinate cells lie in -1 .. 127 and second in -1 .. 127. Each move has one direction with exactly 16 leavers. Among the 512 slots of one tile no owner appears more than 64 times.
All inputs are finite; a program needn't handle non-finite values.
Results may differ from a plain program's by a relative error of at most 0.0003.
Values sent between devices are 32-bit elements; how exact they have to be, the bound alone decides.
No kernel may reach another device: no remote copies, remote signals or barrier semaphores. Data moves between devices by JAX's collectives and lax.ppermute only.
A program may use at most 64 MiB of HBM per device.

v0:
```python
import jax
import jax.numpy as jnp
from jax import lax
from jax.sharding import PartitionSpec as P

STEPS = 2
SAMPLES = 73
HISTORY = 71
MOST = 16


drift = 0.2
moves = ((-1, -1), (-1, 0), (-1, 1), (0, -1), (0, 1), (1, -1), (1, 0), (1, 1))


def shifted(value, axis, by):
    peers = lax.axis_size(axis)
    return lax.ppermute(value, axis, [(i, (i + by) % peers) for i in range(peers)])


def padded_2(block, sides, width):
    for axis, dim in sides:
        count = lax.axis_size(axis)
        forward = [(i, i + 1) for i in range(count - 1)]
        forward.append((count - 1, 0))
        backward = [(target, source) for source, target in forward]
        low = lax.ppermute(
            lax.slice_in_dim(block, block.shape[dim] - width, None, axis=dim), axis, forward
        )
        high = lax.ppermute(lax.slice_in_dim(block, 0, width, axis=dim), axis, backward)
        block = jnp.concatenate([low, block, high], axis=dim)
    return block


def stacked_corners(plane, width):
    extent = plane.shape[1]
    widened = jnp.pad(plane, ((0, 0), (0, width + 1)))
    pieces = [widened[:, offset : offset + extent] for offset in (0, 1, width, width + 1)]
    return jnp.concatenate(pieces, axis=0)


def bilinear(corner_table, point, cell, width):
    corner = (cell[0] + 1) * width + cell[1] + 1
    wy = point[0] - cell[0].astype(jnp.float32)
    wx = point[1] - cell[1].astype(jnp.float32)
    gathered = jnp.take(corner_table, corner, axis=1)
    first = gathered[0:2]
    second = gathered[2:4]
    third = gathered[4:6]
    fourth = gathered[6:8]
    return (1.0 - wy) * ((1.0 - wx) * first + wx * second) + wy * ((1.0 - wx) * third + wx * fourth)


def apply_filter(filter_matrix, columns):
    shaped = columns.reshape(2, SAMPLES, -1)
    return jnp.einsum("tj,cjn->ctn", filter_matrix, shaped, precision=lax.Precision.HIGHEST)


def migrate(record, counts, step, tile_rows, tile_cols):
    band = step * 8 * MOST
    offsets = jnp.cumsum(counts) - counts
    starts = [band + offsets[j] for j in range(8)]
    blocks = [lax.dynamic_slice_in_dim(record, starts[j], MOST, 1) for j in range(8)]
    after_cols = list(blocks)
    for sign, members in ((1, (2, 4, 7)), (-1, (0, 3, 5))):
        stacked = jnp.stack([blocks[j] for j in members])
        arrived = shifted(stacked, "tx", sign)
        for number, j in enumerate(members):
            after_cols[j] = arrived[number]
    moved = list(after_cols)
    for sign, members in ((-1, (0, 1, 2)), (1, (5, 6, 7))):
        stacked = jnp.stack([after_cols[j] for j in members])
        arrived = shifted(stacked, "ty", sign)
        for number, j in enumerate(members):
            moved[j] = arrived[number]
    keep = lax.broadcasted_iota(jnp.int32, (1, MOST), 1)
    for j in range(8):
        dy, dx = moves[j]
        piece = moved[j].at[0].add(-dy * tile_rows).at[1].add(-dx * tile_cols)
        current = lax.dynamic_slice_in_dim(record, starts[j], MOST, 1)
        merged = jnp.where(keep < counts[j], piece, current)
        record = lax.dynamic_update_slice_in_dim(record, merged, starts[j], 1)
    return record


def per_device(velocity, start_position, cells, history, leavers, owner, filter_matrix):
    tile_rows = velocity.shape[2]
    tile_cols = velocity.shape[3]
    slots = start_position.shape[1]
    padded = padded_2(velocity, (("ty", 2), ("tx", 3)), 1)
    width = tile_cols + 2
    planes = [padded[:, a].reshape(2, (tile_rows + 2) * width) for a in range(STEPS + 1)]
    snapshot_tables = [stacked_corners(plane, width) for plane in planes]
    halfway_tables = [
        stacked_corners(0.5 * (planes[a] + planes[a + 1]), width) for a in range(STEPS)
    ]
    series = jnp.concatenate([history, jnp.zeros((2, STEPS, slots), jnp.float32)], axis=1)
    record = jnp.concatenate([start_position, series.reshape(2 * SAMPLES, slots)], axis=0)
    for step in range(STEPS):
        point = record[0:2]
        section_cells = cells[step]
        k_one = bilinear(snapshot_tables[step], point, section_cells[0], width)
        spot = point + 0.5 * drift * k_one
        k_two = bilinear(halfway_tables[step], spot, section_cells[1], width)
        spot = point + 0.5 * drift * k_two
        k_three = bilinear(halfway_tables[step], spot, section_cells[2], width)
        spot = point + drift * k_three
        k_four = bilinear(snapshot_tables[step + 1], spot, section_cells[3], width)
        point = point + drift / 6.0 * (k_one + 2.0 * k_two + 2.0 * k_three + k_four)
        record = record.at[0:2].set(point)
        record = record.at[2 + HISTORY + step].set(k_one[0])
        record = record.at[2 + SAMPLES + HISTORY + step].set(k_one[1])
        if step < STEPS - 1:
            record = migrate(record, leavers[step], step, float(tile_rows), float(tile_cols))
    columns = record[2:]
    tile_count = lax.axis_size("ty") * lax.axis_size("tx")
    per_owner = 4 * slots // tile_count
    owned = owner[:, 0]
    labels = jnp.arange(tile_count, dtype=jnp.int32)[:, None]
    onehot = (owned[None, :] == labels).astype(jnp.int32)
    running = jnp.cumsum(onehot, axis=1)
    ranks = jnp.sum(running * onehot, axis=0) - 1
    target = owned * per_owner + ranks
    outgoing = (
        jnp.zeros((2 * SAMPLES, tile_count * per_owner), jnp.float32).at[:, target].set(columns)
    )
    arrived = lax.all_to_all(outgoing, ("ty", "tx"), split_axis=1, concat_axis=1, tiled=True)
    return apply_filter(filter_matrix, arrived)


def solution(mesh):
    placed = (
        P(None, None, "ty", "tx"),
        P(None, ("ty", "tx")),
        P(None, None, None, ("ty", "tx")),
        P(None, None, ("ty", "tx")),
        P(),
        P(("ty", "tx"), None),
        P(),
    )
    return jax.shard_map(
        per_device,
        mesh=mesh,
        in_specs=placed,
        out_specs=P(None, None, ("ty", "tx")),
        check_vma=False,
    )
```

profile of v0, /device:TPU:0, one launch (start us, length us, event | category | flops | bytes accessed | tf_op | source)
XLA Modules:
  0.0 192.3 jit_solution(15597713260034983692)
XLA Ops:
  1.3 2.0 %collective-permute-start.1 = (f32[2,3,1,128]{3,2,1,0:T(1,128)S(1)}, f32[2,3,1,128]{3,2,1,0:T(1,128)S(1)}, u32[]{:S(2)}, u32[]{:S(2)}) collective-permute-start(f32[2,3,1,128]{3,2,1,0:T(1,128)S(1)} %get-tuple-element.320), channel_id=1, source_target_pairs={{8,0},{16,8},{24,16},{0,24},{9,1},{17,9},{25,17},{1,25},{10,2},{18... | collective-permute-start | bytes 9224 | tf_op jit(solution)/shard_map/ppermute | solution.py:30
  5.1 1.0 copy.257
  12.3 1.2 reduce-window.19
  14.7 2.3 %collective-permute-start.2 = (f32[2,3,130,1]{3,2,1,0:T(8,128)S(1)}, f32[2,3,130,1]{3,2,1,0:T(8,128)S(1)}, u32[]{:S(2)}, u32[]{:S(2)}) collective-permute-start(f32[2,3,130,1]{3,2,1,0:T(8,128)S(1)} %get-tuple-element.317), channel_id=1, source_target_pairs={{0,1},{1,2},{2,3},{3,4},{4,5},{5,6},{6,7},{7,0},{8,9},{9,10},{10,1... | collective-permute-start | bytes 9368 | tf_op jit(solution)/shard_map/ppermute | solution.py:27
  17.1 3.1 %collective-permute-start.3 = (f32[2,3,130,1]{3,2,1,0:T(8,128)S(1)}, f32[2,3,130,1]{3,2,1,0:T(8,128)S(1)}, u32[]{:S(2)}, u32[]{:S(2)}) collective-permute-start(f32[2,3,130,1]{3,2,1,0:T(8,128)S(1)} %get-tuple-element.318), channel_id=1, source_target_pairs={{1,0},{2,1},{3,2},{4,3},{5,4},{6,5},{7,6},{0,7},{9,8},{10,9},{11,1... | collective-permute-start | bytes 9368 | tf_op jit(solution)/shard_map/ppermute | solution.py:30
  35.8 1.4 collective-permute-done.3
  38.5 1.4 add_multiply_fusion
  40.9 5.4 %copy.223 = f32[8,16900]{0,1:T(8,128)} copy(f32[8,16900]{1,0:T(8,128)S(1)} %get-tuple-element.424) | data formatting | bytes 1081600 | tf_op jit(solution)/shard_map/concatenate | solution.py:39
  46.3 4.5 %gather_fusion = f32[512,8]{1,0:T(8,128)S(1)} fusion(f32[8,16900]{0,1:T(8,128)} %copy.223, s32[1024]{0:T(1024)S(1)} %pad_clamp_fusion.7), kind=kCustom, calls=%fused_computation.clone | custom fusion | bytes 34816 | tf_op jit(solution)/shard_map/jit(_take)/gather | solution.py:46
  51.0 5.4 %copy.225 = f32[8,16900]{0,1:T(8,128)} copy(f32[8,16900]{1,0:T(8,128)S(1)} %get-tuple-element.425) | data formatting | bytes 1081600 | tf_op jit(solution)/shard_map/concatenate | solution.py:39
  56.4 4.5 %gather_fusion.1 = f32[512,8]{1,0:T(8,128)S(1)} fusion(f32[8,16900]{0,1:T(8,128)} %copy.225, s32[1024]{0:T(1024)S(1)} %pad_clamp_fusion.6), kind=kCustom, calls=%fused_computation.1.clone | custom fusion | bytes 34816 | tf_op jit(solution)/shard_map/jit(_take)/gather | solution.py:46
  61.0 4.5 %gather_fusion.2 = f32[512,8]{1,0:T(8,128)S(1)} fusion(f32[8,16900]{0,1:T(8,128)} %copy.225, s32[1024]{0:T(1024)S(1)} %pad_clamp_fusion.5), kind=kCustom, calls=%fused_computation.2.clone | custom fusion | bytes 34816 | tf_op jit(solution)/shard_map/jit(_take)/gather | solution.py:46
  66.6 5.4 %copy.229 = f32[8,16900]{0,1:T(8,128)} copy(f32[8,16900]{1,0:T(8,128)S(1)} %get-tuple-element.426) | data formatting | bytes 1081600 | tf_op jit(solution)/shard_map/concatenate | solution.py:39
  72.0 4.5 %gather_fusion.3 = f32[512,8]{1,0:T(8,128)S(1)} fusion(f32[8,16900]{0,1:T(8,128)} %copy.229, s32[1024]{0:T(1024)S(1)} %pad_clamp_fusion.4), kind=kCustom, calls=%fused_computation.3.clone | custom fusion | bytes 34816 | tf_op jit(solution)/shard_map/jit(_take)/gather | solution.py:46
  77.4 3.4 %collective-permute-start.4 = (f32[3,148,16]{2,1,0:T(8,128)S(1)}, f32[3,148,16]{2,1,0:T(8,128)S(1)}, u32[]{:S(2)}, u32[]{:S(2)}) collective-permute-start(f32[3,148,16]{2,1,0:T(8,128)S(1)} %copy.234), channel_id=1, source_target_pairs={{0,7},{1,0},{2,1},{3,2},{4,3},{5,4},{6,5},{7,6},{8,15},{9,8},{10,9... | collective-permute-start | bytes 85256 | tf_op jit(solution)/shard_map/ppermute | solution.py:18
  81.4 4.5 %gather_fusion.4 = f32[512,8]{1,0:T(8,128)S(1)} fusion(f32[8,16900]{0,1:T(8,128)} %copy.229, s32[1024]{0:T(1024)S(1)} %pad_clamp_fusion.3), kind=kCustom, calls=%fused_computation.4.clone | custom fusion | bytes 34816 | tf_op jit(solution)/shard_map/jit(_take)/gather | solution.py:46
  86.0 5.4 %copy.245 = f32[8,16900]{0,1:T(8,128)} copy(f32[8,16900]{1,0:T(8,128)S(1)} %get-tuple-element.427) | data formatting | bytes 1081600 | tf_op jit(solution)/shard_map/concatenate | solution.py:39
  91.4 4.5 %gather_fusion.5 = f32[512,8]{1,0:T(8,128)S(1)} fusion(f32[8,16900]{0,1:T(8,128)} %copy.245, s32[1024]{0:T(1024)S(1)} %pad_clamp_fusion.2), kind=kCustom, calls=%fused_computation.5.clone | custom fusion | bytes 34816 | tf_op jit(solution)/shard_map/jit(_take)/gather | solution.py:46
  96.0 4.5 %gather_fusion.6 = f32[512,8]{1,0:T(8,128)S(1)} fusion(f32[8,16900]{0,1:T(8,128)} %copy.245, s32[1024]{0:T(1024)S(1)} %pad_clamp_fusion.1), kind=kCustom, calls=%fused_computation.6.clone | custom fusion | bytes 34816 | tf_op jit(solution)/shard_map/jit(_take)/gather | solution.py:46
  100.8 5.4 %copy.249 = f32[8,16900]{0,1:T(8,128)} copy(f32[8,16900]{1,0:T(8,128)S(1)} %pad_maximum_fusion.5) | data formatting | bytes 1081600 | tf_op jit(solution)/shard_map/concatenate | solution.py:39
  106.2 4.5 %gather_fusion.7 = f32[512,8]{1,0:T(8,128)S(1)} fusion(f32[8,16900]{0,1:T(8,128)} %copy.249, s32[1024]{0:T(1024)S(1)} %pad_clamp_fusion), kind=kCustom, calls=%fused_computation.7.clone | custom fusion | bytes 34816 | tf_op jit(solution)/shard_map/jit(_take)/gather | solution.py:46
  111.2 1.8 collective-permute-start.6
  113.0 4.9 %collective-permute-done.7 = f32[3,148,16]{2,1,0:T(8,128)S(1)} collective-permute-done((f32[3,148,16]{2,1,0:T(8,128)S(1)}, f32[3,148,16]{2,1,0:T(8,128)S(1)}, u32[]{:S(2)}, u32[]{:S(2)}) %collective-permute-start.7) | collective-permute-done | bytes 28448 | tf_op jit(solution)/shard_map/ppermute | solution.py:18
  119.4 1.0 dynamic_update_slice.25
  120.5 1.0 dynamic_update_slice.26
  121.5 1.0 dynamic_update_slice.27
  124.8 1.0 dynamic_update_slice.30
  127.4 2.8 %scatter_custom_fusion = f32[146,2048]{0,1:T(8,128)S(1)} fusion(s32[512]{0:T(512)S(1)} %bitcast.239, f32[512,146]{1,0:T(8,128)S(1)} %copy.251, f32[]{:T(128)} %constant.530.clone.1), kind=kCustom, calls=%fused_computation.11 | custom fusion | bytes 1196036 | tf_op jit(solution)/shard_map/scatter | solution.py:125
  130.1 55.1 %all_to_all.9 = f32[146,32,64]{0,2,1:T(8,128)} all-to-all(f32[146,32,64]{0,2,1:T(8,128)S(1)} %bitcast.180), channel_id=1, replica_groups=mesh['ty'=4,'tx'=8] {'ty','tx'}, dimensions={1} | all-to-all | bytes 2392064 | tf_op jit(solution)/shard_map/all_to_all | solution.py:127
  185.3 2.6 %reshape.1050 = f32[2,73,2048]{1,0,2:T(2,128)S(1)} reshape(f32[146,32,64]{0,2,1:T(8,128)} %all_to_all.9) | data formatting | bytes 2392064 | tf_op jit(solution)/shard_map/reshape | solution.py:55
  187.9 2.5 %convolution_bitcast_fusion = f32[2,73,2048]{2,1,0:T(8,128)S(1)} fusion(f32[2,73,2048]{1,0,2:T(2,128)S(1)} %reshape.1050, f32[73,73]{1,0:T(8,128)S(1)} %copy-done), kind=kOutput, calls=%fused_computation.9 | convolution fusion | flops 261931008 | bytes 2413380 | tf_op jit(solution)/shard_map/tj,cjn->ctn/dot_general | solution.py:56
  190.4 1.9 %copy.253 = f32[2,73,2048]{2,0,1:T(2,128)} copy(f32[2,73,2048]{2,1,0:T(8,128)S(1)} %convolution_bitcast_fusion) | data formatting | bytes 2392064 | tf_op jit(solution)/shard_map/tj,cjn->ctn/transpose | solution.py:56
  (170 shorter events, 22.4 us)
Async XLA Ops:
  0.0 187.9 %copy-start = (f32[73,73]{1,0:T(8,128)S(1)}, f32[73,73]{1,0:T(8,128)}, u32[]{:S(2)}) copy-start(f32[73,73]{1,0:T(8,128)} %param.59) | copy-start | bytes 63952
  0.0 14.5 %copy-start.1 = (f32[2,3,128,128]{3,2,1,0:T(8,128)S(1)}, f32[2,3,128,128]{3,2,1,0:T(8,128)}, u32[]{:S(2)}) copy-start(f32[2,3,128,128]{3,2,1,0:T(8,128)} %param.53) | copy-start | bytes 1179652
  0.0 7.0 %copy-start.4 = (s32[1,8]{1,0:T(1,128)S(1)}, s32[1,8]{1,0:T(1,128)}, u32[]{:S(2)}) copy-start(s32[1,8]{1,0:T(1,128)} %param.57) | copy-start | bytes 100
  0.0 12.3 %copy-start.5 = (s32[512,1]{0,1:T(1,128)S(1)}, s32[512,1]{0,1:T(1,128)}, u32[]{:S(2)}) copy-start(s32[512,1]{0,1:T(1,128)} %param.58) | copy-start | bytes 6148
  0.8 13.6 %collective-permute-start = (f32[2,3,1,128]{3,2,1,0:T(1,128)S(1)}, f32[2,3,1,128]{3,2,1,0:T(1,128)S(1)}, u32[]{:S(2)}, u32[]{:S(2)}) collective-permute-start(f32[2,3,1,128]{3,2,1,0:T(1,128)S(1)} %get-tuple-element.319), channel_id=1, source_target_pairs={{0,8},{8,16},{16,24},{24,0},{1,9},{9,17},{17,25},{25,1},{2,10},{10... | collective-permute-start | bytes 9224 | tf_op jit(solution)/shard_map/ppermute | solution.py:27
  1.3 13.2 %collective-permute-start.1 = (f32[2,3,1,128]{3,2,1,0:T(1,128)S(1)}, f32[2,3,1,128]{3,2,1,0:T(1,128)S(1)}, u32[]{:S(2)}, u32[]{:S(2)}) collective-permute-start(f32[2,3,1,128]{3,2,1,0:T(1,128)S(1)} %get-tuple-element.320), channel_id=1, source_target_pairs={{8,0},{16,8},{24,16},{0,24},{9,1},{17,9},{25,17},{1,25},{10,2},{18... | collective-permute-start | bytes 9224 | tf_op jit(solution)/shard_map/ppermute | solution.py:30
  14.7 21.0 %collective-permute-start.2 = (f32[2,3,130,1]{3,2,1,0:T(8,128)S(1)}, f32[2,3,130,1]{3,2,1,0:T(8,128)S(1)}, u32[]{:S(2)}, u32[]{:S(2)}) collective-permute-start(f32[2,3,130,1]{3,2,1,0:T(8,128)S(1)} %get-tuple-element.317), channel_id=1, source_target_pairs={{0,1},{1,2},{2,3},{3,4},{4,5},{5,6},{6,7},{7,0},{8,9},{9,10},{10,1... | collective-permute-start | bytes 9368 | tf_op jit(solution)/shard_map/ppermute | solution.py:27
  17.1 20.1 %collective-permute-start.3 = (f32[2,3,130,1]{3,2,1,0:T(8,128)S(1)}, f32[2,3,130,1]{3,2,1,0:T(8,128)S(1)}, u32[]{:S(2)}, u32[]{:S(2)}) collective-permute-start(f32[2,3,130,1]{3,2,1,0:T(8,128)S(1)} %get-tuple-element.318), channel_id=1, source_target_pairs={{1,0},{2,1},{3,2},{4,3},{5,4},{6,5},{7,6},{0,7},{9,8},{10,9},{11,1... | collective-permute-start | bytes 9368 | tf_op jit(solution)/shard_map/ppermute | solution.py:30
  40.9 10.0 %copy-start.2 = (f32[2,512]{1,0:T(2,128)S(1)}, f32[2,512]{1,0:T(2,128)}, u32[]{:S(2)}) copy-start(f32[2,512]{1,0:T(2,128)} %param.54) | copy-start | bytes 12292
  40.9 10.0 %copy-start.3 = (s32[2,4,2,512]{3,2,1,0:T(2,128)S(1)}, s32[2,4,2,512]{3,2,1,0:T(2,128)}, u32[]{:S(2)}) copy-start(s32[2,4,2,512]{3,2,1,0:T(2,128)} %param.55) | copy-start | bytes 98308
  77.4 33.4 %collective-permute-start.4 = (f32[3,148,16]{2,1,0:T(8,128)S(1)}, f32[3,148,16]{2,1,0:T(8,128)S(1)}, u32[]{:S(2)}, u32[]{:S(2)}) collective-permute-start(f32[3,148,16]{2,1,0:T(8,128)S(1)} %copy.234), channel_id=1, source_target_pairs={{0,7},{1,0},{2,1},{3,2},{4,3},{5,4},{6,5},{7,6},{8,15},{9,8},{10,9... | collective-permute-start | bytes 85256 | tf_op jit(solution)/shard_map/ppermute | solution.py:18
  81.2 29.7 %collective-permute-start.5 = (f32[3,148,16]{2,1,0:T(8,128)S(1)}, f32[3,148,16]{2,1,0:T(8,128)S(1)}, u32[]{:S(2)}, u32[]{:S(2)}) collective-permute-start(f32[3,148,16]{2,1,0:T(8,128)S(1)} %copy.239), channel_id=1, source_target_pairs={{0,1},{1,2},{2,3},{3,4},{4,5},{5,6},{6,7},{7,0},{8,9},{9,10},{10,1... | collective-permute-start | bytes 85256 | tf_op jit(solution)/shard_map/ppermute | solution.py:18
  111.0 7.0 %collective-permute-start.7 = (f32[3,148,16]{2,1,0:T(8,128)S(1)}, f32[3,148,16]{2,1,0:T(8,128)S(1)}, u32[]{:S(2)}, u32[]{:S(2)}) collective-permute-start(f32[3,148,16]{2,1,0:T(8,128)S(1)} %pad_maximum_fusion.9), channel_id=1, source_target_pairs={{0,8},{8,16},{16,24},{24,0},{1,9},{9,17},{17,25},{25,1},{2,10},{10... | collective-permute-start | bytes 85256 | tf_op jit(solution)/shard_map/ppermute | solution.py:18
  111.2 7.0 %collective-permute-start.6 = (f32[3,148,16]{2,1,0:T(8,128)S(1)}, f32[3,148,16]{2,1,0:T(8,128)S(1)}, u32[]{:S(2)}, u32[]{:S(2)}) collective-permute-start(f32[3,148,16]{2,1,0:T(8,128)S(1)} %pad_maximum_fusion.8), channel_id=1, source_target_pairs={{0,24},{8,0},{16,8},{24,16},{1,25},{9,1},{17,9},{25,17},{2,26},{10... | collective-permute-start | bytes 85256 | tf_op jit(solution)/shard_map/ppermute | solution.py:18
where the time goes:
time: 193 us; the launch traced here: 192 us
  local copies, waits for them, and re-layouts  86 us (45%)
  blocking collectives  55.1 us (29%)
  between operations  16 us (8%)
  starting transfers between devices  13.3 us (7%)
  other arithmetic  13.1 us (7%)
  waiting for transfers between devices  6.3 us (3%)
  matrix products  2.46 us (1%)
    all_to_all x1, blocking collectives, per_device(): lax.all_to_all(outgoing, ('ty', 'tx'), split_axis=1, concat_axis=1, tiled...  55.1 us
    gather x16, local copies, waits for them, and re-layouts, bilinear(): gathered = jnp.take(corner_table, corner, axis=1)  36.6 us
    concatenate x5, local copies, waits for them, and re-layouts, stacked_corners(): return jnp.concatenate(pieces, axis=0)  26.9 us
    dynamic_update_slice x8, local copies, waits for them, and re-layouts, migrate(): record = lax.dynamic_update_slice_in_dim(record, merged, starts[j], 1)  7.5 us
    ppermute x4, starting transfers between devices, shifted(): lax.ppermute(value, axis, [(i, (i + by) % peers) for i in range(peers)])  5.43 us
    ppermute x2, starting transfers between devices, padded_2(): lax.ppermute(lax.slice_in_dim(block, 0, width, axis=dim), axis, backward)  5.07 us
    ppermute x4, waiting for transfers between devices, shifted(): lax.ppermute(value, axis, [(i, (i + by) % peers) for i in range(peers)])  4.93 us
    lt x8, other arithmetic, migrate(): merged = jnp.where(keep < counts[j], piece, current)  4.83 us
  transfers between devices with their start and end apart: 8, of which 2 were waited for; matrix products, arithmetic and copies ran while one was open for 22% of the time, Pallas kernels for 0%

commit v1 on v0

v1 whole, which is shorter than its diff:
```python
import functools

import jax
import jax.numpy as jnp
from jax import lax
from jax.experimental import pallas as pl
from jax.experimental.pallas import tpu as pltpu
from jax.sharding import PartitionSpec as P

STEPS = 2
SAMPLES = 73
HISTORY = 71
MOST = 16


drift = 0.2
moves = ((-1, -1), (-1, 0), (-1, 1), (0, -1), (0, 1), (1, -1), (1, 0), (1, 1))
f32 = jnp.float32
bf16 = jnp.bfloat16
LANES = 128


def up(value, to):
    return -(-value // to) * to


def shifted(value, axis, by):
    peers = lax.axis_size(axis)
    return lax.ppermute(value, axis, [(i, (i + by) % peers) for i in range(peers)])


def halves(value):
    high = value.astype(bf16)
    return high, (value - high.astype(f32)).astype(bf16)


def picked(condition):
    return jnp.where(condition, 1.0, 0.0).astype(f32)


def iota(shape, dim):
    return lax.broadcasted_iota(jnp.int32, shape, dim)


def whole(count):
    return [pl.BlockSpec(memory_space=pltpu.VMEM) for _ in range(count)]


def build_table(table_ref, number, snapshots, weight, velocity_ref, north_ref, south_ref, west_ref, east_ref, columns):
    rows, cols = velocity_ref.shape[2], velocity_ref.shape[3]
    count = velocity_ref.shape[1]
    block = up(rows + 2, 16)
    lane = iota((16, cols), 1)
    sub = iota((16, cols), 0)
    for c in range(2):
        inner = None
        for a in snapshots:
            k = c * count + a
            body = velocity_ref[c, a]
            side = pltpu.roll(columns, (cols - k) % cols, 1)
            top, low = north_ref[c, a : a + 1], south_ref[c, a : a + 1]
            edge = jnp.where(sub == 0, top, jnp.where(sub == 1, low, 0.0))
            north_west, north_east = west_ref[1, c, a : a + 1, cols - 1 :], east_ref[1, c, a : a + 1, 0:1]
            south_west, south_east = west_ref[2, c, a : a + 1, cols - 1 :], east_ref[2, c, a : a + 1, 0:1]
            west = jnp.where(sub == 0, north_west, jnp.where(sub == 1, south_west, 0.0))
            east = jnp.where(sub == 0, north_east, jnp.where(sub == 1, south_east, 0.0))
            corner = jnp.where(lane == 0, west, jnp.where(lane == 8, east, 0.0))
            parts = (body, side, edge, corner)
            inner = parts if inner is None else tuple(p + q for p, q in zip(inner, parts))
        body, side, edge, corner = (weight * p if weight != 1.0 else p for p in inner)
        for split, (b, s, e, n) in enumerate(zip(halves(body), halves(side), halves(edge), halves(corner))):
            at = (split * 2 + c) * block
            table_ref[number, at : at + rows, 0:cols] = b
            table_ref[number, at : at + rows, cols : 2 * cols] = s
            table_ref[number, at + rows : at + block, 0:cols] = e
            table_ref[number, at + rows : at + block, cols : 2 * cols] = n


def read_corners(table_ref, number, cell, rows, cols):
    block = up(rows + 2, 16)
    slots = cell.shape[1]
    cy, cx = cell[0:1], cell[1:2]
    at = iota((2 * cols, slots), 0)
    left = picked(at == jnp.where(cx < 0, cols, cx)).astype(bf16)
    right = picked(at == jnp.where(cx + 1 >= cols, cols + 8, cx + 1)).astype(bf16)
    row = iota((block, slots), 0)
    upper = row == jnp.where(cy < 0, rows, cy)
    lower = row == jnp.where(cy + 1 >= rows, rows + 1, cy + 1)
    table = table_ref[number]
    values = {}
    for side, onehot in enumerate((left, right)):
        product = jnp.dot(table, onehot, preferred_element_type=f32)
        for c in range(2):
            column = product[c * block : (c + 1) * block] + product[(2 + c) * block : (3 + c) * block]
            values[0, side, c] = jnp.sum(jnp.where(upper, column, 0.0), axis=0, keepdims=True)
            values[1, side, c] = jnp.sum(jnp.where(lower, column, 0.0), axis=0, keepdims=True)
    return [[values[v, h, c] for c in range(2)] for v in range(2) for h in range(2)]


def bilinear(corners, point, cell):
    wy = point[0] - cell[0:1].astype(f32)
    wx = point[1] - cell[1:2].astype(f32)
    first, second, third, fourth = corners
    return [
        (1.0 - wy) * ((1.0 - wx) * first[c] + wx * second[c]) + wy * ((1.0 - wx) * third[c] + wx * fourth[c])
        for c in range(2)
    ]


def along(point, factor, speed):
    return [p + factor * s for p, s in zip(point, speed)]


def halo_columns(west_ref, east_ref, cols):
    count = west_ref.shape[1] * west_ref.shape[2]
    zeros = jnp.zeros((8 - count, cols), f32)
    west = [west_ref[0, c, a : a + 1] for c in range(west_ref.shape[1]) for a in range(west_ref.shape[2])]
    east = [east_ref[0, c, a : a + 1] for c in range(east_ref.shape[1]) for a in range(east_ref.shape[2])]
    flat = jnp.concatenate(west + [zeros] + east + [zeros, jnp.zeros((cols - 16, cols), f32)], axis=0)
    return flat.T


def step_kernel(step, following, velocity_ref, north_ref, south_ref, west_ref, east_ref, point_ref, first_ref, cells_ref, *rest):
    if following:
        record_ref, next_ref, table_ref = rest
    else:
        record_ref, table_ref = rest
    rows, cols = velocity_ref.shape[2], velocity_ref.shape[3]
    columns = halo_columns(west_ref, east_ref, cols)
    fields = (velocity_ref, north_ref, south_ref, west_ref, east_ref, columns)
    build_table(table_ref, 0, (step,), 1.0, *fields)
    build_table(table_ref, 1, (step, step + 1), 0.5, *fields)
    build_table(table_ref, 2, (step + 1,), 1.0, *fields)
    sections = [cells_ref[step, s] for s in range(4)]
    if step == 0:
        first = read_corners(table_ref, 0, sections[0], rows, cols)
    else:
        first = [[first_ref[2 * i + c : 2 * i + c + 1] for c in range(2)] for i in range(4)]
    second = read_corners(table_ref, 1, sections[1], rows, cols)
    third = read_corners(table_ref, 1, sections[2], rows, cols)
    fourth = read_corners(table_ref, 2, sections[3], rows, cols)
    point = [point_ref[0:1], point_ref[1:2]]
    k_one = bilinear(first, point, sections[0])
    k_two = bilinear(second, along(point, 0.5 * drift, k_one), sections[1])
    k_three = bilinear(third, along(point, 0.5 * drift, k_two), sections[2])
    k_four = bilinear(fourth, along(point, drift, k_three), sections[3])
    point = [
        p + drift / 6.0 * (a + 2.0 * b + 2.0 * c + d)
        for p, a, b, c, d in zip(point, k_one, k_two, k_three, k_four)
    ]
    blank = [jnp.zeros_like(point[0])] * 4
    record_ref[...] = jnp.concatenate(point + k_one + blank, axis=0)
    if following:
        ahead = read_corners(table_ref, 2, cells_ref[step + 1, 0], rows, cols)
        next_ref[...] = jnp.concatenate([value for corner in ahead for value in corner], axis=0)


def run_step(step, halo, point, first, cells):
    velocity = halo[0]
    slots = point.shape[1]
    following = step + 1 < STEPS
    rows, cols = velocity.shape[2], velocity.shape[3]
    shape = jax.ShapeDtypeStruct((8, slots), f32)
    block = up(rows + 2, 16)
    return pl.pallas_call(
        functools.partial(step_kernel, step, following),
        out_shape=[shape] * (2 if following else 1),
        in_specs=whole(8),
        out_specs=whole(2 if following else 1),
        scratch_shapes=[pltpu.VMEM((3, 4 * block, 2 * cols), bf16)],
        cost_estimate=pl.CostEstimate(flops=10 * 4 * block * 2 * cols * slots * 2, bytes_accessed=600000, transcendentals=0),
        name="sample_step",
    )(*halo, point, first, cells)


def paired_halves(first, second, width):
    lane = iota(first.shape, 1)
    left = jnp.where(lane < width, first, pltpu.roll(second, width, 1))
    right = jnp.where(lane < width, pltpu.roll(first, width, 1), second)
    return left, right


def place_history_kernel(width, paired, history_ref, arrived_ref, owner_ref, owner_row_ref, out_ref, target_ref):
    slots = owner_ref.shape[0]
    total = out_ref.shape[0] * width if paired else out_ref.shape[2]
    rows = up(HISTORY, 8)
    before = iota((slots, slots), 1) < iota((slots, slots), 0)
    same = owner_ref[...] == owner_row_ref[...]
    rank = jnp.sum(picked(same & before), axis=1, keepdims=True).astype(jnp.int32)
    target = owner_ref[...] * width + rank
    target_ref[...] = jnp.broadcast_to(target, target_ref.shape)
    moved = arrived_ref.shape[2]
    blank = jnp.zeros((rows - HISTORY, slots), f32)
    parts = []
    for c in range(2):
        parts.append(jnp.concatenate([arrived_ref[c], history_ref[c, :, moved:]], axis=1))
        parts.append(blank)
    high, low = halves(jnp.concatenate(parts, axis=0))
    both = jnp.concatenate([high, low], axis=0)
    chunk = 256
    for start in range(0, total, chunk):
        onehot = picked(target == start + iota((slots, chunk), 1)).astype(bf16)
        product = jnp.dot(both, onehot, preferred_element_type=f32)
        placed = product[: 2 * rows] + product[2 * rows :]
        if paired:
            for at in range(0, chunk, LANES):
                left, right = paired_halves(placed[:rows, at : at + LANES], placed[rows:, at : at + LANES], width)
                number = (start + at) // width
                out_ref[number, 0:rows] = left
                out_ref[number + 1, 0:rows] = right
        else:
            out_ref[0, 0:rows, start : start + chunk] = placed[:rows]
            out_ref[1, 0:rows, start : start + chunk] = placed[rows:]


def place_samples_kernel(width, paired, record_ref, moved_ref, next_ref, cells_ref, target_ref, _, out_ref):
    slots = record_ref.shape[1]
    moved = moved_ref.shape[1]
    total = out_ref.shape[0] * width if paired else out_ref.shape[2]
    record = jnp.concatenate([moved_ref[...], record_ref[:, moved:]], axis=1)
    corners = [[next_ref[2 * i + c : 2 * i + c + 1] for c in range(2)] for i in range(4)]
    last = bilinear(corners, [record[0:1], record[1:2]], cells_ref[STEPS - 1, 0])
    blank = jnp.zeros((6, slots), f32)
    columns = [record[2:3], last[0], blank, record[3:4], last[1], blank]
    high, low = halves(jnp.concatenate(columns, axis=0))
    both = jnp.concatenate([high, low], axis=0)
    target = target_ref[:, 0:1]
    chunk = 256
    for start in range(0, total, chunk):
        onehot = picked(target == start + iota((slots, chunk), 1)).astype(bf16)
        product = jnp.dot(both, onehot, preferred_element_type=f32)
        placed = product[:16] + product[16:]
        if paired:
            for at in range(0, chunk, LANES):
                left, right = paired_halves(placed[:8, at : at + LANES], placed[8:, at : at + LANES], width)
                number = (start + at) // width
                out_ref[number] = left
                out_ref[number + 1] = right
        else:
            out_ref[0, :, start : start + chunk] = placed[:8]
            out_ref[1, :, start : start + chunk] = placed[8:]


def filter_kernel(width, paired, matrix_ref, arrived_ref, out_ref):
    outs, depth = matrix_ref.shape
    high, low = halves(matrix_ref[...])
    left = jnp.concatenate([high, low, high], axis=1)
    total = out_ref.shape[2]
    chunk = 512
    for start in range(0, total, chunk):
        if paired:
            tiles = [
                paired_halves(arrived_ref[at // width], arrived_ref[at // width + 1], width)
                for at in range(start, start + chunk, LANES)
            ]
            columns = [jnp.concatenate([t[c] for t in tiles], axis=1) for c in range(2)]
        else:
            columns = [arrived_ref[c, :, start : start + chunk] for c in range(2)]
        for c in range(2):
            x_high, x_low = halves(columns[c])
            right = jnp.concatenate([x_high, x_high, x_low], axis=0)
            product = jnp.dot(left, right, preferred_element_type=f32)
            out_ref[c, :, start : start + chunk] = product[: out_ref.shape[1]]


def cost(flops, moved):
    return pl.CostEstimate(flops=flops, bytes_accessed=moved, transcendentals=0)


def sides_of(counts, axis):
    slot = iota((1, 8 * MOST), 1)
    offsets = jnp.cumsum(counts) - counts
    result = jnp.zeros((1, 8 * MOST), jnp.int32)
    for j in range(8):
        inside = (slot >= offsets[j]) & (slot < offsets[j] + counts[j])
        result = result + jnp.where(inside, moves[j][axis], 0)
    return result


def moved_along(value, side, axis):
    forward = shifted(value, axis, 1)
    backward = shifted(value, axis, -1)
    return jnp.where(side == 1, forward, jnp.where(side == -1, backward, value))


def per_device(velocity, start_position, cells, history, leavers, owner, filter_matrix):
    tile_rows = velocity.shape[2]
    tile_cols = velocity.shape[3]
    slots = start_position.shape[1]
    tile_count = lax.axis_size("ty") * lax.axis_size("tx")
    per_owner = 4 * slots // tile_count
    paired = 2 * per_owner == LANES
    north = shifted(velocity[:, :, tile_rows - 1], "ty", 1)
    south = shifted(velocity[:, :, 0], "ty", -1)
    west = shifted(jnp.stack([velocity[:, :, :, tile_cols - 1], north, south]), "tx", 1)
    east = shifted(jnp.stack([velocity[:, :, :, 0], north, south]), "tx", -1)
    halo = (velocity, north, south, west, east)
    point = start_position
    first = jnp.zeros((8, slots), f32)
    moved_history = history
    record = None
    for step in range(STEPS):
        if step == STEPS - 1:
            waiting = first
        results = run_step(step, halo, point, first, cells)
        if step == STEPS - 1:
            break
        record, first = results
        counts = leavers[step]
        band = step * 8 * MOST
        side_y, side_x = sides_of(counts, 0), sides_of(counts, 1)
        part = record[:, band : band + 8 * MOST]
        part = moved_along(moved_along(part, side_y, "ty"), side_x, "tx")
        lowered = jnp.concatenate([side_y * tile_rows, side_x * tile_cols, jnp.zeros((6, 8 * MOST), jnp.int32)], axis=0)
        part = part - lowered.astype(f32)
        past = history[:, :, band : band + 8 * MOST]
        past = moved_along(moved_along(past, side_y, "ty"), side_x, "tx")
        point = jnp.concatenate([part[0:2], record[0:2, 8 * MOST :]], axis=1)
    depth = up(HISTORY, 8) + 8
    shape = (tile_count, depth, LANES) if paired else (2, depth, tile_count * per_owner)
    placed, target = pl.pallas_call(
        functools.partial(place_history_kernel, per_owner, paired),
        out_shape=[jax.ShapeDtypeStruct(shape, f32), jax.ShapeDtypeStruct((slots, LANES), jnp.int32)],
        in_specs=whole(4),
        out_specs=whole(2),
        cost_estimate=cost(2 * 4 * 80 * slots * 4 * slots, 3000000),
        name="place_history",
    )(history, past, owner, owner.reshape(1, slots))
    blocks = (tile_count, 8, LANES) if paired else (2, 8, tile_count * per_owner)
    placed = pl.pallas_call(
        functools.partial(place_samples_kernel, per_owner, paired),
        out_shape=jax.ShapeDtypeStruct(shape, f32),
        grid=(1,),
        in_specs=[pl.BlockSpec(s, lambda i, n=len(s): (0,) * n) for s in (record.shape, part.shape, waiting.shape, cells.shape, target.shape)]
        + [pl.BlockSpec(memory_space=pl.ANY)],
        out_specs=pl.BlockSpec(blocks, lambda i: (0, depth // 8 - 1, 0)),
        input_output_aliases={5: 0},
        cost_estimate=cost(2 * 2 * 16 * slots * 4 * slots, 1000000),
        name="place_samples",
    )(record, part, waiting, cells, target, placed)
    if not paired:
        placed = placed.reshape(2, depth, tile_count, per_owner).transpose(2, 1, 0, 3)
    arrived = lax.all_to_all(placed, ("ty", "tx"), split_axis=0, concat_axis=0, tiled=True)
    if not paired:
        arrived = arrived.transpose(2, 1, 0, 3).reshape(shape)
    matrix = jnp.zeros((up(SAMPLES, 16), depth), f32)
    matrix = matrix.at[:SAMPLES, :HISTORY].set(filter_matrix[:, :HISTORY])
    matrix = matrix.at[:SAMPLES, depth - 8 : depth - 8 + STEPS].set(filter_matrix[:, HISTORY:])
    return pl.pallas_call(
        functools.partial(filter_kernel, per_owner, paired),
        out_shape=jax.ShapeDtypeStruct((2, SAMPLES, tile_count * per_owner), f32),
        in_specs=whole(2),
        out_specs=whole(1)[0],
        cost_estimate=cost(2 * 3 * 80 * 80 * 8 * slots, 3000000),
        name="filter_series",
    )(matrix, arrived)


def solution(mesh):
    placed = (
        P(None, None, "ty", "tx"),
        P(None, ("ty", "tx")),
        P(None, None, None, ("ty", "tx")),
        P(None, None, ("ty", "tx")),
        P(),
        P(("ty", "tx"), None),
        P(),
    )
    return jax.shard_map(
        per_device,
        mesh=mesh,
        in_specs=placed,
        out_specs=P(None, None, ("ty", "tx")),
        check_vma=False,
    )
```

time: 193 us -> 114 us (0.59)
  local copies, waits for them, and re-layouts: 86 us -> 14.4 us
  blocking collectives: 55.1 us -> 0 us
  waiting for transfers between devices: 6.3 us -> 31 us
  starting transfers between devices: 13.3 us -> 27.1 us
  Pallas kernels: 0 us -> 13 us
  between operations: 16 us -> 10.2 us
  other arithmetic: 13.1 us -> 17.1 us
  matrix products: 2.46 us -> 0 us
    all_to_all x1 -> x0, blocking collectives: 55.1 us -> none  [per_device(): lax.all_to_all(outgoing, ('ty', 'tx'), split_axis=1, concat_axis=1, tiled...]
    gather x16 -> x0, local copies, waits for them, and re-layouts: 36.6 us -> none  [bilinear(): gathered = jnp.take(corner_table, corner, axis=1)]
    all_to_all x0 -> x1, waiting for transfers between devices: none -> 27.7 us  [per_device(): lax.all_to_all(placed, ('ty', 'tx'), split_axis=0, concat_axis=0, tiled=T...]
    concatenate x6 -> x1, local copies, waits for them, and re-layouts: 26.9 us -> 0.08 us  [per_device(): jnp.concatenate([side_y * tile_rows, side_x * tile_cols, jnp.zeros((6, 8...]
    ppermute x4 -> x12, starting transfers between devices: 5.43 us -> 21 us  [shifted(): lax.ppermute(value, axis, [(i, (i + by) % peers) for i in range(peers)])]
    pallas_call x0 -> x4, Pallas kernels: none -> 13 us  [the longest x1 4.22 us: run_step(): pl.pallas_call(functools.partial(step_kernel, step, following), out_shape...]
    ppermute x4 -> x0, starting transfers between devices: 7.9 us -> none  [the longest x2 5.07 us: padded_2(): lax.ppermute(lax.slice_in_dim(block, 0, width, axis=dim), axis, backward)]
    dynamic_update_slice x8 -> x0, local copies, waits for them, and re-layouts: 7.5 us -> none  [migrate(): record = lax.dynamic_update_slice_in_dim(record, merged, starts[j], 1)]
  transfers between devices with their start and end apart: 8 -> 13, of which waited for: 2 -> 3; matrix products, arithmetic and copies ran while one was open for 22% -> 23% of each run, Pallas kernels for 0% -> 4%
where the time goes in v1:
time: 114 us; the launch traced here: 113 us
  waiting for transfers between devices  31 us (27%)
  starting transfers between devices  27.1 us (24%)
  other arithmetic  17.1 us (15%)
  local copies, waits for them, and re-layouts  14.4 us (13%)
  Pallas kernels  13 us (11%)
  between operations  10.2 us (9%)
    all_to_all x1, waiting for transfers between devices, per_device(): lax.all_to_all(placed, ('ty', 'tx'), split_axis=0, concat_axis=0, tiled=T...  27.7 us
    ppermute x12, starting transfers between devices, shifted(): lax.ppermute(value, axis, [(i, (i + by) % peers) for i in range(peers)])  21 us
    eq x4, other arithmetic, moved_along(): return jnp.where(side == 1, forward, jnp.where(side == -1, backward, value))  7.4 us
    all_to_all x1, starting transfers between devices, per_device(): lax.all_to_all(placed, ('ty', 'tx'), split_axis=0, concat_axis=0, tiled=T...  6.11 us
    mul x1, other arithmetic, per_device(): side_x * tile_cols  4.93 us
    pallas_call x1, Pallas kernels, run_step(): pl.pallas_call(functools.partial(step_kernel, step, following), out_shape...  4.22 us
    pallas_call x1, Pallas kernels, per_device(): pl.pallas_call(functools.partial(place_history_kernel, per_owner, paired)...  3.45 us
    unnamed x28, local copies, waits for them, and re-layouts  3.43 us
  transfers between devices with their start and end apart: 13, of which 3 were waited for; matrix products, arithmetic and copies ran while one was open for 23% of the time, Pallas kernels for 4%

profile of v1, /device:TPU:0, one launch (start us, length us, event | category | flops | bytes accessed | tf_op | source)
XLA Modules:
  0.0 112.8 jit_solution(16319143421246724756)
XLA Ops:
  0.0 1.0 copy.14.history_ref
  1.6 2.0 %collective-permute-start.9 = (f32[2,71,128]{2,1,0:T(8,128)S(1)}, f32[2,71,128]{2,1,0:T(8,128)S(1)}, u32[]{:S(2)}, u32[]{:S(2)}) collective-permute-start(f32[2,71,128]{2,1,0:T(8,128)S(1)} %slice.184), channel_id=1, source_target_pairs={{0,24},{8,0},{16,8},{24,16},{1,25},{9,1},{17,9},{25,17},{2,26},{10... | collective-permute-start | bytes 218120 | tf_op jit(solution)/shard_map/ppermute | solution.py:29
  3.6 0.8 fusion.12
  5.0 1.1 %collective-permute-start.1 = (f32[2,3,128]{2,1,0:T(4,128)S(1)}, f32[2,3,128]{2,1,0:T(4,128)S(1)}, u32[]{:S(2)}, u32[]{:S(2)}) collective-permute-start(f32[2,3,128]{2,1,0:T(4,128)S(1)} %bitcast.43), channel_id=1, source_target_pairs={{0,24},{8,0},{16,8},{24,16},{1,25},{9,1},{17,9},{25,17},{2,26},{10... | collective-permute-start | bytes 9224 | tf_op jit(solution)/shard_map/ppermute | solution.py:29
  6.1 1.4 %fusion.11 = (f32[2,3,128,1]{3,2,1,0:T(8,128)S(1)}, f32[2,3,128,1]{3,2,1,0:T(8,128)S(1)}) fusion(f32[2,3,128,128]{3,2,1,0:T(8,128)} %velocity_ref.1), kind=kLoop, calls=%fused_computation.47 | loop fusion | bytes 12288 | tf_op jit(solution)/shard_map/slice | solution.py:296
  7.5 0.7 fusion.13
  8.4 0.7 fusion.14
  16.5 3.7 %broadcast_compare_fusion = (pred[128]{0:T(512)(128)(4,1)S(1)}, s32[128]{0:T(128)S(1)}) fusion(s32[]{:T(128)S(6)} %add.261, s32[]{:T(128)} %bitcast.21, s32[]{:T(128)S(6)} %add.267, s32[]{:T(128)} %bitcast.25, s32[]{:T(128)S(6)} %add.259, s32[]{:T(128)} %bitcast.19, s32[]{:T(128)S(6)} %add.253, s32[]{:T(128)} %bitcast.13, s32[]{:T(128)S(6)} %add.263, ...), kind=kLoop, calls=%fused_computation.43 | loop fusion | flops 3840 | bytes 688 | tf_op jit(solution)/shard_map/eq | solution.py:283
  22.7 3.7 %broadcast_compare_fusion.1 = (pred[128]{0:T(512)(128)(4,1)S(1)}, s32[128]{0:T(128)S(1)}) fusion(s32[]{:T(128)S(6)} %add.261, s32[]{:T(128)} %bitcast.21, s32[]{:T(128)S(6)} %add.259, s32[]{:T(128)} %bitcast.19, s32[]{:T(128)S(6)} %add.257, s32[]{:T(128)} %bitcast.17, s32[]{:T(128)S(6)} %add.255, s32[]{:T(128)} %bitcast.15, s32[]{:T(128)S(6)} %add.253, ...), kind=kLoop, calls=%fused_computation.44 | loop fusion | flops 3840 | bytes 688 | tf_op jit(solution)/shard_map/eq | solution.py:283
  26.9 2.3 %collective-permute-start.2 = (f32[3,2,3,128]{3,2,1,0:T(4,128)S(1)}, f32[3,2,3,128]{3,2,1,0:T(4,128)S(1)}, u32[]{:S(2)}, u32[]{:S(2)}) collective-permute-start(f32[3,2,3,128]{3,2,1,0:T(4,128)S(1)} %get-tuple-element.46), channel_id=1, source_target_pairs={{0,1},{1,2},{2,3},{3,4},{4,5},{5,6},{6,7},{7,0},{8,9},{9,10},{10,1... | collective-permute-start | bytes 27656 | tf_op jit(solution)/shard_map/ppermute | solution.py:29
  29.2 3.1 %collective-permute-start.3 = (f32[3,2,3,128]{3,2,1,0:T(4,128)S(1)}, f32[3,2,3,128]{3,2,1,0:T(4,128)S(1)}, u32[]{:S(2)}, u32[]{:S(2)}) collective-permute-start(f32[3,2,3,128]{3,2,1,0:T(4,128)S(1)} %get-tuple-element.45), channel_id=1, source_target_pairs={{0,7},{1,0},{2,1},{3,2},{4,3},{5,4},{6,5},{7,6},{8,15},{9,8},{10,9... | collective-permute-start | bytes 27656 | tf_op jit(solution)/shard_map/ppermute | solution.py:29
  32.3 1.6 %collective-permute-done.2.west_ref = f32[3,2,3,128]{3,2,1,0:T(4,128)S(1)} collective-permute-done((f32[3,2,3,128]{3,2,1,0:T(4,128)S(1)}, f32[3,2,3,128]{3,2,1,0:T(4,128)S(1)}, u32[]{:S(2)}, u32[]{:S(2)}) %collective-permute-start.2) | collective-permute-done | bytes 9248 | tf_op jit(solution)/shard_map/ppermute | solution.py:29
  34.5 4.2 %sample_step.1 = (f32[8,512]{1,0:T(8,128)}, f32[8,512]{1,0:T(8,128)}) custom-call(f32[2,3,128,128]{3,2,1,0:T(8,128)} %velocity_ref.1, f32[2,3,128]{2,1,0:T(4,128)} %copy-done.5, f32[2,3,128]{2,1,0:T(4,128)} %copy-done.6, f32[3,2,3,128]{3,2,1,0:T(4,128)} %copy-done.8, f32[3,2,3,128]{3,2,1,0:T(4,128)} %copy-done.9, f32[2,512]{1,0:T(2,128)} %point_ref.1, ...), custom_call_target="tpu_custom_call" | custom-call | flops 1509949440 | bytes 600000 | tf_op jit(solution)/shard_map/sample_step/pallas_call | solution.py:165
  38.8 0.7 slice.182
  39.4 1.7 %collective-permute-start.5 = (f32[8,128]{1,0:T(8,128)S(1)}, f32[8,128]{1,0:T(8,128)S(1)}, u32[]{:S(2)}, u32[]{:S(2)}) collective-permute-start(f32[8,128]{1,0:T(8,128)S(1)} %slice.182), channel_id=1, source_target_pairs={{0,24},{8,0},{16,8},{24,16},{1,25},{9,1},{17,9},{25,17},{2,26},{10... | collective-permute-start | bytes 12296 | tf_op jit(solution)/shard_map/ppermute | solution.py:29
  41.2 4.9 %add_multiply_fusion = (s32[1,128]{1,0:T(1,128)S(1)}, s32[1,128]{1,0:T(1,128)S(1)}) fusion(s32[]{:T(128)S(6)} %add.257, s32[]{:T(128)} %bitcast.17, s32[]{:T(128)S(6)} %add.255, s32[]{:T(128)} %bitcast.15, s32[]{:T(128)S(6)} %add.253, s32[]{:T(128)} %bitcast.13, s32[]{:T(128)S(6)} %add.259, s32[]{:T(128)} %bitcast.19, s32[]{:T(128)S(6)} %add.252, ...), kind=kLoop, calls=%fused_computation.38 | loop fusion | flops 5888 | bytes 1088 | tf_op jit(solution)/shard_map/mul | solution.py:314
  46.1 0.9 copy.15.owner_ref
  47.1 0.7 select_select_fusion.2
  47.8 1.4 %collective-permute-start.6 = (f32[8,128]{1,0:T(8,128)S(1)}, f32[8,128]{1,0:T(8,128)S(1)}, u32[]{:S(2)}, u32[]{:S(2)}) collective-permute-start(f32[8,128]{1,0:T(8,128)S(1)} %select_select_fusion.2), channel_id=1, source_target_pairs={{0,1},{1,2},{2,3},{3,4},{4,5},{5,6},{6,7},{7,0},{8,9},{9,10},{10,1... | collective-permute-start | bytes 12296 | tf_op jit(solution)/shard_map/ppermute | solution.py:29
  49.2 3.4 %collective-permute-start.7 = (f32[8,128]{1,0:T(8,128)S(1)}, f32[8,128]{1,0:T(8,128)S(1)}, u32[]{:S(2)}, u32[]{:S(2)}) collective-permute-start(f32[8,128]{1,0:T(8,128)S(1)} %select_select_fusion.2), channel_id=1, source_target_pairs={{0,7},{1,0},{2,1},{3,2},{4,3},{5,4},{6,5},{7,6},{8,15},{9,8},{10,9... | collective-permute-start | bytes 12296 | tf_op jit(solution)/shard_map/ppermute | solution.py:29
  52.7 4.7 %collective-permute-start.11 = (f32[2,71,128]{2,1,0:T(8,128)S(1)}, f32[2,71,128]{2,1,0:T(8,128)S(1)}, u32[]{:S(2)}, u32[]{:S(2)}) collective-permute-start(f32[2,71,128]{2,1,0:T(8,128)S(1)} %select_select_fusion.1), channel_id=1, source_target_pairs={{0,7},{1,0},{2,1},{3,2},{4,3},{5,4},{6,5},{7,6},{8,15},{9,8},{10,9... | collective-permute-start | bytes 218120 | tf_op jit(solution)/shard_map/ppermute | solution.py:29
  57.4 0.7 fusion.moved_ref
  58.0 1.7 %collective-permute-done.10 = f32[2,71,128]{2,1,0:T(8,128)S(1)} collective-permute-done((f32[2,71,128]{2,1,0:T(8,128)S(1)}, f32[2,71,128]{2,1,0:T(8,128)S(1)}, u32[]{:S(2)}, u32[]{:S(2)}) %collective-permute-start.10) | collective-permute-done | bytes 72736 | tf_op jit(solution)/shard_map/ppermute | solution.py:29
  60.3 3.4 %place_history.1 = (f32[32,80,128]{2,1,0:T(8,128)}, s32[512,128]{1,0:T(8,128)}) custom-call(f32[2,71,512]{2,1,0:T(8,128)} %copy-done.1, f32[2,71,128]{2,1,0:T(8,128)} %select_select_fusion.arrived_ref, s32[512,1]{1,0:T(8,128)} %copy.15.owner_ref, s32[1,512]{1,0:T(1,128)} %bitcast.44), custom_call_target="tpu_custom_call" | custom-call | flops 671088640 | bytes 3000000 | tf_op jit(solution)/shard_map/place_history/pallas_call | solution.py:321
  63.8 2.3 %place_samples.1 = f32[32,80,128]{2,1,0:T(8,128)} custom-call(f32[8,512]{1,0:T(8,128)} %get-tuple-element.33.record_ref, f32[8,128]{1,0:T(8,128)} %fusion.moved_ref, f32[8,512]{1,0:T(8,128)} %get-tuple-element.34.next_ref, s32[2,4,2,512]{3,2,1,0:T(2,128)} %cells_ref.3, s32[512,128]{1,0:T(8,128)} %get-tuple-element.35.target_ref, ...), custom_call_target="tpu_custom_call", output_to_operand_aliasing={{}: (5, {})} | custom-call | flops 67108864 | bytes 1000000 | tf_op jit(solution)/shard_map/place_samples/pallas_call | solution.py:330
  66.1 6.1 %all-to-all-start = ((f32[32,80,128]{2,1,0:T(8,128)}), f32[32,80,128]{2,1,0:T(8,128)S(1)}, u32[]{:S(2)}, u32[]{:S(2)}) async-start(f32[32,80,128]{2,1,0:T(8,128)} %place_samples.1), calls=%async_computation | async-start | bytes 2621440 | tf_op jit(solution)/shard_map/all_to_all | solution.py:343
  73.5 1.9 %dynamic-slice_select_fusion = f32[73,2]{1,0:T(8,128)S(1)} fusion(s32[]{:T(128)} %bitcast, s32[]{:T(128)} %bitcast.1, f32[73,73]{1,0:T(8,128)S(1)} %copy-done.2, pred[]{:T(512)} %and_reduce_fusion, f32[73,71]{1,0:T(8,128)S(1)} %bitcast.36), kind=kLoop, calls=%fused_computation.2 | loop fusion | flops 146 | bytes 21909 | tf_op jit(solution)/shard_map/select.3
  75.4 2.3 %scatter.9.matrix_ref = f32[80,80]{1,0:T(8,128)S(1)} dynamic-update-slice(f32[80,80]{1,0:T(8,128)S(1)} %scatter.6, f32[73,2]{1,0:T(8,128)S(1)} %dynamic-slice_select_fusion, s32[]{:T(128)} %bitcast, s32[]{:T(128)} %bitcast.1) | dynamic-update-slice | bytes 1172 | tf_op jit(solution)/shard_map/scatter | solution.py:348
  77.7 27.7 %all-to-all-done.arrived_ref = f32[32,80,128]{2,1,0:T(8,128)S(1)} async-done(((f32[32,80,128]{2,1,0:T(8,128)}), f32[32,80,128]{2,1,0:T(8,128)S(1)}, u32[]{:S(2)}, u32[]{:S(2)}) %all-to-all-start) | async-done | bytes 1310752 | tf_op jit(solution)/shard_map/all_to_all | solution.py:343
  105.3 1.1 copy-done
  106.4 3.1 %filter_series.1 = f32[2,73,2048]{2,1,0:T(8,128)} custom-call(f32[80,80]{1,0:T(8,128)} %copy-done.3, f32[32,80,128]{2,1,0:T(8,128)} %copy-done), custom_call_target="tpu_custom_call" | custom-call | flops 157286400 | bytes 3000000 | tf_op jit(solution)/shard_map/filter_series/pallas_call | solution.py:349
  109.5 3.3 %copy.16 = f32[2,73,2048]{2,0,1:T(2,128)} copy(f32[2,73,2048]{2,1,0:T(8,128)} %filter_series.1) | data formatting | bytes 2392064 | tf_op jit(solution)/shard_map/filter_series/pallas_call | solution.py:349
  (54 shorter events, 4.5 us)
Async XLA Ops:
  0.0 7.5 %copy-start.4 = (s32[1,8]{1,0:T(1,128)S(1)}, s32[1,8]{1,0:T(1,128)}, u32[]{:S(2)}) copy-start(s32[1,8]{1,0:T(1,128)} %param.15) | copy-start | bytes 100
  1.0 51.5 %copy-start.1 = (f32[2,71,512]{2,1,0:T(8,128)}, f32[2,71,512]{2,1,0:T(8,128)S(1)}, u32[]{:S(2)}) copy-start(f32[2,71,512]{2,1,0:T(8,128)S(1)} %copy.14.history_ref) | copy-start | bytes 872452
  1.1 51.5 %collective-permute-start.8 = (f32[2,71,128]{2,1,0:T(8,128)S(1)}, f32[2,71,128]{2,1,0:T(8,128)S(1)}, u32[]{:S(2)}, u32[]{:S(2)}) collective-permute-start(f32[2,71,128]{2,1,0:T(8,128)S(1)} %slice.184), channel_id=1, source_target_pairs={{0,8},{8,16},{16,24},{24,0},{1,9},{9,17},{17,25},{25,1},{2,10},{10... | collective-permute-start | bytes 218120 | tf_op jit(solution)/shard_map/ppermute | solution.py:29
  1.6 50.9 %collective-permute-start.9 = (f32[2,71,128]{2,1,0:T(8,128)S(1)}, f32[2,71,128]{2,1,0:T(8,128)S(1)}, u32[]{:S(2)}, u32[]{:S(2)}) collective-permute-start(f32[2,71,128]{2,1,0:T(8,128)S(1)} %slice.184), channel_id=1, source_target_pairs={{0,24},{8,0},{16,8},{24,16},{1,25},{9,1},{17,9},{25,17},{2,26},{10... | collective-permute-start | bytes 218120 | tf_op jit(solution)/shard_map/ppermute | solution.py:29
  4.4 22.5 %collective-permute-start = (f32[2,3,128]{2,1,0:T(4,128)S(1)}, f32[2,3,128]{2,1,0:T(4,128)S(1)}, u32[]{:S(2)}, u32[]{:S(2)}) collective-permute-start(f32[2,3,128]{2,1,0:T(4,128)S(1)} %bitcast.42), channel_id=1, source_target_pairs={{0,8},{8,16},{16,24},{24,0},{1,9},{9,17},{17,25},{25,1},{2,10},{10... | collective-permute-start | bytes 9224 | tf_op jit(solution)/shard_map/ppermute | solution.py:29
  5.0 21.8 %collective-permute-start.1 = (f32[2,3,128]{2,1,0:T(4,128)S(1)}, f32[2,3,128]{2,1,0:T(4,128)S(1)}, u32[]{:S(2)}, u32[]{:S(2)}) collective-permute-start(f32[2,3,128]{2,1,0:T(4,128)S(1)} %bitcast.43), channel_id=1, source_target_pairs={{0,24},{8,0},{16,8},{24,16},{1,25},{9,1},{17,9},{25,17},{2,26},{10... | collective-permute-start | bytes 9224 | tf_op jit(solution)/shard_map/ppermute | solution.py:29
  26.8 7.7 %copy-start.5 = (f32[2,3,128]{2,1,0:T(4,128)}, f32[2,3,128]{2,1,0:T(4,128)S(1)}, u32[]{:S(2)}) copy-start(f32[2,3,128]{2,1,0:T(4,128)S(1)} %collective-permute-done.north_ref) | copy-start | bytes 9220
  26.8 7.7 %copy-start.6 = (f32[2,3,128]{2,1,0:T(4,128)}, f32[2,3,128]{2,1,0:T(4,128)S(1)}, u32[]{:S(2)}) copy-start(f32[2,3,128]{2,1,0:T(4,128)S(1)} %collective-permute-done.1.south_ref) | copy-start | bytes 9220
  26.9 7.0 %collective-permute-start.2 = (f32[3,2,3,128]{3,2,1,0:T(4,128)S(1)}, f32[3,2,3,128]{3,2,1,0:T(4,128)S(1)}, u32[]{:S(2)}, u32[]{:S(2)}) collective-permute-start(f32[3,2,3,128]{3,2,1,0:T(4,128)S(1)} %get-tuple-element.46), channel_id=1, source_target_pairs={{0,1},{1,2},{2,3},{3,4},{4,5},{5,6},{6,7},{7,0},{8,9},{9,10},{10,1... | collective-permute-start | bytes 27656 | tf_op jit(solution)/shard_map/ppermute | solution.py:29
  29.2 4.7 %collective-permute-start.3 = (f32[3,2,3,128]{3,2,1,0:T(4,128)S(1)}, f32[3,2,3,128]{3,2,1,0:T(4,128)S(1)}, u32[]{:S(2)}, u32[]{:S(2)}) collective-permute-start(f32[3,2,3,128]{3,2,1,0:T(4,128)S(1)} %get-tuple-element.45), channel_id=1, source_target_pairs={{0,7},{1,0},{2,1},{3,2},{4,3},{5,4},{6,5},{7,6},{8,15},{9,8},{10,9... | collective-permute-start | bytes 27656 | tf_op jit(solution)/shard_map/ppermute | solution.py:29
  33.9 0.6 copy-start.8
  33.9 0.6 copy-start.9
  34.5 11.6 %copy-start.7 = (s32[512,1]{0,1:T(1,128)S(1)}, s32[512,1]{0,1:T(1,128)}, u32[]{:S(2)}) copy-start(s32[512,1]{0,1:T(1,128)} %param.16) | copy-start | bytes 6148
  39.4 7.7 %collective-permute-start.4 = (f32[8,128]{1,0:T(8,128)S(1)}, f32[8,128]{1,0:T(8,128)S(1)}, u32[]{:S(2)}, u32[]{:S(2)}) collective-permute-start(f32[8,128]{1,0:T(8,128)S(1)} %slice.182), channel_id=1, source_target_pairs={{0,8},{8,16},{16,24},{24,0},{1,9},{9,17},{17,25},{25,1},{2,10},{10... | collective-permute-start | bytes 12296 | tf_op jit(solution)/shard_map/ppermute | solution.py:29
  39.4 7.7 %collective-permute-start.5 = (f32[8,128]{1,0:T(8,128)S(1)}, f32[8,128]{1,0:T(8,128)S(1)}, u32[]{:S(2)}, u32[]{:S(2)}) collective-permute-start(f32[8,128]{1,0:T(8,128)S(1)} %slice.182), channel_id=1, source_target_pairs={{0,24},{8,0},{16,8},{24,16},{1,25},{9,1},{17,9},{25,17},{2,26},{10... | collective-permute-start | bytes 12296 | tf_op jit(solution)/shard_map/ppermute | solution.py:29
  47.8 9.6 %collective-permute-start.6 = (f32[8,128]{1,0:T(8,128)S(1)}, f32[8,128]{1,0:T(8,128)S(1)}, u32[]{:S(2)}, u32[]{:S(2)}) collective-permute-start(f32[8,128]{1,0:T(8,128)S(1)} %select_select_fusion.2), channel_id=1, source_target_pairs={{0,1},{1,2},{2,3},{3,4},{4,5},{5,6},{6,7},{7,0},{8,9},{9,10},{10,1... | collective-permute-start | bytes 12296 | tf_op jit(solution)/shard_map/ppermute | solution.py:29
  49.2 8.2 %collective-permute-start.7 = (f32[8,128]{1,0:T(8,128)S(1)}, f32[8,128]{1,0:T(8,128)S(1)}, u32[]{:S(2)}, u32[]{:S(2)}) collective-permute-start(f32[8,128]{1,0:T(8,128)S(1)} %select_select_fusion.2), channel_id=1, source_target_pairs={{0,7},{1,0},{2,1},{3,2},{4,3},{5,4},{6,5},{7,6},{8,15},{9,8},{10,9... | collective-permute-start | bytes 12296 | tf_op jit(solution)/shard_map/ppermute | solution.py:29
  52.6 7.1 %collective-permute-start.10 = (f32[2,71,128]{2,1,0:T(8,128)S(1)}, f32[2,71,128]{2,1,0:T(8,128)S(1)}, u32[]{:S(2)}, u32[]{:S(2)}) collective-permute-start(f32[2,71,128]{2,1,0:T(8,128)S(1)} %select_select_fusion.1), channel_id=1, source_target_pairs={{0,1},{1,2},{2,3},{3,4},{4,5},{5,6},{6,7},{7,0},{8,9},{9,10},{10,1... | collective-permute-start | bytes 218120 | tf_op jit(solution)/shard_map/ppermute | solution.py:29
  52.7 7.0 %collective-permute-start.11 = (f32[2,71,128]{2,1,0:T(8,128)S(1)}, f32[2,71,128]{2,1,0:T(8,128)S(1)}, u32[]{:S(2)}, u32[]{:S(2)}) collective-permute-start(f32[2,71,128]{2,1,0:T(8,128)S(1)} %select_select_fusion.1), channel_id=1, source_target_pairs={{0,7},{1,0},{2,1},{3,2},{4,3},{5,4},{6,5},{7,6},{8,15},{9,8},{10,9... | collective-permute-start | bytes 218120 | tf_op jit(solution)/shard_map/ppermute | solution.py:29
  66.1 6.1 %copy-start.2 = (f32[73,73]{1,0:T(8,128)S(1)}, f32[73,73]{1,0:T(8,128)}, u32[]{:S(2)}) copy-start(f32[73,73]{1,0:T(8,128)} %param.17) | copy-start | bytes 63952
  66.1 6.7 %copy-start.10 = (s32[2]{0:T(128)S(1)}, s32[2]{0:T(128)}, u32[]{:S(2)}) copy-start(s32[2]{0:T(128)} %constant.61.clone.1) | copy-start | bytes 28
  66.1 39.3 %all-to-all-start = ((f32[32,80,128]{2,1,0:T(8,128)}), f32[32,80,128]{2,1,0:T(8,128)S(1)}, u32[]{:S(2)}, u32[]{:S(2)}) async-start(f32[32,80,128]{2,1,0:T(8,128)} %place_samples.1), calls=%async_computation | async-start | bytes 2621440 | tf_op jit(solution)/shard_map/all_to_all | solution.py:343
  77.6 27.7 %copy-start.3 = (f32[80,80]{1,0:T(8,128)}, f32[80,80]{1,0:T(8,128)S(1)}, u32[]{:S(2)}) copy-start(f32[80,80]{1,0:T(8,128)S(1)} %scatter.9.matrix_ref) | copy-start | bytes 76804
  105.3 1.1 copy-start

commit v2 on v1

--- a/solution.py
+++ b/solution.py
@@ -44,6 +44,13 @@
 
 def whole(count):
     return [pl.BlockSpec(memory_space=pltpu.VMEM) for _ in range(count)]
+
+
+def cost(flops, moved):
+    return pl.CostEstimate(flops=flops, bytes_accessed=moved, transcendentals=0)
+
+
+grant = pltpu.CompilerParams(vmem_limit_bytes=16 * 1024 * 1024)
 
 
 def build_table(table_ref, number, snapshots, weight, velocity_ref, north_ref, south_ref, west_ref, east_ref, columns):
@@ -120,11 +127,13 @@
     return flat.T
 
 
-def step_kernel(step, following, velocity_ref, north_ref, south_ref, west_ref, east_ref, point_ref, first_ref, cells_ref, *rest):
+def step_kernel(step, following, velocity_ref, north_ref, south_ref, west_ref, east_ref, point_ref, cells_ref, *rest):
+    if step > 0:
+        first_ref, rest = rest[0], rest[1:]
     if following:
-        record_ref, next_ref, table_ref = rest
+        record_ref, lead_ref, next_ref, table_ref = rest
     else:
-        record_ref, table_ref = rest
+        record_ref, lead_ref, table_ref = rest
     rows, cols = velocity_ref.shape[2], velocity_ref.shape[3]
     columns = halo_columns(west_ref, east_ref, cols)
     fields = (velocity_ref, north_ref, south_ref, west_ref, east_ref, columns)
@@ -149,7 +158,10 @@
         for p, a, b, c, d in zip(point, k_one, k_two, k_three, k_four)
     ]
     blank = [jnp.zeros_like(point[0])] * 4
-    record_ref[...] = jnp.concatenate(point + k_one + blank, axis=0)
+    record = jnp.concatenate(point + k_one + blank, axis=0)
+    record_ref[...] = record
+    band = step * 8 * MOST
+    lead_ref[...] = record[:, band : band + 8 * MOST]
     if following:
         ahead = read_corners(table_ref, 2, cells_ref[step + 1, 0], rows, cols)
         next_ref[...] = jnp.concatenate([value for corner in ahead for value in corner], axis=0)
@@ -159,18 +171,50 @@
     velocity = halo[0]
     slots = point.shape[1]
     following = step + 1 < STEPS
-    rows, cols = velocity.shape[2], velocity.shape[3]
+    cols = velocity.shape[3]
+    block = up(velocity.shape[2] + 2, 16)
+    operands = (*halo, point, cells) + ((first,) if step > 0 else ())
     shape = jax.ShapeDtypeStruct((8, slots), f32)
-    block = up(rows + 2, 16)
+    shapes = [shape, jax.ShapeDtypeStruct((8, 8 * MOST), f32)] + ([shape] if following else [])
     return pl.pallas_call(
         functools.partial(step_kernel, step, following),
-        out_shape=[shape] * (2 if following else 1),
-        in_specs=whole(8),
-        out_specs=whole(2 if following else 1),
+        out_shape=shapes,
+        in_specs=whole(len(operands)),
+        out_specs=whole(len(shapes)),
         scratch_shapes=[pltpu.VMEM((3, 4 * block, 2 * cols), bf16)],
-        cost_estimate=pl.CostEstimate(flops=10 * 4 * block * 2 * cols * slots * 2, bytes_accessed=600000, transcendentals=0),
+        cost_estimate=cost(10 * 4 * block * 2 * cols * slots * 2, 600000),
+        compiler_params=grant,
         name="sample_step",
-    )(*halo, point, first, cells)
+    )(*operands)
+
+
+def sides_kernel(leavers_ref, sides_ref):
+    slot = iota((1, 8 * MOST), 1)
+    for step in range(leavers_ref.shape[0]):
+        rows = [jnp.zeros((1, 8 * MOST), f32) for _ in range(2)]
+        start = 0
+        for j in range(8):
+            end = start + leavers_ref[step, j]
+            inside = (slot >= start) & (slot < end)
+            rows = [jnp.where(inside, float(moves[j][axis]), rows[axis]) for axis in range(2)]
+            start = end
+        sides_ref[step] = jnp.concatenate(rows + [jnp.zeros((6, 8 * MOST), f32)], axis=0)
+
+
+def find_sides(leavers):
+    return pl.pallas_call(
+        sides_kernel,
+        out_shape=jax.ShapeDtypeStruct((leavers.shape[0], 8, 8 * MOST), f32),
+        in_specs=[pl.BlockSpec(memory_space=pltpu.SMEM)],
+        out_specs=whole(1)[0],
+        compiler_params=grant,
+        cost_estimate=cost(100000, 5000),
+        name="find_sides",
+    )(leavers)
+
+
+def chosen(side, value, forward, backward):
+    return jnp.where(side > 0.0, forward, jnp.where(side < 0.0, backward, value))
 
 
 def paired_halves(first, second, width):
@@ -180,21 +224,25 @@
     return left, right
 
 
-def place_history_kernel(width, paired, history_ref, arrived_ref, owner_ref, owner_row_ref, out_ref, target_ref):
-    slots = owner_ref.shape[0]
+def place_history_kernel(width, paired, history_ref, past_ref, west_ref, east_ref, sides_ref, owner_ref, out_ref, target_ref):
+    slots = owner_ref.shape[1]
     total = out_ref.shape[0] * width if paired else out_ref.shape[2]
     rows = up(HISTORY, 8)
+    groups = slots // LANES
+    moving = 8 * MOST // LANES
+    owner_row = owner_ref[...]
+    owner = jnp.broadcast_to(owner_row, (LANES, slots)).T[:, 0:1]
     before = iota((slots, slots), 1) < iota((slots, slots), 0)
-    same = owner_ref[...] == owner_row_ref[...]
-    rank = jnp.sum(picked(same & before), axis=1, keepdims=True).astype(jnp.int32)
-    target = owner_ref[...] * width + rank
+    rank = jnp.sum(picked((owner == owner_row) & before), axis=1, keepdims=True).astype(jnp.int32)
+    target = owner * width + rank
     target_ref[...] = jnp.broadcast_to(target, target_ref.shape)
-    moved = arrived_ref.shape[2]
-    blank = jnp.zeros((rows - HISTORY, slots), f32)
+    side = sides_ref[0, 1:2]
     parts = []
     for c in range(2):
-        parts.append(jnp.concatenate([arrived_ref[c], history_ref[c, :, moved:]], axis=1))
-        parts.append(blank)
+        at = pl.ds(c, HISTORY, stride=2)
+        pieces = [chosen(side, past_ref[at, :], west_ref[at, :], east_ref[at, :])]
+        pieces += [history_ref[pl.ds(2 * g + c, HISTORY, stride=2 * groups), :] for g in range(moving, groups)]
+        parts += [jnp.concatenate(pieces, axis=1), jnp.zeros((rows - HISTORY, slots), f32)]
     high, low = halves(jnp.concatenate(parts, axis=0))
     both = jnp.concatenate([high, low], axis=0)
     chunk = 256
@@ -206,81 +254,82 @@
             for at in range(0, chunk, LANES):
                 left, right = paired_halves(placed[:rows, at : at + LANES], placed[rows:, at : at + LANES], width)
                 number = (start + at) // width
-                out_ref[number, 0:rows] = left
-                out_ref[number + 1, 0:rows] = right
+                out_ref[number] = left
+                out_ref[number + 1] = right
         else:
-            out_ref[0, 0:rows, start : start + chunk] = placed[:rows]
-            out_ref[1, 0:rows, start : start + chunk] = placed[rows:]
-
-
-def place_samples_kernel(width, paired, record_ref, moved_ref, next_ref, cells_ref, target_ref, _, out_ref):
+            out_ref[0, :, start : start + chunk] = placed[:rows]
+            out_ref[1, :, start : start + chunk] = placed[rows:]
+
+
+def place_samples_kernel(
+    width, paired, tile, record_ref, lead_ref, west_ref, east_ref, sides_ref, next_ref, cells_ref, target_ref, placed_ref, out_ref
+):
     slots = record_ref.shape[1]
-    moved = moved_ref.shape[1]
+    moved = lead_ref.shape[1]
     total = out_ref.shape[0] * width if paired else out_ref.shape[2]
-    record = jnp.concatenate([moved_ref[...], record_ref[:, moved:]], axis=1)
+    rows = up(HISTORY, 8)
+    sides = sides_ref[0]
+    lead = chosen(sides[1:2], lead_ref[...], west_ref[...], east_ref[...])
+    sub = iota(lead.shape, 0)
+    lowered = jnp.where(sub == 0, sides[0:1] * tile[0], jnp.where(sub == 1, sides[1:2] * tile[1], 0.0))
+    record = jnp.concatenate([lead - lowered, record_ref[:, moved:]], axis=1)
     corners = [[next_ref[2 * i + c : 2 * i + c + 1] for c in range(2)] for i in range(4)]
     last = bilinear(corners, [record[0:1], record[1:2]], cells_ref[STEPS - 1, 0])
     blank = jnp.zeros((6, slots), f32)
-    columns = [record[2:3], last[0], blank, record[3:4], last[1], blank]
+    columns = [last[0], blank, record[2:3], last[1], blank, record[3:4]]
     high, low = halves(jnp.concatenate(columns, axis=0))
     both = jnp.concatenate([high, low], axis=0)
     target = target_ref[:, 0:1]
     chunk = 256
+    row = iota((8, LANES), 0)
+    wide = iota((8, chunk), 0)
     for start in range(0, total, chunk):
         onehot = picked(target == start + iota((slots, chunk), 1)).astype(bf16)
         product = jnp.dot(both, onehot, preferred_element_type=f32)
-        placed = product[:16] + product[16:]
+        values = product[:16] + product[16:]
         if paired:
             for at in range(0, chunk, LANES):
-                left, right = paired_halves(placed[:8, at : at + LANES], placed[8:, at : at + LANES], width)
-                number = (start + at) // width
-                out_ref[number] = left
-                out_ref[number + 1] = right
+                pair = paired_halves(values[:8, at : at + LANES], values[8:, at : at + LANES], width)
+                for i in range(2):
+                    number = (start + at) // width + i
+                    out_ref[number, 0 : rows - 8] = placed_ref[number, 0 : rows - 8]
+                    out_ref[number, rows - 8 : rows] = jnp.where(row == 7, pair[i], placed_ref[number, rows - 8 : rows])
+                    out_ref[number, rows : rows + 8] = jnp.where(row == 0, pair[i], 0.0)
         else:
-            out_ref[0, :, start : start + chunk] = placed[:8]
-            out_ref[1, :, start : start + chunk] = placed[8:]
-
-
-def filter_kernel(width, paired, matrix_ref, arrived_ref, out_ref):
-    outs, depth = matrix_ref.shape
-    high, low = halves(matrix_ref[...])
+            span = slice(start, start + chunk)
+            for c in range(2):
+                value = values[8 * c : 8 * c + 8]
+                out_ref[c, 0 : rows - 8, span] = placed_ref[c, 0 : rows - 8, span]
+                out_ref[c, rows - 8 : rows, span] = jnp.where(wide == 7, value, placed_ref[c, rows - 8 : rows, span])
+                out_ref[c, rows : rows + 8, span] = jnp.where(wide == 0, value, 0.0)
+
+
+def filter_kernel(width, paired, matrix_ref, arrived_ref, out_ref, wide_ref):
+    depth = arrived_ref.shape[1]
+    samples = matrix_ref.shape[0]
+    wide_ref[...] = jnp.zeros_like(wide_ref)
+    wide_ref[0:samples, 0:samples] = matrix_ref[...]
+    high, low = halves(wide_ref[:, 0:depth])
     left = jnp.concatenate([high, low, high], axis=1)
-    total = out_ref.shape[2]
-    chunk = 512
-    for start in range(0, total, chunk):
+    groups = out_ref.shape[0] // (2 * samples)
+    step = 4
+    for first in range(0, groups, step):
+        start = first * LANES
         if paired:
             tiles = [
                 paired_halves(arrived_ref[at // width], arrived_ref[at // width + 1], width)
-                for at in range(start, start + chunk, LANES)
+                for at in range(start, start + step * LANES, LANES)
             ]
             columns = [jnp.concatenate([t[c] for t in tiles], axis=1) for c in range(2)]
         else:
-            columns = [arrived_ref[c, :, start : start + chunk] for c in range(2)]
+            columns = [arrived_ref[c, :, start : start + step * LANES] for c in range(2)]
         for c in range(2):
             x_high, x_low = halves(columns[c])
             right = jnp.concatenate([x_high, x_high, x_low], axis=0)
             product = jnp.dot(left, right, preferred_element_type=f32)
-            out_ref[c, :, start : start + chunk] = product[: out_ref.shape[1]]
-
-
-def cost(flops, moved):
-    return pl.CostEstimate(flops=flops, bytes_accessed=moved, transcendentals=0)
-
-
-def sides_of(counts, axis):
-    slot = iota((1, 8 * MOST), 1)
-    offsets = jnp.cumsum(counts) - counts
-    result = jnp.zeros((1, 8 * MOST), jnp.int32)
-    for j in range(8):
-        inside = (slot >= offsets[j]) & (slot < offsets[j] + counts[j])
-        result = result + jnp.where(inside, moves[j][axis], 0)
-    return result
-
-
-def moved_along(value, side, axis):
-    forward = shifted(value, axis, 1)
-    backward = shifted(value, axis, -1)
-    return jnp.where(side == 1, forward, jnp.where(side == -1, backward, value))
+            for g in range(step):
+                rows = pl.ds(2 * (first + g) + c, samples, stride=2 * groups)
+                out_ref[rows, :] = product[:samples, g * LANES : (g + 1) * LANES]
 
 
 def per_device(velocity, start_position, cells, history, leavers, owner, filter_matrix):
@@ -290,70 +339,58 @@
     tile_count = lax.axis_size("ty") * lax.axis_size("tx")
     per_owner = 4 * slots // tile_count
     paired = 2 * per_owner == LANES
+    groups = slots // LANES
     north = shifted(velocity[:, :, tile_rows - 1], "ty", 1)
     south = shifted(velocity[:, :, 0], "ty", -1)
     west = shifted(jnp.stack([velocity[:, :, :, tile_cols - 1], north, south]), "tx", 1)
     east = shifted(jnp.stack([velocity[:, :, :, 0], north, south]), "tx", -1)
     halo = (velocity, north, south, west, east)
-    point = start_position
-    first = jnp.zeros((8, slots), f32)
-    moved_history = history
-    record = None
-    for step in range(STEPS):
-        if step == STEPS - 1:
-            waiting = first
-        results = run_step(step, halo, point, first, cells)
-        if step == STEPS - 1:
-            break
-        record, first = results
-        counts = leavers[step]
-        band = step * 8 * MOST
-        side_y, side_x = sides_of(counts, 0), sides_of(counts, 1)
-        part = record[:, band : band + 8 * MOST]
-        part = moved_along(moved_along(part, side_y, "ty"), side_x, "tx")
-        lowered = jnp.concatenate([side_y * tile_rows, side_x * tile_cols, jnp.zeros((6, 8 * MOST), jnp.int32)], axis=0)
-        part = part - lowered.astype(f32)
-        past = history[:, :, band : band + 8 * MOST]
-        past = moved_along(moved_along(past, side_y, "ty"), side_x, "tx")
-        point = jnp.concatenate([part[0:2], record[0:2, 8 * MOST :]], axis=1)
-    depth = up(HISTORY, 8) + 8
-    shape = (tile_count, depth, LANES) if paired else (2, depth, tile_count * per_owner)
+    sides = find_sides(leavers)
+    by_rows = history.reshape(2, HISTORY, groups, LANES).transpose(1, 2, 0, 3)
+    past = by_rows[:, 0].reshape(2 * HISTORY, LANES)
+    past = chosen(sides[0, 0:1], past, shifted(past, "ty", 1), shifted(past, "ty", -1))
+    past_west, past_east = shifted(past, "tx", 1), shifted(past, "tx", -1)
+    record, lead, first = run_step(0, halo, start_position, None, cells)
+    lead = chosen(sides[0, 0:1], lead, shifted(lead, "ty", 1), shifted(lead, "ty", -1))
+    lead_west, lead_east = shifted(lead, "tx", 1), shifted(lead, "tx", -1)
+    rows = up(HISTORY, 8)
+    shape = (tile_count, rows, LANES) if paired else (2, rows, tile_count * per_owner)
     placed, target = pl.pallas_call(
         functools.partial(place_history_kernel, per_owner, paired),
         out_shape=[jax.ShapeDtypeStruct(shape, f32), jax.ShapeDtypeStruct((slots, LANES), jnp.int32)],
-        in_specs=whole(4),
+        in_specs=whole(6),
         out_specs=whole(2),
-        cost_estimate=cost(2 * 4 * 80 * slots * 4 * slots, 3000000),
+        cost_estimate=cost(2 * 4 * rows * slots * 4 * slots, 3000000),
+        compiler_params=grant,
         name="place_history",
-    )(history, past, owner, owner.reshape(1, slots))
-    blocks = (tile_count, 8, LANES) if paired else (2, 8, tile_count * per_owner)
-    placed = pl.pallas_call(
-        functools.partial(place_samples_kernel, per_owner, paired),
+    )(by_rows.reshape(2 * groups * HISTORY, LANES), past, past_west, past_east, sides, owner.reshape(1, slots))
+    shape = (shape[0], rows + 8, shape[2])
+    outgoing = pl.pallas_call(
+        functools.partial(place_samples_kernel, per_owner, paired, (float(tile_rows), float(tile_cols))),
         out_shape=jax.ShapeDtypeStruct(shape, f32),
-        grid=(1,),
-        in_specs=[pl.BlockSpec(s, lambda i, n=len(s): (0,) * n) for s in (record.shape, part.shape, waiting.shape, cells.shape, target.shape)]
-        + [pl.BlockSpec(memory_space=pl.ANY)],
-        out_specs=pl.BlockSpec(blocks, lambda i: (0, depth // 8 - 1, 0)),
-        input_output_aliases={5: 0},
-        cost_estimate=cost(2 * 2 * 16 * slots * 4 * slots, 1000000),
+        in_specs=whole(9),
+        out_specs=whole(1)[0],
+        cost_estimate=cost(2 * 2 * 16 * slots * 4 * slots, 3000000),
+        compiler_params=grant,
         name="place_samples",
-    )(record, part, waiting, cells, target, placed)
+    )(record, lead, lead_west, lead_east, sides, first, cells, target, placed)
     if not paired:
-        placed = placed.reshape(2, depth, tile_count, per_owner).transpose(2, 1, 0, 3)
-    arrived = lax.all_to_all(placed, ("ty", "tx"), split_axis=0, concat_axis=0, tiled=True)
+        outgoing = outgoing.reshape(2, rows + 8, tile_count, per_owner).transpose(2, 1, 0, 3)
+    arrived = lax.all_to_all(outgoing, ("ty", "tx"), split_axis=0, concat_axis=0, tiled=True)
     if not paired:
         arrived = arrived.transpose(2, 1, 0, 3).reshape(shape)
-    matrix = jnp.zeros((up(SAMPLES, 16), depth), f32)
-    matrix = matrix.at[:SAMPLES, :HISTORY].set(filter_matrix[:, :HISTORY])
-    matrix = matrix.at[:SAMPLES, depth - 8 : depth - 8 + STEPS].set(filter_matrix[:, HISTORY:])
-    return pl.pallas_call(
+    filtered = pl.pallas_call(
         functools.partial(filter_kernel, per_owner, paired),
-        out_shape=jax.ShapeDtypeStruct((2, SAMPLES, tile_count * per_owner), f32),
+        out_shape=jax.ShapeDtypeStruct((SAMPLES * 4 * groups * 2, LANES), f32),
         in_specs=whole(2),
         out_specs=whole(1)[0],
+        scratch_shapes=[pltpu.VMEM((rows + 8, LANES), f32)],
         cost_estimate=cost(2 * 3 * 80 * 80 * 8 * slots, 3000000),
+        compiler_params=grant,
         name="filter_series",
-    )(matrix, arrived)
+    )(filter_matrix, arrived)
+    filtered = filtered.reshape(SAMPLES, 4 * groups, 2, LANES)
+    return filtered.transpose(2, 0, 1, 3).reshape(2, SAMPLES, 4 * slots)
 
 
 def solution(mesh):

time: 114 us -> 71.2 us (0.62)
  blocking collectives: 0 us -> 34.8 us
  waiting for transfers between devices: 31 us -> 12.2 us
  other arithmetic: 17.1 us -> 0.03 us
  starting transfers between devices: 27.1 us -> 14 us
  local copies, waits for them, and re-layouts: 14.4 us -> 2.53 us
  between operations: 10.2 us -> 0.12 us
  Pallas kernels: 13 us -> 7.3 us
    all_to_all x0 -> x1, blocking collectives: none -> 34.8 us  [per_device(): lax.all_to_all(outgoing, ('ty', 'tx'), split_axis=0, concat_axis=0, tiled...]
    all_to_all x1 -> x0, waiting for transfers between devices: 27.7 us -> none  [per_device(): lax.all_to_all(placed, ('ty', 'tx'), split_axis=0, concat_axis=0, tiled=T...]
    ppermute x12, waiting for transfers between devices: 3.3 us -> 12.2 us  [shifted(): lax.ppermute(value, axis, [(i, (i + by) % peers) for i in range(peers)])]
    eq x4 -> x0, other arithmetic: 7.4 us -> none  [moved_along(): return jnp.where(side == 1, forward, jnp.where(side == -1, backward, value))]
    ppermute x12, starting transfers between devices: 21 us -> 14 us  [shifted(): lax.ppermute(value, axis, [(i, (i + by) % peers) for i in range(peers)])]
    all_to_all x1 -> x0, starting transfers between devices: 6.11 us -> none  [per_device(): lax.all_to_all(placed, ('ty', 'tx'), split_axis=0, concat_axis=0, tiled=T...]
    mul x1 -> x0, other arithmetic: 4.93 us -> none  [per_device(): side_x * tile_cols]
    pallas_call x1 -> x0, local copies, waits for them, and re-layouts: 3.26 us -> none  [per_device(): pl.pallas_call(functools.partial(filter_kernel, per_owner, paired), out_s...]
  transfers between devices with their start and end apart: 13 -> 12, of which waited for: 3 -> 7; matrix products, arithmetic and copies ran while one was open for 23% -> 2% of each run, Pallas kernels for 4% -> 6%
where the time goes in v2:
time: 71.2 us; the launch traced here: 71 us
  blocking collectives  34.8 us (49%)
  starting transfers between devices  14 us (20%)
  waiting for transfers between devices  12.2 us (17%)
  Pallas kernels  7.3 us (10%)
  local copies, waits for them, and re-layouts  2.53 us (4%)
    all_to_all x1, blocking collectives, per_device(): lax.all_to_all(outgoing, ('ty', 'tx'), split_axis=0, concat_axis=0, tiled...  34.8 us
    ppermute x12, starting transfers between devices, shifted(): lax.ppermute(value, axis, [(i, (i + by) % peers) for i in range(peers)])  14 us
    ppermute x12, waiting for transfers between devices, shifted(): lax.ppermute(value, axis, [(i, (i + by) % peers) for i in range(peers)])  12.2 us
    pallas_call x1, Pallas kernels, run_step(): pl.pallas_call(functools.partial(step_kernel, step, following), out_shape...  2.57 us
    pallas_call x1, Pallas kernels, per_device(): pl.pallas_call(functools.partial(filter_kernel, per_owner, paired), out_s...  2.21 us
  transfers between devices with their start and end apart: 12, of which 7 were waited for; matrix products, arithmetic and copies ran while one was open for 2% of the time, Pallas kernels for 6%

profile of v2, /device:TPU:0, one launch (start us, length us, event | category | flops | bytes accessed | tf_op | source)
XLA Modules:
  0.0 71.0 jit_solution(9303113611967257960)
XLA Ops:
  0.0 1.1 %bitcast_bitcast_fusion = f32[71,4,2,128]{3,2,0,1:T(2,128)S(1)} fusion(f32[2,71,512]{2,0,1:T(2,128)} %param.10), kind=kLoop, calls=%fused_computation | loop fusion | bytes 581632 | tf_op jit(solution)/shard_map/transpose | solution.py:349
  1.1 0.0 copy-start.3
  1.1 0.0 copy-start.5
  1.2 0.1 reshape_squeeze.3
  1.2 2.5 %collective-permute-start.9 = (f32[142,128]{1,0:T(8,128)S(1)}, f32[142,128]{1,0:T(8,128)S(1)}, u32[]{:S(2)}, u32[]{:S(2)}) collective-permute-start(f32[142,128]{1,0:T(8,128)S(1)} %reshape_squeeze.3), channel_id=1, source_target_pairs={{0,24},{8,0},{16,8},{24,16},{1,25},{9,1},{17,9},{25,17},{2,26},{10... | collective-permute-start | bytes 218120 | tf_op jit(solution)/shard_map/ppermute | solution.py:29
  3.7 0.8 %fusion.1 = (f32[2,3,1,128]{3,2,1,0:T(1,128)S(1)}, f32[2,3,1,128]{3,2,1,0:T(1,128)S(1)}) fusion(f32[2,3,128,128]{3,2,1,0:T(8,128)} %velocity_ref.1), kind=kLoop, calls=%fused_computation.12 | loop fusion | bytes 12288 | tf_op jit(solution)/shard_map/slice | solution.py:344
  4.4 0.8 %collective-permute-start = (f32[2,3,128]{2,1,0:T(4,128)S(1)}, f32[2,3,128]{2,1,0:T(4,128)S(1)}, u32[]{:S(2)}, u32[]{:S(2)}) collective-permute-start(f32[2,3,128]{2,1,0:T(4,128)S(1)} %bitcast.40), channel_id=1, source_target_pairs={{0,8},{8,16},{16,24},{24,0},{1,9},{9,17},{17,25},{25,1},{2,10},{10... | collective-permute-start | bytes 9224 | tf_op jit(solution)/shard_map/ppermute | solution.py:29
  5.2 1.1 %collective-permute-start.1 = (f32[2,3,128]{2,1,0:T(4,128)S(1)}, f32[2,3,128]{2,1,0:T(4,128)S(1)}, u32[]{:S(2)}, u32[]{:S(2)}) collective-permute-start(f32[2,3,128]{2,1,0:T(4,128)S(1)} %bitcast.41), channel_id=1, source_target_pairs={{0,24},{8,0},{16,8},{24,16},{1,25},{9,1},{17,9},{25,17},{2,26},{10... | collective-permute-start | bytes 9224 | tf_op jit(solution)/shard_map/ppermute | solution.py:29
  6.3 0.2 fusion
  6.5 0.6 find_sides.1.sides_ref
  7.1 0.2 copy.19
  7.2 0.2 copy.18
  7.4 0.1 collective-permute-done.north_ref
  7.5 0.1 collective-permute-done.1.south_ref
  7.6 4.6 %collective-permute-start.3 = (f32[3,2,3,128]{3,2,1,0:T(4,128)S(1)}, f32[3,2,3,128]{3,2,1,0:T(4,128)S(1)}, u32[]{:S(2)}, u32[]{:S(2)}) collective-permute-start(f32[3,2,3,128]{3,2,1,0:T(4,128)S(1)} %get-tuple-element.19), channel_id=1, source_target_pairs={{0,7},{1,0},{2,1},{3,2},{4,3},{5,4},{6,5},{7,6},{8,15},{9,8},{10,9... | collective-permute-start | bytes 27656 | tf_op jit(solution)/shard_map/ppermute | solution.py:29
  12.2 0.0 copy-start.6
  12.2 1.4 %collective-permute-done.3.east_ref = f32[3,2,3,128]{3,2,1,0:T(4,128)S(1)} collective-permute-done((f32[3,2,3,128]{3,2,1,0:T(4,128)S(1)}, f32[3,2,3,128]{3,2,1,0:T(4,128)S(1)}, u32[]{:S(2)}, u32[]{:S(2)}) %collective-permute-start.3) | collective-permute-done | bytes 9248 | tf_op jit(solution)/shard_map/ppermute | solution.py:29
  13.6 5.0 %collective-permute-done.2.west_ref = f32[3,2,3,128]{3,2,1,0:T(4,128)S(1)} collective-permute-done((f32[3,2,3,128]{3,2,1,0:T(4,128)S(1)}, f32[3,2,3,128]{3,2,1,0:T(4,128)S(1)}, u32[]{:S(2)}, u32[]{:S(2)}) %collective-permute-start.2) | collective-permute-done | bytes 9248 | tf_op jit(solution)/shard_map/ppermute | solution.py:29
  18.6 2.6 %sample_step.1 = (f32[8,512]{1,0:T(8,128)S(1)}, f32[8,128]{1,0:T(8,128)S(1)}, f32[8,512]{1,0:T(8,128)S(1)}) custom-call(f32[2,3,128,128]{3,2,1,0:T(8,128)S(1)} %copy-done, f32[2,3,128]{2,1,0:T(4,128)S(1)} %collective-permute-done.north_ref, f32[2,3,128]{2,1,0:T(4,128)S(1)} %collective-permute-done.1.south_ref, ...), custom_call_target="tpu_custom_call" | custom-call | flops 1509949440 | bytes 600000 | tf_op jit(solution)/shard_map/sample_step/pallas_call | solution.py:179
  21.2 0.4 collective-permute-start.5
  21.6 0.2 collective-permute-start.4
  21.8 0.5 collective-permute-start.11
  22.2 1.6 %collective-permute-start.10 = (f32[142,128]{1,0:T(8,128)S(1)}, f32[142,128]{1,0:T(8,128)S(1)}, u32[]{:S(2)}, u32[]{:S(2)}) collective-permute-start(f32[142,128]{1,0:T(8,128)S(1)} %select_select_fusion.past_ref), channel_id=1, source_target_pairs={{0,1},{1,2},{2,3},{3,4},{4,5},{5,6},{6,7},{7,0},{8,9},{9,10},{10,1... | collective-permute-start | bytes 218120 | tf_op jit(solution)/shard_map/ppermute | solution.py:29
  23.8 0.7 %collective-permute-done.4 = f32[8,128]{1,0:T(8,128)S(1)} collective-permute-done((f32[8,128]{1,0:T(8,128)S(1)}, f32[8,128]{1,0:T(8,128)S(1)}, u32[]{:S(2)}, u32[]{:S(2)}) %collective-permute-start.4) | collective-permute-done | bytes 4128 | tf_op jit(solution)/shard_map/ppermute | solution.py:29
  24.6 2.4 %collective-permute-start.7 = (f32[8,128]{1,0:T(8,128)S(1)}, f32[8,128]{1,0:T(8,128)S(1)}, u32[]{:S(2)}, u32[]{:S(2)}) collective-permute-start(f32[8,128]{1,0:T(8,128)S(1)} %select_select_fusion.1.lead_ref), channel_id=1, source_target_pairs={{0,7},{1,0},{2,1},{3,2},{4,3},{5,4},{6,5},{7,6},{8,15},{9,8},{10,9... | collective-permute-start | bytes 12296 | tf_op jit(solution)/shard_map/ppermute | solution.py:29
  27.0 2.7 %collective-permute-done.10.west_ref = f32[142,128]{1,0:T(8,128)S(1)} collective-permute-done((f32[142,128]{1,0:T(8,128)S(1)}, f32[142,128]{1,0:T(8,128)S(1)}, u32[]{:S(2)}, u32[]{:S(2)}) %collective-permute-start.10) | collective-permute-done | bytes 72736 | tf_op jit(solution)/shard_map/ppermute | solution.py:29
  29.8 1.4 %place_history.1 = (f32[32,72,128]{2,1,0:T(8,128)S(1)}, s32[512,128]{1,0:T(8,128)S(1)}) custom-call(f32[568,128]{1,0:T(8,128)S(1)} %bitcast.34, f32[142,128]{1,0:T(8,128)S(1)} %select_select_fusion.past_ref, f32[142,128]{1,0:T(8,128)S(1)} %collective-permute-done.10.west_ref, f32[142,128]{1,0:T(8,128)S(1)} %collective-permute-done.11.east_ref, ...), custom_call_target="tpu_custom_call" | custom-call | flops 603979776 | bytes 3000000 | tf_op jit(solution)/shard_map/place_history/pallas_call | solution.py:358
  31.2 2.2 %collective-permute-done.6.west_ref = f32[8,128]{1,0:T(8,128)S(1)} collective-permute-done((f32[8,128]{1,0:T(8,128)S(1)}, f32[8,128]{1,0:T(8,128)S(1)}, u32[]{:S(2)}, u32[]{:S(2)}) %collective-permute-start.6) | collective-permute-done | bytes 4128 | tf_op jit(solution)/shard_map/ppermute | solution.py:29
  33.3 0.6 place_samples.1
  34.0 0.0 copy-start.2
  34.0 34.8 %all_to_all.5.arrived_ref = f32[32,80,128]{2,1,0:T(8,128)S(1)} all-to-all(f32[32,80,128]{2,1,0:T(8,128)S(1)} %place_samples.1), channel_id=1, replica_groups=mesh['ty'=4,'tx'=8] {'ty','tx'}, dimensions={0} | all-to-all | bytes 2621440 | tf_op jit(solution)/shard_map/all_to_all | solution.py:379
  68.8 2.2 %filter_series.1 = f32[2336,128]{1,0:T(8,128)} custom-call(f32[73,73]{1,0:T(8,128)S(1)} %copy-done.2, f32[32,80,128]{2,1,0:T(8,128)S(1)} %all_to_all.5.arrived_ref), custom_call_target="tpu_custom_call" | custom-call | flops 157286400 | bytes 3000000 | tf_op jit(solution)/shard_map/filter_series/pallas_call | solution.py:382
  (25 shorter events, 0.1 us)
Async XLA Ops:
  0.0 6.3 %copy-start = (f32[2,3,128,128]{3,2,1,0:T(8,128)S(1)}, f32[2,3,128,128]{3,2,1,0:T(8,128)}, u32[]{:S(2)}) copy-start(f32[2,3,128,128]{3,2,1,0:T(8,128)} %velocity_ref.1) | copy-start | bytes 1179652
  0.0 6.5 %copy-start.4 = (s32[1,8]{1,0:T(1,128)S(1)}, s32[1,8]{1,0:T(1,128)}, u32[]{:S(2)}) copy-start(s32[1,8]{1,0:T(1,128)} %leavers_ref.1) | copy-start | bytes 100
  1.1 17.5 %copy-start.3 = (s32[2,4,2,512]{3,2,1,0:T(2,128)S(1)}, s32[2,4,2,512]{3,2,1,0:T(2,128)}, u32[]{:S(2)}) copy-start(s32[2,4,2,512]{3,2,1,0:T(2,128)} %cells_ref.3) | copy-start | bytes 98308
  1.1 17.5 %copy-start.5 = (f32[2,512]{1,0:T(2,128)S(1)}, f32[2,512]{1,0:T(2,128)}, u32[]{:S(2)}) copy-start(f32[2,512]{1,0:T(2,128)} %point_ref.1) | copy-start | bytes 12292
  1.2 20.5 %collective-permute-start.9 = (f32[142,128]{1,0:T(8,128)S(1)}, f32[142,128]{1,0:T(8,128)S(1)}, u32[]{:S(2)}, u32[]{:S(2)}) collective-permute-start(f32[142,128]{1,0:T(8,128)S(1)} %reshape_squeeze.3), channel_id=1, source_target_pairs={{0,24},{8,0},{16,8},{24,16},{1,25},{9,1},{17,9},{25,17},{2,26},{10... | collective-permute-start | bytes 218120 | tf_op jit(solution)/shard_map/ppermute | solution.py:29
  3.7 18.1 %collective-permute-start.8 = (f32[142,128]{1,0:T(8,128)S(1)}, f32[142,128]{1,0:T(8,128)S(1)}, u32[]{:S(2)}, u32[]{:S(2)}) collective-permute-start(f32[142,128]{1,0:T(8,128)S(1)} %reshape_squeeze.3), channel_id=1, source_target_pairs={{0,8},{8,16},{16,24},{24,0},{1,9},{9,17},{17,25},{25,1},{2,10},{10... | collective-permute-start | bytes 218120 | tf_op jit(solution)/shard_map/ppermute | solution.py:29
  4.4 3.1 %collective-permute-start = (f32[2,3,128]{2,1,0:T(4,128)S(1)}, f32[2,3,128]{2,1,0:T(4,128)S(1)}, u32[]{:S(2)}, u32[]{:S(2)}) collective-permute-start(f32[2,3,128]{2,1,0:T(4,128)S(1)} %bitcast.40), channel_id=1, source_target_pairs={{0,8},{8,16},{16,24},{24,0},{1,9},{9,17},{17,25},{25,1},{2,10},{10... | collective-permute-start | bytes 9224 | tf_op jit(solution)/shard_map/ppermute | solution.py:29
  5.2 2.4 %collective-permute-start.1 = (f32[2,3,128]{2,1,0:T(4,128)S(1)}, f32[2,3,128]{2,1,0:T(4,128)S(1)}, u32[]{:S(2)}, u32[]{:S(2)}) collective-permute-start(f32[2,3,128]{2,1,0:T(4,128)S(1)} %bitcast.41), channel_id=1, source_target_pairs={{0,24},{8,0},{16,8},{24,16},{1,25},{9,1},{17,9},{25,17},{2,26},{10... | collective-permute-start | bytes 9224 | tf_op jit(solution)/shard_map/ppermute | solution.py:29
  7.6 6.0 %collective-permute-start.3 = (f32[3,2,3,128]{3,2,1,0:T(4,128)S(1)}, f32[3,2,3,128]{3,2,1,0:T(4,128)S(1)}, u32[]{:S(2)}, u32[]{:S(2)}) collective-permute-start(f32[3,2,3,128]{3,2,1,0:T(4,128)S(1)} %get-tuple-element.19), channel_id=1, source_target_pairs={{0,7},{1,0},{2,1},{3,2},{4,3},{5,4},{6,5},{7,6},{8,15},{9,8},{10,9... | collective-permute-start | bytes 27656 | tf_op jit(solution)/shard_map/ppermute | solution.py:29
  12.2 6.4 %collective-permute-start.2 = (f32[3,2,3,128]{3,2,1,0:T(4,128)S(1)}, f32[3,2,3,128]{3,2,1,0:T(4,128)S(1)}, u32[]{:S(2)}, u32[]{:S(2)}) collective-permute-start(f32[3,2,3,128]{3,2,1,0:T(4,128)S(1)} %get-tuple-element.20), channel_id=1, source_target_pairs={{0,1},{1,2},{2,3},{3,4},{4,5},{5,6},{6,7},{7,0},{8,9},{9,10},{10,1... | collective-permute-start | bytes 27656 | tf_op jit(solution)/shard_map/ppermute | solution.py:29
  12.2 17.6 %copy-start.1 = (f32[2,71,512]{2,0,1:T(2,128)S(1)}, f32[2,71,512]{2,0,1:T(2,128)}, u32[]{:S(2)}) copy-start(f32[2,71,512]{2,0,1:T(2,128)} %param.10) | copy-start | bytes 872452
  12.2 17.6 %copy-start.6 = (s32[512,1]{0,1:T(1,128)S(1)}, s32[512,1]{0,1:T(1,128)}, u32[]{:S(2)}) copy-start(s32[512,1]{0,1:T(1,128)} %param.12) | copy-start | bytes 6148
  21.2 2.7 %collective-permute-start.5 = (f32[8,128]{1,0:T(8,128)S(1)}, f32[8,128]{1,0:T(8,128)S(1)}, u32[]{:S(2)}, u32[]{:S(2)}) collective-permute-start(f32[8,128]{1,0:T(8,128)S(1)} %get-tuple-element.11), channel_id=1, source_target_pairs={{0,24},{8,0},{16,8},{24,16},{1,25},{9,1},{17,9},{25,17},{2,26},{10... | collective-permute-start | bytes 12296 | tf_op jit(solution)/shard_map/ppermute | solution.py:29
  21.6 3.0 %collective-permute-start.4 = (f32[8,128]{1,0:T(8,128)S(1)}, f32[8,128]{1,0:T(8,128)S(1)}, u32[]{:S(2)}, u32[]{:S(2)}) collective-permute-start(f32[8,128]{1,0:T(8,128)S(1)} %get-tuple-element.11), channel_id=1, source_target_pairs={{0,8},{8,16},{16,24},{24,0},{1,9},{9,17},{17,25},{25,1},{2,10},{10... | collective-permute-start | bytes 12296 | tf_op jit(solution)/shard_map/ppermute | solution.py:29
  21.8 5.3 %collective-permute-start.11 = (f32[142,128]{1,0:T(8,128)S(1)}, f32[142,128]{1,0:T(8,128)S(1)}, u32[]{:S(2)}, u32[]{:S(2)}) collective-permute-start(f32[142,128]{1,0:T(8,128)S(1)} %select_select_fusion.past_ref), channel_id=1, source_target_pairs={{0,7},{1,0},{2,1},{3,2},{4,3},{5,4},{6,5},{7,6},{8,15},{9,8},{10,9... | collective-permute-start | bytes 218120 | tf_op jit(solution)/shard_map/ppermute | solution.py:29
  22.2 7.5 %collective-permute-start.10 = (f32[142,128]{1,0:T(8,128)S(1)}, f32[142,128]{1,0:T(8,128)S(1)}, u32[]{:S(2)}, u32[]{:S(2)}) collective-permute-start(f32[142,128]{1,0:T(8,128)S(1)} %select_select_fusion.past_ref), channel_id=1, source_target_pairs={{0,1},{1,2},{2,3},{3,4},{4,5},{5,6},{6,7},{7,0},{8,9},{9,10},{10,1... | collective-permute-start | bytes 218120 | tf_op jit(solution)/shard_map/ppermute | solution.py:29
  24.6 6.6 %collective-permute-start.7 = (f32[8,128]{1,0:T(8,128)S(1)}, f32[8,128]{1,0:T(8,128)S(1)}, u32[]{:S(2)}, u32[]{:S(2)}) collective-permute-start(f32[8,128]{1,0:T(8,128)S(1)} %select_select_fusion.1.lead_ref), channel_id=1, source_target_pairs={{0,7},{1,0},{2,1},{3,2},{4,3},{5,4},{6,5},{7,6},{8,15},{9,8},{10,9... | collective-permute-start | bytes 12296 | tf_op jit(solution)/shard_map/ppermute | solution.py:29
  27.0 6.3 %collective-permute-start.6 = (f32[8,128]{1,0:T(8,128)S(1)}, f32[8,128]{1,0:T(8,128)S(1)}, u32[]{:S(2)}, u32[]{:S(2)}) collective-permute-start(f32[8,128]{1,0:T(8,128)S(1)} %select_select_fusion.1.lead_ref), channel_id=1, source_target_pairs={{0,1},{1,2},{2,3},{3,4},{4,5},{5,6},{6,7},{7,0},{8,9},{9,10},{10,1... | collective-permute-start | bytes 12296 | tf_op jit(solution)/shard_map/ppermute | solution.py:29
  34.0 34.8 %copy-start.2 = (f32[73,73]{1,0:T(8,128)S(1)}, f32[73,73]{1,0:T(8,128)}, u32[]{:S(2)}) copy-start(f32[73,73]{1,0:T(8,128)} %matrix_ref.1) | copy-start | bytes 63952

commit v3 on v2

v3 whole, which is shorter than its diff:
```python
import functools

import jax
import jax.numpy as jnp
from jax import lax
from jax.experimental import pallas as pl
from jax.experimental.pallas import tpu as pltpu
from jax.sharding import Mesh
from jax.sharding import PartitionSpec as P


STEPS = 2
SAMPLES = 73
HISTORY = 71
MOST = 16


drift = 0.2
moves = ((-1, -1), (-1, 0), (-1, 1), (0, -1), (0, 1), (1, -1), (1, 0), (1, 1))
f32 = jnp.float32
bf16 = jnp.bfloat16
LANES = 128


def up(value, to):
    return -(-value // to) * to


places = {"ty": "ty", "tx": ("half", "within")}


def shifted(value, axis, by):
    peers = lax.axis_size(places[axis])
    return lax.ppermute(value, places[axis], [(i, (i + by) % peers) for i in range(peers)])


def swapped(value):
    return lax.ppermute(value, "half", [(0, 1), (1, 0)])


def halves(value):
    high = value.astype(bf16)
    return high, (value - high.astype(f32)).astype(bf16)


def picked(condition):
    return jnp.where(condition, 1.0, 0.0).astype(f32)


def iota(shape, dim):
    return lax.broadcasted_iota(jnp.int32, shape, dim)


def whole(count):
    return [pl.BlockSpec(memory_space=pltpu.VMEM) for _ in range(count)]


def cost(flops, moved):
    return pl.CostEstimate(flops=flops, bytes_accessed=moved, transcendentals=0)


grant = pltpu.CompilerParams(vmem_limit_bytes=16 * 1024 * 1024)


def build_table(table_ref, number, snapshots, weight, velocity_ref, north_ref, south_ref, west_ref, east_ref, columns):
    rows, cols = velocity_ref.shape[2], velocity_ref.shape[3]
    count = velocity_ref.shape[1]
    base = 2 * HISTORY
    block = up(rows + 2, 16)
    lane = iota((16, cols), 1)
    sub = iota((16, cols), 0)
    for c in range(2):
        inner = None
        for a in snapshots:
            k = c * count + a
            body = velocity_ref[c, a]
            side = pltpu.roll(columns, (cols - k) % cols, 1)
            at = base + k
            top, low = north_ref[at : at + 1], south_ref[at : at + 1]
            edge = jnp.where(sub == 0, top, jnp.where(sub == 1, low, 0.0))
            at += 2 * count
            north_west, north_east = west_ref[at : at + 1, cols - 1 :], east_ref[at : at + 1, 0:1]
            at += 2 * count
            south_west, south_east = west_ref[at : at + 1, cols - 1 :], east_ref[at : at + 1, 0:1]
            west = jnp.where(sub == 0, north_west, jnp.where(sub == 1, south_west, 0.0))
            east = jnp.where(sub == 0, north_east, jnp.where(sub == 1, south_east, 0.0))
            corner = jnp.where(lane == 0, west, jnp.where(lane == 8, east, 0.0))
            parts = (body, side, edge, corner)
            inner = parts if inner is None else tuple(p + q for p, q in zip(inner, parts))
        body, side, edge, corner = (weight * p if weight != 1.0 else p for p in inner)
        for split, (b, s, e, n) in enumerate(zip(halves(body), halves(side), halves(edge), halves(corner))):
            at = (split * 2 + c) * block
            table_ref[number, at : at + rows, 0:cols] = b
            table_ref[number, at : at + rows, cols : 2 * cols] = s
            table_ref[number, at + rows : at + block, 0:cols] = e
            table_ref[number, at + rows : at + block, cols : 2 * cols] = n


def read_corners(table_ref, number, cell, rows, cols):
    block = up(rows + 2, 16)
    slots = cell.shape[1]
    cy, cx = cell[0:1], cell[1:2]
    at = iota((2 * cols, slots), 0)
    left = picked(at == jnp.where(cx < 0, cols, cx)).astype(bf16)
    right = picked(at == jnp.where(cx + 1 >= cols, cols + 8, cx + 1)).astype(bf16)
    row = iota((block, slots), 0)
    upper = row == jnp.where(cy < 0, rows, cy)
    lower = row == jnp.where(cy + 1 >= rows, rows + 1, cy + 1)
    table = table_ref[number]
    values = {}
    for side, onehot in enumerate((left, right)):
        product = jnp.dot(table, onehot, preferred_element_type=f32)
        for c in range(2):
            column = product[c * block : (c + 1) * block] + product[(2 + c) * block : (3 + c) * block]
            values[0, side, c] = jnp.sum(jnp.where(upper, column, 0.0), axis=0, keepdims=True)
            values[1, side, c] = jnp.sum(jnp.where(lower, column, 0.0), axis=0, keepdims=True)
    return [[values[v, h, c] for c in range(2)] for v in range(2) for h in range(2)]


def bilinear(corners, point, cell):
    wy = point[0] - cell[0:1].astype(f32)
    wx = point[1] - cell[1:2].astype(f32)
    first, second, third, fourth = corners
    return [
        (1.0 - wy) * ((1.0 - wx) * first[c] + wx * second[c]) + wy * ((1.0 - wx) * third[c] + wx * fourth[c])
        for c in range(2)
    ]


def along(point, factor, speed):
    return [p + factor * s for p, s in zip(point, speed)]


def halo_columns(west_ref, east_ref, count, cols):
    zeros = jnp.zeros((8 - count, cols), f32)
    base = 2 * HISTORY
    west, east = west_ref[base : base + count], east_ref[base : base + count]
    flat = jnp.concatenate([west, zeros, east, zeros, jnp.zeros((cols - 16, cols), f32)], axis=0)
    return flat.T


def step_kernel(step, following, velocity_ref, north_ref, south_ref, west_ref, east_ref, point_ref, cells_ref, *rest):
    if step > 0:
        first_ref, rest = rest[0], rest[1:]
    if following:
        record_ref, lead_ref, next_ref, table_ref = rest
    else:
        record_ref, lead_ref, table_ref = rest
    rows, cols = velocity_ref.shape[2], velocity_ref.shape[3]
    columns = halo_columns(west_ref, east_ref, 2 * velocity_ref.shape[1], cols)
    fields = (velocity_ref, north_ref, south_ref, west_ref, east_ref, columns)
    build_table(table_ref, 0, (step,), 1.0, *fields)
    build_table(table_ref, 1, (step, step + 1), 0.5, *fields)
    build_table(table_ref, 2, (step + 1,), 1.0, *fields)
    sections = [cells_ref[step, s] for s in range(4)]
    if step == 0:
        first = read_corners(table_ref, 0, sections[0], rows, cols)
    else:
        first = [[first_ref[2 * i + c : 2 * i + c + 1] for c in range(2)] for i in range(4)]
    second = read_corners(table_ref, 1, sections[1], rows, cols)
    third = read_corners(table_ref, 1, sections[2], rows, cols)
    fourth = read_corners(table_ref, 2, sections[3], rows, cols)
    point = [point_ref[0:1], point_ref[1:2]]
    k_one = bilinear(first, point, sections[0])
    k_two = bilinear(second, along(point, 0.5 * drift, k_one), sections[1])
    k_three = bilinear(third, along(point, 0.5 * drift, k_two), sections[2])
    k_four = bilinear(fourth, along(point, drift, k_three), sections[3])
    point = [
        p + drift / 6.0 * (a + 2.0 * b + 2.0 * c + d)
        for p, a, b, c, d in zip(point, k_one, k_two, k_three, k_four)
    ]
    blank = [jnp.zeros_like(point[0])] * 4
    record = jnp.concatenate(point + k_one + blank, axis=0)
    record_ref[...] = record
    band = step * 8 * MOST
    lead_ref[...] = record[:, band : band + 8 * MOST]
    if following:
        ahead = read_corners(table_ref, 2, cells_ref[step + 1, 0], rows, cols)
        next_ref[...] = jnp.concatenate([value for corner in ahead for value in corner], axis=0)


def run_step(step, halo, point, first, cells):
    velocity = halo[0]
    slots = point.shape[1]
    following = step + 1 < STEPS
    cols = velocity.shape[3]
    block = up(velocity.shape[2] + 2, 16)
    operands = (*halo, point, cells) + ((first,) if step > 0 else ())
    shape = jax.ShapeDtypeStruct((8, slots), f32)
    shapes = [shape, jax.ShapeDtypeStruct((8, 8 * MOST), f32)] + ([shape] if following else [])
    return pl.pallas_call(
        functools.partial(step_kernel, step, following),
        out_shape=shapes,
        in_specs=whole(len(operands)),
        out_specs=whole(len(shapes)),
        scratch_shapes=[pltpu.VMEM((3, 4 * block, 2 * cols), bf16)],
        cost_estimate=cost(10 * 4 * block * 2 * cols * slots * 2, 600000),
        compiler_params=grant,
        name="sample_step",
    )(*operands)


def sides_kernel(leavers_ref, sides_ref):
    slot = iota((1, 8 * MOST), 1)
    for step in range(leavers_ref.shape[0]):
        rows = [jnp.zeros((1, 8 * MOST), f32) for _ in range(2)]
        start = 0
        for j in range(8):
            end = start + leavers_ref[step, j]
            inside = (slot >= start) & (slot < end)
            rows = [jnp.where(inside, float(moves[j][axis]), rows[axis]) for axis in range(2)]
            start = end
        sides_ref[step] = jnp.concatenate(rows + [jnp.zeros((6, 8 * MOST), f32)], axis=0)


def find_sides(leavers):
    return pl.pallas_call(
        sides_kernel,
        out_shape=jax.ShapeDtypeStruct((leavers.shape[0], 8, 8 * MOST), f32),
        in_specs=[pl.BlockSpec(memory_space=pltpu.SMEM)],
        out_specs=whole(1)[0],
        compiler_params=grant,
        cost_estimate=cost(100000, 5000),
        name="find_sides",
    )(leavers)


def chosen(side, value, forward, backward):
    return jnp.where(side > 0.0, forward, jnp.where(side < 0.0, backward, value))


def paired_halves(first, second, width):
    lane = iota(first.shape, 1)
    left = jnp.where(lane < width, first, pltpu.roll(second, width, 1))
    right = jnp.where(lane < width, pltpu.roll(first, width, 1), second)
    return left, right


def targets_of(owner_row, half, within, width):
    slots = owner_row.shape[1]
    half = half.astype(f32)
    column = jnp.floor((owner_row + 0.5) / within)
    line = jnp.floor((column + 0.5) * 0.5)
    block = line * within + (owner_row - column * within)
    base = jnp.where(column - 2.0 * line == half, block * width, -1.0e6)
    row = iota((LANES, slots), 0)
    turned = jnp.where(row == 0, owner_row, base).T
    owner, base = turned[:, 0:1], turned[:, 1:2]
    before = iota((slots, slots), 1) < iota((slots, slots), 0)
    rank = jnp.sum(picked((owner == owner_row) & before), axis=1, keepdims=True)
    return (base + rank).astype(jnp.int32)


def place_history_kernel(
    width, paired, within, half_ref, owner_ref, history_ref, past_ref, far_owner_ref, far_history_ref, far_past_ref, out_ref, target_ref
):
    slots = owner_ref.shape[1]
    half = half_ref[0]
    rows = up(HISTORY, 8)
    groups = slots // LANES
    moving = 8 * MOST // LANES
    total = out_ref.shape[0] * width if paired else out_ref.shape[3]
    tiles = ((half, owner_ref, history_ref, past_ref), (1 - half, far_owner_ref, far_history_ref, far_past_ref))
    for order, (number, owners, raw, past) in enumerate(tiles):
        target = targets_of(owners[...], half, within, width)
        target_ref[order] = jnp.broadcast_to(target, (slots, LANES))
        parts = []
        for c in range(2):
            pieces = [past[pl.ds(c, HISTORY, stride=2), :]]
            pieces += [raw[pl.ds(2 * g + c, HISTORY, stride=2 * groups), :] for g in range(moving, groups)]
            parts += [jnp.concatenate(pieces, axis=1), jnp.zeros((rows - HISTORY, slots), f32)]
        joined = jnp.concatenate(halves(jnp.concatenate(parts, axis=0)), axis=0)
        chunk = 256
        base = pl.multiple_of(number * rows, 8)
        for start in range(0, total, chunk):
            onehot = picked(target == start + iota((slots, chunk), 1)).astype(bf16)
            product = jnp.dot(joined, onehot, preferred_element_type=f32)
            placed = product[: 2 * rows] + product[2 * rows :]
            if paired:
                for at in range(0, chunk, LANES):
                    pair = paired_halves(placed[:rows, at : at + LANES], placed[rows:, at : at + LANES], width)
                    for i in range(2):
                        out_ref[(start + at) // width + i, pl.ds(base, rows), :] = pair[i]
            else:
                out_ref[number, 0, :, start : start + chunk] = placed[:rows]
                out_ref[number, 1, :, start : start + chunk] = placed[rows:]


def last_samples_kernel(tile, record_ref, lead_ref, west_ref, east_ref, sides_ref, next_ref, cells_ref, out_ref):
    slots = record_ref.shape[1]
    moved = lead_ref.shape[1]
    sides = sides_ref[0]
    lead = chosen(sides[1:2], lead_ref[...], west_ref[...], east_ref[...])
    sub = iota(lead.shape, 0)
    lowered = jnp.where(sub == 0, sides[0:1] * tile[0], jnp.where(sub == 1, sides[1:2] * tile[1], 0.0))
    record = jnp.concatenate([lead - lowered, record_ref[:, moved:]], axis=1)
    corners = [[next_ref[2 * i + c : 2 * i + c + 1] for c in range(2)] for i in range(4)]
    last = bilinear(corners, [record[0:1], record[1:2]], cells_ref[STEPS - 1, 0])
    blank = jnp.zeros((4, slots), f32)
    out_ref[...] = jnp.concatenate([last[0], record[2:3], last[1], record[3:4], blank], axis=0)


def place_samples_kernel(width, paired, half_ref, samples_ref, far_samples_ref, target_ref, placed_ref, out_ref):
    slots = samples_ref.shape[1]
    half = half_ref[0]
    rows = up(HISTORY, 8)
    total = out_ref.shape[0] * width if paired else out_ref.shape[3]
    chunk = 256
    row = iota((8, LANES), 0)
    wide = iota((8, chunk), 0)
    blank = jnp.zeros((6, slots), f32)
    numbers = (half, 1 - half)
    lefts = []
    for samples in (samples_ref, far_samples_ref):
        columns = []
        for c in range(2):
            columns += [samples[2 * c : 2 * c + 1], blank, samples[2 * c + 1 : 2 * c + 2]]
        lefts.append(jnp.concatenate(halves(jnp.concatenate(columns, axis=0)), axis=0))
    for start in range(0, total, chunk):
        values = []
        for order in range(2):
            onehot = picked(target_ref[order, :, 0:1] == start + iota((slots, chunk), 1)).astype(bf16)
            product = jnp.dot(lefts[order], onehot, preferred_element_type=f32)
            values.append(product[:16] + product[16:])
        if paired:
            for at in range(0, chunk, LANES):
                pairs = [paired_halves(v[:8, at : at + LANES], v[8:, at : at + LANES], width) for v in values]
                for i in range(2):
                    block = (start + at) // width + i
                    out_ref[block, 0 : 2 * rows] = placed_ref[block, 0 : 2 * rows]
                    behind = jnp.zeros((8, LANES), f32)
                    for order in range(2):
                        value = pairs[order][i]
                        place = pl.ds(pl.multiple_of(numbers[order] * rows + rows - 8, 8), 8)
                        out_ref[block, place, :] = jnp.where(row == 7, value, placed_ref[block, place, :])
                        behind = jnp.where(row == numbers[order], value[0:1], behind)
                    out_ref[block, 2 * rows : 2 * rows + 8] = behind
        else:
            span = slice(start, start + chunk)
            for order in range(2):
                for c in range(2):
                    value = values[order][8 * c : 8 * c + 8]
                    old = placed_ref[numbers[order], c, :, span]
                    out_ref[numbers[order], c, 0 : rows - 8, span] = old[0 : rows - 8]
                    out_ref[numbers[order], c, rows - 8 : rows, span] = jnp.where(wide == 7, value, old[rows - 8 : rows])
                    out_ref[numbers[order], c, rows : rows + 8, span] = jnp.where(wide == 0, value, 0.0)


def filter_kernel(width, paired, across, matrix_ref, arrived_ref, out_ref, wide_ref):
    depth = wide_ref.shape[0]
    rows = depth - 8
    samples = matrix_ref.shape[0]
    groups = out_ref.shape[0] // (2 * samples)
    wide_ref[...] = jnp.zeros_like(wide_ref)
    wide_ref[0:samples, 0:samples] = matrix_ref[...]
    wide_ref[0:samples, samples : samples + 1] = matrix_ref[:, samples - 1 : samples]
    high, low = halves(wide_ref[:, 0:depth])
    left = jnp.concatenate([high, low, high], axis=1)
    row = iota((8, LANES), 0)

    def block_of(tile):
        line, column = tile // across, tile % across
        number, column = column // (across // 2), column % (across // 2)
        block = line * (across // 2) + column
        behind = jnp.where(row == number, arrived_ref[block, 2 * rows : 2 * rows + 8], 0.0)
        return jnp.concatenate([arrived_ref[block, number * rows : (number + 1) * rows], behind], axis=0)

    step = 4
    for first in range(0, groups, step):
        start = first * LANES
        if paired:
            tiles = [
                paired_halves(block_of(at // width), block_of(at // width + 1), width)
                for at in range(start, start + step * LANES, LANES)
            ]
            columns = [jnp.concatenate([t[c] for t in tiles], axis=1) for c in range(2)]
        else:
            columns = [arrived_ref[c, :, start : start + step * LANES] for c in range(2)]
        for c in range(2):
            x_high, x_low = halves(columns[c])
            right = jnp.concatenate([x_high, x_high, x_low], axis=0)
            product = jnp.dot(left, right, preferred_element_type=f32)
            for g in range(step):
                target = pl.ds(2 * (first + g) + c, samples, stride=2 * groups)
                out_ref[target, :] = product[:samples, g * LANES : (g + 1) * LANES]


def run(velocity, start_position, cells, history, leavers, owner, filter_matrix):
    tile_rows = velocity.shape[2]
    tile_cols = velocity.shape[3]
    slots = start_position.shape[1]
    within = lax.axis_size("within")
    members = lax.axis_size("ty") * within
    tile_count = 2 * members
    per_owner = 4 * slots // tile_count
    paired = 2 * per_owner == LANES
    groups = slots // LANES
    lines = 2 * HISTORY
    by_rows = history.reshape(2, HISTORY, groups, LANES).transpose(1, 2, 0, 3)
    raw = by_rows.reshape(2 * groups * HISTORY, LANES)
    past = by_rows[:, 0].reshape(lines, LANES)
    sides = find_sides(leavers)

    def joined(*parts):
        return jnp.concatenate([part.reshape(-1, LANES) for part in parts], axis=0)

    north = shifted(joined(past, velocity[:, :, tile_rows - 1]), "ty", 1)
    south = shifted(joined(past, velocity[:, :, 0]), "ty", -1)
    past = chosen(sides[0, 0:1], past, north[:lines], south[:lines])
    west = shifted(joined(past, velocity[:, :, :, tile_cols - 1], north[lines:], south[lines:]), "tx", 1)
    east = shifted(joined(past, velocity[:, :, :, 0], north[lines:], south[lines:]), "tx", -1)
    past = chosen(sides[0, 1:2], past, west[:lines], east[:lines])
    halo = (velocity, north, south, west, east)
    owner = owner.astype(f32)
    past = jnp.concatenate([past, owner.reshape(groups, LANES), jnp.zeros((2, LANES), f32)], axis=0)
    far_raw = swapped(raw)
    far_past = swapped(past)
    far_owner = far_past[2 * HISTORY : 2 * HISTORY + groups].reshape(1, slots)
    half = lax.axis_index("half").reshape(1)
    record, lead, first = run_step(0, halo, start_position, None, cells)
    lead = chosen(sides[0, 0:1], lead, shifted(lead, "ty", 1), shifted(lead, "ty", -1))
    lead_west, lead_east = shifted(lead, "tx", 1), shifted(lead, "tx", -1)
    rows = up(HISTORY, 8)
    scalar = [pl.BlockSpec(memory_space=pltpu.SMEM)]
    shape = (members, 2 * rows, LANES) if paired else (2, 2, rows, members * per_owner)
    placed, target = pl.pallas_call(
        functools.partial(place_history_kernel, per_owner, paired, within),
        out_shape=[jax.ShapeDtypeStruct(shape, f32), jax.ShapeDtypeStruct((2, slots, LANES), jnp.int32)],
        in_specs=scalar + whole(6),
        out_specs=whole(2),
        cost_estimate=cost(2 * 4 * rows * slots * 4 * slots, 3000000),
        compiler_params=grant,
        name="place_history",
    )(half, owner.reshape(1, slots), raw, past, far_owner, far_raw, far_past)
    samples = pl.pallas_call(
        functools.partial(last_samples_kernel, (float(tile_rows), float(tile_cols))),
        out_shape=jax.ShapeDtypeStruct((8, slots), f32),
        in_specs=whole(7),
        out_specs=whole(1)[0],
        cost_estimate=cost(1000000, 100000),
        compiler_params=grant,
        name="last_samples",
    )(record, lead, lead_west, lead_east, sides, first, cells)
    far_samples = swapped(samples)
    shape = (members, 2 * rows + 8, LANES) if paired else (2, 2, rows + 8, members * per_owner)
    outgoing = pl.pallas_call(
        functools.partial(place_samples_kernel, per_owner, paired),
        out_shape=jax.ShapeDtypeStruct(shape, f32),
        in_specs=scalar + whole(4),
        out_specs=whole(1)[0],
        cost_estimate=cost(2 * 2 * 16 * slots * 4 * slots, 3000000),
        compiler_params=grant,
        name="place_samples",
    )(half, samples, far_samples, target, placed)
    if not paired:
        outgoing = outgoing.reshape(2, 2, rows + 8, members, per_owner).transpose(3, 2, 0, 1, 4)
    arrived = lax.all_to_all(outgoing, ("ty", "within"), split_axis=0, concat_axis=0, tiled=True)
    if not paired:
        arrived = arrived.reshape(-1, within, rows + 8, 2, 2, per_owner).transpose(4, 2, 0, 3, 1, 5)
        arrived = arrived.reshape(2, rows + 8, tile_count * per_owner)
    filtered = pl.pallas_call(
        functools.partial(filter_kernel, per_owner, paired, 2 * within),
        out_shape=jax.ShapeDtypeStruct((SAMPLES * 4 * groups * 2, LANES), f32),
        in_specs=whole(2),
        out_specs=whole(1)[0],
        scratch_shapes=[pltpu.VMEM((rows + 8, LANES), f32)],
        cost_estimate=cost(2 * 3 * 80 * 80 * 8 * slots, 3000000),
        compiler_params=grant,
        name="filter_series",
    )(filter_matrix, arrived)
    filtered = filtered.reshape(SAMPLES, 4 * groups, 2, LANES)
    return filtered.transpose(2, 0, 1, 3).reshape(2, SAMPLES, 4 * slots)


def solution(mesh):
    lines, across = mesh.devices.shape
    halved = Mesh(mesh.devices.reshape(lines, 2, across // 2), ("ty", "half", "within"))
    tile = ("ty", "half", "within")
    placed = (
        P(None, None, "ty", ("half", "within")),
        P(None, tile),
        P(None, None, None, tile),
        P(None, None, tile),
        P(),
        P(tile, None),
        P(),
    )
    return jax.shard_map(
        run,
        mesh=halved,
        in_specs=placed,
        out_specs=P(None, None, tile),
        check_vma=False,
    )
```

time: 71.2 us -> 66.3 us (0.931)
  blocking collectives: 34.8 us -> 20.5 us
  starting transfers between devices: 14 us -> 19.5 us
  waiting for transfers between devices: 12.2 us -> 14.2 us
  Pallas kernels: 7.3 us -> 8.36 us
    all_to_all x1, blocking collectives: 34.8 us -> 20.5 us  [run(): lax.all_to_all(outgoing, ('ty', 'within'), split_axis=0, concat_axis=0, t...]
    ppermute x12 -> x11, starting transfers between devices: 14 us -> 19.5 us  [the longest x3 10.3 us: swapped(): return lax.ppermute(value, 'half', [(0, 1), (1, 0)])]
    ppermute x12 -> x11, waiting for transfers between devices: 12.2 us -> 14.2 us  [the longest x8 11.9 us: shifted(): lax.ppermute(value, places[axis], [(i, (i + by) % peers) for i in range(p...]
    pallas_call x3 -> x4, Pallas kernels: 4.18 us -> 5.25 us  [the longest x1 2.23 us: run(): pl.pallas_call(functools.partial(filter_kernel, per_owner, paired, 2 * wi...]
  transfers between devices with their start and end apart: 12 -> 11, of which waited for: 7 -> 5; matrix products, arithmetic and copies ran while one was open for 2% -> 1% of each run, Pallas kernels for 6% -> 7%
where the time goes in v3:
time: 66.3 us; the launch traced here: 66.1 us
  blocking collectives  20.5 us (31%)
  starting transfers between devices  19.5 us (29%)
  waiting for transfers between devices  14.2 us (21%)
  Pallas kernels  8.36 us (13%)
  local copies, waits for them, and re-layouts  3.19 us (5%)
    all_to_all x1, blocking collectives, run(): lax.all_to_all(outgoing, ('ty', 'within'), split_axis=0, concat_axis=0, t...  20.5 us
    ppermute x8, waiting for transfers between devices, shifted(): lax.ppermute(value, places[axis], [(i, (i + by) % peers) for i in range(p...  11.9 us
    ppermute x3, starting transfers between devices, swapped(): return lax.ppermute(value, 'half', [(0, 1), (1, 0)])  10.3 us
    ppermute x8, starting transfers between devices, shifted(): lax.ppermute(value, places[axis], [(i, (i + by) % peers) for i in range(p...  9.22 us
    pallas_call x1, Pallas kernels, run_step(): pl.pallas_call(functools.partial(step_kernel, step, following), out_shape...  2.55 us
    ppermute x3, waiting for transfers between devices, swapped(): return lax.ppermute(value, 'half', [(0, 1), (1, 0)])  2.31 us
    pallas_call x1, Pallas kernels, run(): pl.pallas_call(functools.partial(filter_kernel, per_owner, paired, 2 * wi...  2.23 us
    pallas_call x1, Pallas kernels, run(): pl.pallas_call(functools.partial(place_history_kernel, per_owner, paired,...  1.7 us
  transfers between devices with their start and end apart: 11, of which 5 were waited for; matrix products, arithmetic and copies ran while one was open for 1% of the time, Pallas kernels for 7%

profile of v3, /device:TPU:0, one launch (start us, length us, event | category | flops | bytes accessed | tf_op | source)
XLA Modules:
  0.0 66.1 jit_solution(13042864884665307684)
XLA Ops:
  0.0 0.8 %slice_reduce_fusion.2 = (f32[2,3,128]{2,1,0:T(4,128)S(1)}, f32[2,3,128]{2,1,0:T(4,128)S(1)}) fusion(f32[2,3,128,128]{3,2,1,0:T(8,128)} %velocity_ref.1), kind=kLoop, calls=%fused_computation.15 | loop fusion | bytes 12288 | tf_op jit(solution)/shard_map/slice | solution.py:408
  0.9 0.0 copy-start.6
  0.9 0.0 copy-start.3
  0.9 0.0 copy-start.5
  0.9 1.1 %bitcast_bitcast_fusion = f32[71,4,2,128]{3,2,0,1:T(2,128)S(1)} fusion(f32[2,71,512]{2,0,1:T(2,128)} %param.10), kind=kLoop, calls=%fused_computation.2 | loop fusion | bytes 581632 | tf_op jit(solution)/shard_map/transpose | solution.py:399
  2.0 0.1 reshape_squeeze.15
  2.1 2.5 %collective-permute-start.1 = (f32[148,128]{1,0:T(8,128)S(1)}, f32[148,128]{1,0:T(8,128)S(1)}, u32[]{:S(2)}, u32[]{:S(2)}) collective-permute-start(f32[148,128]{1,0:T(8,128)S(1)} %get-tuple-element.21), channel_id=1, source_target_pairs={{0,24},{8,0},{16,8},{24,16},{1,25},{9,1},{17,9},{25,17},{2,26},{10... | collective-permute-start | bytes 227336 | tf_op jit(solution)/shard_map/ppermute | solution.py:34
  4.5 2.6 %collective-permute-start.10 = (f32[568,128]{1,0:T(8,128)}, f32[568,128]{1,0:T(8,128)S(1)}, u32[]{:S(2)}, u32[]{:S(2)}) collective-permute-start(f32[568,128]{1,0:T(8,128)} %bitcast.32), channel_id=1, source_target_pairs={{0,4},{4,0},{1,5},{5,1},{2,6},{6,2},{3,7},{7,3},{8,12},{12,8},{9,1... | collective-permute-start | bytes 872456 | tf_op jit(solution)/shard_map/ppermute | solution.py:38
  7.1 0.7 copy-done.4
  7.8 0.6 find_sides.1.sides_ref
  8.4 0.4 slice_reduce_fusion
  8.8 0.0 collective-permute-done.1.south_ref
  8.9 4.1 %collective-permute-start.3 = (f32[160,128]{1,0:T(8,128)S(1)}, f32[160,128]{1,0:T(8,128)S(1)}, u32[]{:S(2)}, u32[]{:S(2)}) collective-permute-start(f32[160,128]{1,0:T(8,128)S(1)} %get-tuple-element.19), channel_id=1, source_target_pairs={{0,7},{1,0},{2,1},{3,2},{4,3},{5,4},{6,5},{7,6},{8,15},{9,8},{10,9... | collective-permute-start | bytes 245768 | tf_op jit(solution)/shard_map/ppermute | solution.py:34
  13.0 0.1 pad.2.clone
  13.1 3.1 %collective-permute-done.3.east_ref = f32[160,128]{1,0:T(8,128)S(1)} collective-permute-done((f32[160,128]{1,0:T(8,128)S(1)}, f32[160,128]{1,0:T(8,128)S(1)}, u32[]{:S(2)}, u32[]{:S(2)}) %collective-permute-start.3) | collective-permute-done | bytes 81952 | tf_op jit(solution)/shard_map/ppermute | solution.py:34
  16.2 4.0 %collective-permute-done.2.west_ref = f32[160,128]{1,0:T(8,128)S(1)} collective-permute-done((f32[160,128]{1,0:T(8,128)S(1)}, f32[160,128]{1,0:T(8,128)S(1)}, u32[]{:S(2)}, u32[]{:S(2)}) %collective-permute-start.2) | collective-permute-done | bytes 81952 | tf_op jit(solution)/shard_map/ppermute | solution.py:34
  20.3 2.6 %sample_step.1 = (f32[8,512]{1,0:T(8,128)S(1)}, f32[8,128]{1,0:T(8,128)S(1)}, f32[8,512]{1,0:T(8,128)S(1)}) custom-call(f32[2,3,128,128]{3,2,1,0:T(8,128)S(1)} %copy-done, f32[148,128]{1,0:T(8,128)S(1)} %collective-permute-done.north_ref, f32[148,128]{1,0:T(8,128)S(1)} %collective-permute-done.1.south_ref, f32[160,128]{1,0:T(8,128)S(1)} %collective-permute-done.2.west_ref, ...), custom_call_target="tpu_custom_call" | custom-call | flops 1509949440 | bytes 600000 | tf_op jit(solution)/shard_map/sample_step/pallas_call | solution.py:191
  22.8 0.1 collective-permute-start.5
  22.9 0.5 collective-permute-start.4
  23.4 0.1 maximum_maximum_fusion.past_ref
  23.5 7.1 %collective-permute-start.9 = (f32[148,128]{1,0:T(8,128)S(1)}, f32[148,128]{1,0:T(8,128)S(1)}, u32[]{:S(2)}, u32[]{:S(2)}) collective-permute-start(f32[148,128]{1,0:T(8,128)S(1)} %maximum_maximum_fusion.past_ref), channel_id=1, source_target_pairs={{0,4},{4,0},{1,5},{5,1},{2,6},{6,2},{3,7},{7,3},{8,12},{12,8},{9,1... | collective-permute-start | bytes 227336 | tf_op jit(solution)/shard_map/ppermute | solution.py:38
  30.6 0.5 collective-permute-start.7
  31.1 1.6 %collective-permute-start.6 = (f32[8,128]{1,0:T(8,128)S(1)}, f32[8,128]{1,0:T(8,128)S(1)}, u32[]{:S(2)}, u32[]{:S(2)}) collective-permute-start(f32[8,128]{1,0:T(8,128)S(1)} %select_select_fusion.lead_ref), channel_id=1, source_target_pairs={{0,1},{1,2},{2,3},{3,4},{4,5},{5,6},{6,7},{7,0},{8,9},{9,10},{10,1... | collective-permute-start | bytes 12296 | tf_op jit(solution)/shard_map/ppermute | solution.py:34
  32.6 1.6 %collective-permute-done.7.east_ref = f32[8,128]{1,0:T(8,128)S(1)} collective-permute-done((f32[8,128]{1,0:T(8,128)S(1)}, f32[8,128]{1,0:T(8,128)S(1)}, u32[]{:S(2)}, u32[]{:S(2)}) %collective-permute-start.7) | collective-permute-done | bytes 4128 | tf_op jit(solution)/shard_map/ppermute | solution.py:34
  34.2 3.1 %collective-permute-done.6.west_ref = f32[8,128]{1,0:T(8,128)S(1)} collective-permute-done((f32[8,128]{1,0:T(8,128)S(1)}, f32[8,128]{1,0:T(8,128)S(1)}, u32[]{:S(2)}, u32[]{:S(2)}) %collective-permute-start.6) | collective-permute-done | bytes 4128 | tf_op jit(solution)/shard_map/ppermute | solution.py:34
  37.4 0.7 %collective-permute-start.8 = (f32[8,512]{1,0:T(8,128)S(1)}, f32[8,512]{1,0:T(8,128)S(1)}, u32[]{:S(2)}, u32[]{:S(2)}) collective-permute-start(f32[8,512]{1,0:T(8,128)S(1)} %last_samples.1.samples_ref), channel_id=1, source_target_pairs={{0,4},{4,0},{1,5},{5,1},{2,6},{6,2},{3,7},{7,3},{8,12},{12,8},{9,1... | collective-permute-start | bytes 49160 | tf_op jit(solution)/shard_map/ppermute | solution.py:38
  38.1 1.7 %place_history.1 = (f32[16,144,128]{2,1,0:T(8,128)S(1)}, s32[2,512,128]{2,1,0:T(8,128)S(1)}) custom-call(s32[1]{0:T(128)} %bitcast.half_ref, f32[1,512]{1,0:T(1,128)S(1)} %get-tuple-element.28.owner_ref, f32[568,128]{1,0:T(8,128)S(1)} %bitcast.33, f32[148,128]{1,0:T(8,128)S(1)} %maximum_maximum_fusion.past_ref, f32[1,512]{1,0:T(1,128)S(1)} %bitcast.34, ...), custom_call_target="tpu_custom_call" | custom-call | flops 603979776 | bytes 3000000 | tf_op jit(solution)/shard_map/place_history/pallas_call | solution.py:426
  39.8 2.3 %collective-permute-done.8.far_samples_ref = f32[8,512]{1,0:T(8,128)S(1)} collective-permute-done((f32[8,512]{1,0:T(8,128)S(1)}, f32[8,512]{1,0:T(8,128)S(1)}, u32[]{:S(2)}, u32[]{:S(2)}) %collective-permute-start.8) | collective-permute-done | bytes 16416 | tf_op jit(solution)/shard_map/ppermute | solution.py:38
  42.1 1.3 %place_samples.1 = f32[16,152,128]{2,1,0:T(8,128)S(1)} custom-call(s32[1]{0:T(128)} %bitcast.half_ref, f32[8,512]{1,0:T(8,128)S(1)} %last_samples.1.samples_ref, f32[8,512]{1,0:T(8,128)S(1)} %collective-permute-done.8.far_samples_ref, s32[2,512,128]{2,1,0:T(8,128)S(1)} %get-tuple-element.13.target_ref, f32[16,144,128]{2,1,0:T(8,128)S(1)} %get-tuple-element.14.placed_ref), custom_call_target="tpu_custom_call" | custom-call | flops 67108864 | bytes 3000000 | tf_op jit(solution)/shard_map/place_samples/pallas_call | solution.py:446
  43.4 0.0 copy-start.2
  43.4 20.5 %all_to_all.5.arrived_ref = f32[16,152,128]{2,1,0:T(8,128)S(1)} all-to-all(f32[16,152,128]{2,1,0:T(8,128)S(1)} %place_samples.1), channel_id=1, replica_groups=mesh['ty'=4,'half'=2,'within'=4] {'ty','within'}, dimensions={0} | all-to-all | bytes 2490368 | tf_op jit(solution)/shard_map/all_to_all | solution.py:457
  63.9 2.2 %filter_series.1 = f32[2336,128]{1,0:T(8,128)} custom-call(f32[73,73]{1,0:T(8,128)S(1)} %copy-done.2, f32[16,152,128]{2,1,0:T(8,128)S(1)} %all_to_all.5.arrived_ref), custom_call_target="tpu_custom_call" | custom-call | flops 157286400 | bytes 3000000 | tf_op jit(solution)/shard_map/filter_series/pallas_call | solution.py:461
  (33 shorter events, 0.2 us)
Async XLA Ops:
  0.0 8.4 %copy-start = (f32[2,3,128,128]{3,2,1,0:T(8,128)S(1)}, f32[2,3,128,128]{3,2,1,0:T(8,128)}, u32[]{:S(2)}) copy-start(f32[2,3,128,128]{3,2,1,0:T(8,128)} %velocity_ref.1) | copy-start | bytes 1179652
  0.9 12.2 %copy-start.6 = (s32[512,1]{0,1:T(1,128)S(1)}, s32[512,1]{0,1:T(1,128)}, u32[]{:S(2)}) copy-start(s32[512,1]{0,1:T(1,128)} %param.12) | copy-start | bytes 6148
  0.9 19.4 %copy-start.3 = (s32[2,4,2,512]{3,2,1,0:T(2,128)S(1)}, s32[2,4,2,512]{3,2,1,0:T(2,128)}, u32[]{:S(2)}) copy-start(s32[2,4,2,512]{3,2,1,0:T(2,128)} %cells_ref.3) | copy-start | bytes 98308
  0.9 19.4 %copy-start.5 = (f32[2,512]{1,0:T(2,128)S(1)}, f32[2,512]{1,0:T(2,128)}, u32[]{:S(2)}) copy-start(f32[2,512]{1,0:T(2,128)} %point_ref.1) | copy-start | bytes 12292
  2.1 6.7 %collective-permute-start.1 = (f32[148,128]{1,0:T(8,128)S(1)}, f32[148,128]{1,0:T(8,128)S(1)}, u32[]{:S(2)}, u32[]{:S(2)}) collective-permute-start(f32[148,128]{1,0:T(8,128)S(1)} %get-tuple-element.21), channel_id=1, source_target_pairs={{0,24},{8,0},{16,8},{24,16},{1,25},{9,1},{17,9},{25,17},{2,26},{10... | collective-permute-start | bytes 227336 | tf_op jit(solution)/shard_map/ppermute | solution.py:34
  4.5 4.3 %collective-permute-start = (f32[148,128]{1,0:T(8,128)S(1)}, f32[148,128]{1,0:T(8,128)S(1)}, u32[]{:S(2)}, u32[]{:S(2)}) collective-permute-start(f32[148,128]{1,0:T(8,128)S(1)} %get-tuple-element.22), channel_id=1, source_target_pairs={{0,8},{8,16},{16,24},{24,0},{1,9},{9,17},{17,25},{25,1},{2,10},{10... | collective-permute-start | bytes 227336 | tf_op jit(solution)/shard_map/ppermute | solution.py:34
  4.5 33.6 %collective-permute-start.10 = (f32[568,128]{1,0:T(8,128)}, f32[568,128]{1,0:T(8,128)S(1)}, u32[]{:S(2)}, u32[]{:S(2)}) collective-permute-start(f32[568,128]{1,0:T(8,128)} %bitcast.32), channel_id=1, source_target_pairs={{0,4},{4,0},{1,5},{5,1},{2,6},{6,2},{3,7},{7,3},{8,12},{12,8},{9,1... | collective-permute-start | bytes 872456 | tf_op jit(solution)/shard_map/ppermute | solution.py:38
  7.1 0.7 copy-start.4
  8.9 7.3 %collective-permute-start.3 = (f32[160,128]{1,0:T(8,128)S(1)}, f32[160,128]{1,0:T(8,128)S(1)}, u32[]{:S(2)}, u32[]{:S(2)}) collective-permute-start(f32[160,128]{1,0:T(8,128)S(1)} %get-tuple-element.19), channel_id=1, source_target_pairs={{0,7},{1,0},{2,1},{3,2},{4,3},{5,4},{6,5},{7,6},{8,15},{9,8},{10,9... | collective-permute-start | bytes 245768 | tf_op jit(solution)/shard_map/ppermute | solution.py:34
  13.0 7.2 %collective-permute-start.2 = (f32[160,128]{1,0:T(8,128)S(1)}, f32[160,128]{1,0:T(8,128)S(1)}, u32[]{:S(2)}, u32[]{:S(2)}) collective-permute-start(f32[160,128]{1,0:T(8,128)S(1)} %get-tuple-element.20), channel_id=1, source_target_pairs={{0,1},{1,2},{2,3},{3,4},{4,5},{5,6},{6,7},{7,0},{8,9},{9,10},{10,1... | collective-permute-start | bytes 245768 | tf_op jit(solution)/shard_map/ppermute | solution.py:34
  13.1 25.0 %copy-start.1 = (f32[2,71,512]{2,0,1:T(2,128)S(1)}, f32[2,71,512]{2,0,1:T(2,128)}, u32[]{:S(2)}) copy-start(f32[2,71,512]{2,0,1:T(2,128)} %param.10) | copy-start | bytes 872452
  22.8 7.7 %collective-permute-start.5 = (f32[8,128]{1,0:T(8,128)S(1)}, f32[8,128]{1,0:T(8,128)S(1)}, u32[]{:S(2)}, u32[]{:S(2)}) collective-permute-start(f32[8,128]{1,0:T(8,128)S(1)} %get-tuple-element.11), channel_id=1, source_target_pairs={{0,24},{8,0},{16,8},{24,16},{1,25},{9,1},{17,9},{25,17},{2,26},{10... | collective-permute-start | bytes 12296 | tf_op jit(solution)/shard_map/ppermute | solution.py:34
  22.9 7.7 %collective-permute-start.4 = (f32[8,128]{1,0:T(8,128)S(1)}, f32[8,128]{1,0:T(8,128)S(1)}, u32[]{:S(2)}, u32[]{:S(2)}) collective-permute-start(f32[8,128]{1,0:T(8,128)S(1)} %get-tuple-element.11), channel_id=1, source_target_pairs={{0,8},{8,16},{16,24},{24,0},{1,9},{9,17},{17,25},{25,1},{2,10},{10... | collective-permute-start | bytes 12296 | tf_op jit(solution)/shard_map/ppermute | solution.py:34
  23.5 14.6 %collective-permute-start.9 = (f32[148,128]{1,0:T(8,128)S(1)}, f32[148,128]{1,0:T(8,128)S(1)}, u32[]{:S(2)}, u32[]{:S(2)}) collective-permute-start(f32[148,128]{1,0:T(8,128)S(1)} %maximum_maximum_fusion.past_ref), channel_id=1, source_target_pairs={{0,4},{4,0},{1,5},{5,1},{2,6},{6,2},{3,7},{7,3},{8,12},{12,8},{9,1... | collective-permute-start | bytes 227336 | tf_op jit(solution)/shard_map/ppermute | solution.py:38
  30.6 3.7 %collective-permute-start.7 = (f32[8,128]{1,0:T(8,128)S(1)}, f32[8,128]{1,0:T(8,128)S(1)}, u32[]{:S(2)}, u32[]{:S(2)}) collective-permute-start(f32[8,128]{1,0:T(8,128)S(1)} %select_select_fusion.lead_ref), channel_id=1, source_target_pairs={{0,7},{1,0},{2,1},{3,2},{4,3},{5,4},{6,5},{7,6},{8,15},{9,8},{10,9... | collective-permute-start | bytes 12296 | tf_op jit(solution)/shard_map/ppermute | solution.py:34
  31.1 6.3 %collective-permute-start.6 = (f32[8,128]{1,0:T(8,128)S(1)}, f32[8,128]{1,0:T(8,128)S(1)}, u32[]{:S(2)}, u32[]{:S(2)}) collective-permute-start(f32[8,128]{1,0:T(8,128)S(1)} %select_select_fusion.lead_ref), channel_id=1, source_target_pairs={{0,1},{1,2},{2,3},{3,4},{4,5},{5,6},{6,7},{7,0},{8,9},{9,10},{10,1... | collective-permute-start | bytes 12296 | tf_op jit(solution)/shard_map/ppermute | solution.py:34
  37.4 4.7 %collective-permute-start.8 = (f32[8,512]{1,0:T(8,128)S(1)}, f32[8,512]{1,0:T(8,128)S(1)}, u32[]{:S(2)}, u32[]{:S(2)}) collective-permute-start(f32[8,512]{1,0:T(8,128)S(1)} %last_samples.1.samples_ref), channel_id=1, source_target_pairs={{0,4},{4,0},{1,5},{5,1},{2,6},{6,2},{3,7},{7,3},{8,12},{12,8},{9,1... | collective-permute-start | bytes 49160 | tf_op jit(solution)/shard_map/ppermute | solution.py:38
  43.4 20.5 %copy-start.2 = (f32[73,73]{1,0:T(8,128)S(1)}, f32[73,73]{1,0:T(8,128)}, u32[]{:S(2)}) copy-start(f32[73,73]{1,0:T(8,128)} %matrix_ref.1) | copy-start | bytes 63952

commit v4 on v3

--- a/solution.py
+++ b/solution.py
@@ -251,43 +251,37 @@
     return (base + rank).astype(jnp.int32)
 
 
-def place_history_kernel(
-    width, paired, within, half_ref, owner_ref, history_ref, past_ref, far_owner_ref, far_history_ref, far_past_ref, out_ref, target_ref
-):
+def place_history_kernel(width, paired, within, skipped, half_ref, owner_ref, history_ref, past_ref, out_ref, onehot_ref):
     slots = owner_ref.shape[1]
-    half = half_ref[0]
     rows = up(HISTORY, 8)
     groups = slots // LANES
     moving = 8 * MOST // LANES
-    total = out_ref.shape[0] * width if paired else out_ref.shape[3]
-    tiles = ((half, owner_ref, history_ref, past_ref), (1 - half, far_owner_ref, far_history_ref, far_past_ref))
-    for order, (number, owners, raw, past) in enumerate(tiles):
-        target = targets_of(owners[...], half, within, width)
-        target_ref[order] = jnp.broadcast_to(target, (slots, LANES))
-        parts = []
-        for c in range(2):
-            pieces = [past[pl.ds(c, HISTORY, stride=2), :]]
-            pieces += [raw[pl.ds(2 * g + c, HISTORY, stride=2 * groups), :] for g in range(moving, groups)]
-            parts += [jnp.concatenate(pieces, axis=1), jnp.zeros((rows - HISTORY, slots), f32)]
-        joined = jnp.concatenate(halves(jnp.concatenate(parts, axis=0)), axis=0)
-        chunk = 256
-        base = pl.multiple_of(number * rows, 8)
-        for start in range(0, total, chunk):
-            onehot = picked(target == start + iota((slots, chunk), 1)).astype(bf16)
-            product = jnp.dot(joined, onehot, preferred_element_type=f32)
-            placed = product[: 2 * rows] + product[2 * rows :]
-            if paired:
-                for at in range(0, chunk, LANES):
-                    pair = paired_halves(placed[:rows, at : at + LANES], placed[rows:, at : at + LANES], width)
-                    for i in range(2):
-                        out_ref[(start + at) // width + i, pl.ds(base, rows), :] = pair[i]
-            else:
-                out_ref[number, 0, :, start : start + chunk] = placed[:rows]
-                out_ref[number, 1, :, start : start + chunk] = placed[rows:]
+    total = onehot_ref.shape[1]
+    target = targets_of(owner_ref[...], half_ref[0], within, width)
+    parts = []
+    for c in range(2):
+        pieces = [past_ref[pl.ds(c, HISTORY, stride=2), :]]
+        for g in range(moving, groups):
+            pieces.append(history_ref[pl.ds(2 * (g - skipped) + c, HISTORY, stride=2 * (groups - skipped)), :])
+        parts += [jnp.concatenate(pieces, axis=1), jnp.zeros((rows - HISTORY, slots), f32)]
+    joined = jnp.concatenate(halves(jnp.concatenate(parts, axis=0)), axis=0)
+    chunk = 256
+    for start in range(0, total, chunk):
+        onehot = picked(target == start + iota((slots, chunk), 1)).astype(bf16)
+        onehot_ref[:, start : start + chunk] = onehot
+        product = jnp.dot(joined, onehot, preferred_element_type=f32)
+        placed = product[: 2 * rows] + product[2 * rows :]
+        if paired:
+            for at in range(0, chunk, LANES):
+                pair = paired_halves(placed[:rows, at : at + LANES], placed[rows:, at : at + LANES], width)
+                for i in range(2):
+                    out_ref[(start + at) // width + i] = pair[i]
+        else:
+            out_ref[0, :, start : start + chunk] = placed[:rows]
+            out_ref[1, :, start : start + chunk] = placed[rows:]
 
 
 def last_samples_kernel(tile, record_ref, lead_ref, west_ref, east_ref, sides_ref, next_ref, cells_ref, out_ref):
-    slots = record_ref.shape[1]
     moved = lead_ref.shape[1]
     sides = sides_ref[0]
     lead = chosen(sides[1:2], lead_ref[...], west_ref[...], east_ref[...])
@@ -296,93 +290,95 @@
     record = jnp.concatenate([lead - lowered, record_ref[:, moved:]], axis=1)
     corners = [[next_ref[2 * i + c : 2 * i + c + 1] for c in range(2)] for i in range(4)]
     last = bilinear(corners, [record[0:1], record[1:2]], cells_ref[STEPS - 1, 0])
-    blank = jnp.zeros((4, slots), f32)
-    out_ref[...] = jnp.concatenate([last[0], record[2:3], last[1], record[3:4], blank], axis=0)
-
-
-def place_samples_kernel(width, paired, half_ref, samples_ref, far_samples_ref, target_ref, placed_ref, out_ref):
-    slots = samples_ref.shape[1]
+    out_ref[...] = jnp.concatenate([record[2:3], last[0], record[3:4], last[1]], axis=0)
+
+
+def place_samples_kernel(
+    width, paired, half_ref, samples_ref, far_samples_ref, onehot_ref, far_onehot_ref, placed_ref, far_placed_ref, out_ref
+):
     half = half_ref[0]
     rows = up(HISTORY, 8)
-    total = out_ref.shape[0] * width if paired else out_ref.shape[3]
+    total = onehot_ref.shape[1]
     chunk = 256
     row = iota((8, LANES), 0)
     wide = iota((8, chunk), 0)
-    blank = jnp.zeros((6, slots), f32)
-    numbers = (half, 1 - half)
+    tiles = (
+        (half, samples_ref, onehot_ref, placed_ref),
+        (1 - half, far_samples_ref, far_onehot_ref, far_placed_ref),
+    )
     lefts = []
-    for samples in (samples_ref, far_samples_ref):
+    for number, samples, _, _ in tiles:
         columns = []
         for c in range(2):
-            columns += [samples[2 * c : 2 * c + 1], blank, samples[2 * c + 1 : 2 * c + 2]]
+            early, late = samples[2 * c : 2 * c + 1], samples[2 * c + 1 : 2 * c + 2]
+            at = iota((8, early.shape[1]), 0)
+            columns.append(jnp.where(at == number, early, jnp.where(at == number + 2, late, 0.0)))
         lefts.append(jnp.concatenate(halves(jnp.concatenate(columns, axis=0)), axis=0))
     for start in range(0, total, chunk):
-        values = []
-        for order in range(2):
-            onehot = picked(target_ref[order, :, 0:1] == start + iota((slots, chunk), 1)).astype(bf16)
-            product = jnp.dot(lefts[order], onehot, preferred_element_type=f32)
-            values.append(product[:16] + product[16:])
+        span = slice(start, start + chunk)
+        values = None
+        for left, (_, _, onehot, _) in zip(lefts, tiles):
+            product = jnp.dot(left, onehot[:, span], preferred_element_type=f32)
+            value = product[:16] + product[16:]
+            values = value if values is None else values + value
         if paired:
             for at in range(0, chunk, LANES):
-                pairs = [paired_halves(v[:8, at : at + LANES], v[8:, at : at + LANES], width) for v in values]
+                pair = paired_halves(values[:8, at : at + LANES], values[8:, at : at + LANES], width)
                 for i in range(2):
                     block = (start + at) // width + i
-                    out_ref[block, 0 : 2 * rows] = placed_ref[block, 0 : 2 * rows]
-                    behind = jnp.zeros((8, LANES), f32)
-                    for order in range(2):
-                        value = pairs[order][i]
-                        place = pl.ds(pl.multiple_of(numbers[order] * rows + rows - 8, 8), 8)
-                        out_ref[block, place, :] = jnp.where(row == 7, value, placed_ref[block, place, :])
-                        behind = jnp.where(row == numbers[order], value[0:1], behind)
-                    out_ref[block, 2 * rows : 2 * rows + 8] = behind
+                    for number, _, _, placed in tiles:
+                        out_ref[block, pl.ds(pl.multiple_of(number * rows, 8), rows), :] = placed[block]
+                    out_ref[block, 2 * rows : 2 * rows + 8] = pair[i]
         else:
-            span = slice(start, start + chunk)
-            for order in range(2):
-                for c in range(2):
-                    value = values[order][8 * c : 8 * c + 8]
-                    old = placed_ref[numbers[order], c, :, span]
-                    out_ref[numbers[order], c, 0 : rows - 8, span] = old[0 : rows - 8]
-                    out_ref[numbers[order], c, rows - 8 : rows, span] = jnp.where(wide == 7, value, old[rows - 8 : rows])
-                    out_ref[numbers[order], c, rows : rows + 8, span] = jnp.where(wide == 0, value, 0.0)
-
-
-def filter_kernel(width, paired, across, matrix_ref, arrived_ref, out_ref, wide_ref):
+            for c in range(2):
+                for number, _, _, placed in tiles:
+                    out_ref[c, pl.ds(pl.multiple_of(number * rows, 8), rows), span] = placed[c, :, span]
+                out_ref[c, 2 * rows : 2 * rows + 8, span] = values[8 * c : 8 * c + 8]
+
+
+def filter_kernel(width, paired, across, matrix_ref, arrived_ref, out_ref, wide_ref, ready_ref, sems):
     depth = wide_ref.shape[0]
     rows = depth - 8
     samples = matrix_ref.shape[0]
-    groups = out_ref.shape[0] // (2 * samples)
+    groups = out_ref.shape[2] // 2
+    row = iota((8, LANES), 0)
     wide_ref[...] = jnp.zeros_like(wide_ref)
-    wide_ref[0:samples, 0:samples] = matrix_ref[...]
-    wide_ref[0:samples, samples : samples + 1] = matrix_ref[:, samples - 1 : samples]
+    wide_ref[0:samples, 0:HISTORY] = matrix_ref[:, 0:HISTORY]
+    for late in range(STEPS):
+        for number in range(2):
+            at = rows + 2 * late + number
+            wide_ref[0:samples, at : at + 1] = matrix_ref[:, HISTORY + late : HISTORY + late + 1]
     high, low = halves(wide_ref[:, 0:depth])
     left = jnp.concatenate([high, low, high], axis=1)
-    row = iota((8, LANES), 0)
 
     def block_of(tile):
         line, column = tile // across, tile % across
         number, column = column // (across // 2), column % (across // 2)
         block = line * (across // 2) + column
-        behind = jnp.where(row == number, arrived_ref[block, 2 * rows : 2 * rows + 8], 0.0)
+        behind = jnp.where((row == number) | (row == number + 2), arrived_ref[block, 2 * rows : 2 * rows + 8], 0.0)
         return jnp.concatenate([arrived_ref[block, number * rows : (number + 1) * rows], behind], axis=0)
 
-    step = 4
-    for first in range(0, groups, step):
-        start = first * LANES
+    copies = []
+    for run in range(out_ref.shape[1]):
+        start = run * groups * LANES
         if paired:
-            tiles = [
-                paired_halves(block_of(at // width), block_of(at // width + 1), width)
-                for at in range(start, start + step * LANES, LANES)
-            ]
+            spots = range(start // width, (start + groups * LANES) // width, 2)
+            tiles = [paired_halves(block_of(at), block_of(at + 1), width) for at in spots]
             columns = [jnp.concatenate([t[c] for t in tiles], axis=1) for c in range(2)]
         else:
-            columns = [arrived_ref[c, :, start : start + step * LANES] for c in range(2)]
+            columns = [arrived_ref[c, :, start : start + groups * LANES] for c in range(2)]
         for c in range(2):
             x_high, x_low = halves(columns[c])
             right = jnp.concatenate([x_high, x_high, x_low], axis=0)
             product = jnp.dot(left, right, preferred_element_type=f32)
-            for g in range(step):
-                target = pl.ds(2 * (first + g) + c, samples, stride=2 * groups)
-                out_ref[target, :] = product[:samples, g * LANES : (g + 1) * LANES]
+            for g in range(groups):
+                target = pl.ds(2 * g + c, samples, stride=2 * groups)
+                ready_ref[run, target, :] = product[:samples, g * LANES : (g + 1) * LANES]
+        source = ready_ref.at[run].reshape(samples, 2 * groups, LANES)
+        copies.append(pltpu.make_async_copy(source, out_ref.at[:, run], sems.at[run]))
+        copies[-1].start()
+    for copy in copies:
+        copy.wait()
 
 
 def run(velocity, start_position, cells, history, leavers, owner, filter_matrix):
@@ -412,29 +408,36 @@
     past = chosen(sides[0, 1:2], past, west[:lines], east[:lines])
     halo = (velocity, north, south, west, east)
     owner = owner.astype(f32)
-    past = jnp.concatenate([past, owner.reshape(groups, LANES), jnp.zeros((2, LANES), f32)], axis=0)
-    far_raw = swapped(raw)
+    past = joined(past, owner, jnp.zeros((2, LANES), f32))
+    moving = 8 * MOST // LANES
+    far_raw = swapped(by_rows[:, moving:].reshape(2 * (groups - moving) * HISTORY, LANES))
     far_past = swapped(past)
-    far_owner = far_past[2 * HISTORY : 2 * HISTORY + groups].reshape(1, slots)
+    far_owner = far_past[lines : lines + groups].reshape(1, slots)
     half = lax.axis_index("half").reshape(1)
     record, lead, first = run_step(0, halo, start_position, None, cells)
     lead = chosen(sides[0, 0:1], lead, shifted(lead, "ty", 1), shifted(lead, "ty", -1))
     lead_west, lead_east = shifted(lead, "tx", 1), shifted(lead, "tx", -1)
     rows = up(HISTORY, 8)
     scalar = [pl.BlockSpec(memory_space=pltpu.SMEM)]
-    shape = (members, 2 * rows, LANES) if paired else (2, 2, rows, members * per_owner)
-    placed, target = pl.pallas_call(
-        functools.partial(place_history_kernel, per_owner, paired, within),
-        out_shape=[jax.ShapeDtypeStruct(shape, f32), jax.ShapeDtypeStruct((2, slots, LANES), jnp.int32)],
-        in_specs=scalar + whole(6),
-        out_specs=whole(2),
-        cost_estimate=cost(2 * 4 * rows * slots * 4 * slots, 3000000),
-        compiler_params=grant,
-        name="place_history",
-    )(half, owner.reshape(1, slots), raw, past, far_owner, far_raw, far_past)
+    span = members * per_owner
+    shape = (members, rows, LANES) if paired else (2, rows, span)
+
+    def place(owner, raw, past, skipped):
+        return pl.pallas_call(
+            functools.partial(place_history_kernel, per_owner, paired, within, skipped),
+            out_shape=[jax.ShapeDtypeStruct(shape, f32), jax.ShapeDtypeStruct((slots, span), bf16)],
+            in_specs=scalar + whole(3),
+            out_specs=whole(2),
+            cost_estimate=cost(2 * 4 * rows * slots * span, 3000000),
+            compiler_params=grant,
+            name="place_history",
+        )(half, owner, raw, past)
+
+    placed, onehot = place(owner.reshape(1, slots), raw, past, 0)
+    far_placed, far_onehot = place(far_owner, far_raw, far_past, moving)
     samples = pl.pallas_call(
         functools.partial(last_samples_kernel, (float(tile_rows), float(tile_cols))),
-        out_shape=jax.ShapeDtypeStruct((8, slots), f32),
+        out_shape=jax.ShapeDtypeStruct((2 * STEPS, slots), f32),
         in_specs=whole(7),
         out_specs=whole(1)[0],
         cost_estimate=cost(1000000, 100000),
@@ -442,28 +445,38 @@
         name="last_samples",
     )(record, lead, lead_west, lead_east, sides, first, cells)
     far_samples = swapped(samples)
-    shape = (members, 2 * rows + 8, LANES) if paired else (2, 2, rows + 8, members * per_owner)
+    depth = 2 * rows + 8
     outgoing = pl.pallas_call(
         functools.partial(place_samples_kernel, per_owner, paired),
-        out_shape=jax.ShapeDtypeStruct(shape, f32),
-        in_specs=scalar + whole(4),
+        out_shape=jax.ShapeDtypeStruct((members, depth, LANES) if paired else (2, depth, span), f32),
+        in_specs=scalar + whole(6),
         out_specs=whole(1)[0],
-        cost_estimate=cost(2 * 2 * 16 * slots * 4 * slots, 3000000),
+        cost_estimate=cost(2 * 2 * 32 * slots * span, 3000000),
         compiler_params=grant,
         name="place_samples",
-    )(half, samples, far_samples, target, placed)
+    )(half, samples, far_samples, onehot, far_onehot, placed, far_placed)
     if not paired:
-        outgoing = outgoing.reshape(2, 2, rows + 8, members, per_owner).transpose(3, 2, 0, 1, 4)
+        outgoing = outgoing.reshape(2, depth, members, per_owner).transpose(2, 1, 0, 3)
     arrived = lax.all_to_all(outgoing, ("ty", "within"), split_axis=0, concat_axis=0, tiled=True)
+    runs = 4 * groups // 4
     if not paired:
+        behind = arrived[:, 2 * rows :]
+        number = jnp.arange(8)[:, None] % 2 == jnp.arange(2)
+        behind = jnp.where(number[None, :, :, None, None], behind[:, :, None], 0.0)
+        arrived = arrived[:, : 2 * rows].reshape(members, 2, rows, 2, per_owner).transpose(0, 2, 1, 3, 4)
+        arrived = jnp.concatenate([arrived, behind], axis=1)
         arrived = arrived.reshape(-1, within, rows + 8, 2, 2, per_owner).transpose(4, 2, 0, 3, 1, 5)
         arrived = arrived.reshape(2, rows + 8, tile_count * per_owner)
     filtered = pl.pallas_call(
         functools.partial(filter_kernel, per_owner, paired, 2 * within),
-        out_shape=jax.ShapeDtypeStruct((SAMPLES * 4 * groups * 2, LANES), f32),
+        out_shape=jax.ShapeDtypeStruct((SAMPLES, runs, 8, LANES), f32),
         in_specs=whole(2),
-        out_specs=whole(1)[0],
-        scratch_shapes=[pltpu.VMEM((rows + 8, LANES), f32)],
+        out_specs=pl.BlockSpec(memory_space=pltpu.HBM),
+        scratch_shapes=[
+            pltpu.VMEM((rows + 8, LANES), f32),
+            pltpu.VMEM((runs, SAMPLES * 8, LANES), f32),
+            pltpu.SemaphoreType.DMA((runs,)),
+        ],
         cost_estimate=cost(2 * 3 * 80 * 80 * 8 * slots, 3000000),
         compiler_params=grant,
         name="filter_series",

time: 66.3 us -> 62 us (0.935)
  starting transfers between devices: 19.5 us -> 17.1 us
  waiting for transfers between devices: 14.2 us -> 13.4 us
  Pallas kernels: 8.36 us -> 7.59 us
    ppermute x3, starting transfers between devices: 10.3 us -> 7.59 us  [swapped(): return lax.ppermute(value, 'half', [(0, 1), (1, 0)])]
    ppermute x8, waiting for transfers between devices: 11.9 us -> 10.7 us  [shifted(): lax.ppermute(value, places[axis], [(i, (i + by) % peers) for i in range(p...]
    pallas_call x1, Pallas kernels: 1.3 us -> 0.56 us  [run(): pl.pallas_call(functools.partial(place_samples_kernel, per_owner, paired)...]
    pallas_call x1, Pallas kernels: 2.23 us -> 1.53 us  [run(): pl.pallas_call(functools.partial(filter_kernel, per_owner, paired, 2 * wi...]
    pallas_call x1 -> x2, Pallas kernels: 1.7 us -> 2.37 us  [place(): pl.pallas_call(functools.partial(place_history_kernel, per_owner, paired,...]
  transfers between devices with their start and end apart: 11 -> 11, of which waited for: 5 -> 5; matrix products, arithmetic and copies ran while one was open for 1% -> 1% of each run, Pallas kernels for 7% -> 9%
where the time goes in v4:
time: 62 us; the launch traced here: 61.8 us
  blocking collectives  20.5 us (33%)
  starting transfers between devices  17.1 us (28%)
  waiting for transfers between devices  13.4 us (22%)
  Pallas kernels  7.59 us (12%)
  local copies, waits for them, and re-layouts  2.77 us (4%)
    all_to_all x1, blocking collectives, run(): lax.all_to_all(outgoing, ('ty', 'within'), split_axis=0, concat_axis=0, t...  20.5 us
    ppermute x8, waiting for transfers between devices, shifted(): lax.ppermute(value, places[axis], [(i, (i + by) % peers) for i in range(p...  10.7 us
    ppermute x8, starting transfers between devices, shifted(): lax.ppermute(value, places[axis], [(i, (i + by) % peers) for i in range(p...  9.52 us
    ppermute x3, starting transfers between devices, swapped(): return lax.ppermute(value, 'half', [(0, 1), (1, 0)])  7.59 us
    ppermute x3, waiting for transfers between devices, swapped(): return lax.ppermute(value, 'half', [(0, 1), (1, 0)])  2.75 us
    pallas_call x1, Pallas kernels, run_step(): pl.pallas_call(functools.partial(step_kernel, step, following), out_shape...  2.55 us
    pallas_call x2, Pallas kernels, place(): pl.pallas_call(functools.partial(place_history_kernel, per_owner, paired,...  2.37 us
    pallas_call x1, Pallas kernels, run(): pl.pallas_call(functools.partial(filter_kernel, per_owner, paired, 2 * wi...  1.53 us
  transfers between devices with their start and end apart: 11, of which 5 were waited for; matrix products, arithmetic and copies ran while one was open for 1% of the time, Pallas kernels for 9%

profile of v4, /device:TPU:0, one launch (start us, length us, event | category | flops | bytes accessed | tf_op | source)
XLA Modules:
  0.0 61.8 jit_solution(8850076129353462228)
XLA Ops:
  0.0 0.8 %slice_reduce_fusion.2 = (f32[2,3,128]{2,1,0:T(4,128)S(1)}, f32[2,3,128]{2,1,0:T(4,128)S(1)}) fusion(f32[2,3,128,128]{3,2,1,0:T(8,128)} %velocity_ref.1), kind=kLoop, calls=%fused_computation.15 | loop fusion | bytes 12288 | tf_op jit(solution)/shard_map/slice | solution.py:404
  0.9 1.1 %bitcast_bitcast_fusion = f32[71,4,2,128]{3,2,0,1:T(2,128)S(1)} fusion(f32[2,71,512]{2,0,1:T(2,128)} %param.10), kind=kLoop, calls=%fused_computation.2 | loop fusion | bytes 581632 | tf_op jit(solution)/shard_map/transpose | solution.py:395
  2.0 0.1 reshape_squeeze.15
  2.0 2.5 %collective-permute-start.1 = (f32[148,128]{1,0:T(8,128)S(1)}, f32[148,128]{1,0:T(8,128)S(1)}, u32[]{:S(2)}, u32[]{:S(2)}) collective-permute-start(f32[148,128]{1,0:T(8,128)S(1)} %get-tuple-element.25), channel_id=1, source_target_pairs={{0,24},{8,0},{16,8},{24,16},{1,25},{9,1},{17,9},{25,17},{2,26},{10... | collective-permute-start | bytes 227336 | tf_op jit(solution)/shard_map/ppermute | solution.py:34
  4.5 0.0 copy-start.3
  4.5 0.0 copy-start.5
  4.5 0.1 copy.14
  4.6 0.2 reshape.69
  4.8 2.7 %collective-permute-start.10 = (f32[426,128]{1,0:T(8,128)S(1)}, f32[426,128]{1,0:T(8,128)S(1)}, u32[]{:S(2)}, u32[]{:S(2)}) collective-permute-start(f32[426,128]{1,0:T(8,128)S(1)} %reshape.69), channel_id=1, source_target_pairs={{0,4},{4,0},{1,5},{5,1},{2,6},{6,2},{3,7},{7,3},{8,12},{12,8},{9,1... | collective-permute-start | bytes 654344 | tf_op jit(solution)/shard_map/ppermute | solution.py:38
  7.4 0.6 find_sides.1.sides_ref
  8.0 0.4 slice_reduce_fusion
  8.5 4.4 %collective-permute-start.3 = (f32[160,128]{1,0:T(8,128)S(1)}, f32[160,128]{1,0:T(8,128)S(1)}, u32[]{:S(2)}, u32[]{:S(2)}) collective-permute-start(f32[160,128]{1,0:T(8,128)S(1)} %get-tuple-element.23), channel_id=1, source_target_pairs={{0,7},{1,0},{2,1},{3,2},{4,3},{5,4},{6,5},{7,6},{8,15},{9,8},{10,9... | collective-permute-start | bytes 245768 | tf_op jit(solution)/shard_map/ppermute | solution.py:34
  13.0 0.1 pad.2.clone
  13.1 2.0 %collective-permute-done.3.east_ref = f32[160,128]{1,0:T(8,128)S(1)} collective-permute-done((f32[160,128]{1,0:T(8,128)S(1)}, f32[160,128]{1,0:T(8,128)S(1)}, u32[]{:S(2)}, u32[]{:S(2)}) %collective-permute-start.3) | collective-permute-done | bytes 81952 | tf_op jit(solution)/shard_map/ppermute | solution.py:34
  15.0 5.2 %collective-permute-done.2.west_ref = f32[160,128]{1,0:T(8,128)S(1)} collective-permute-done((f32[160,128]{1,0:T(8,128)S(1)}, f32[160,128]{1,0:T(8,128)S(1)}, u32[]{:S(2)}, u32[]{:S(2)}) %collective-permute-start.2) | collective-permute-done | bytes 81952 | tf_op jit(solution)/shard_map/ppermute | solution.py:34
  20.2 2.6 %sample_step.1 = (f32[8,512]{1,0:T(8,128)S(1)}, f32[8,128]{1,0:T(8,128)S(1)}, f32[8,512]{1,0:T(8,128)S(1)}) custom-call(f32[2,3,128,128]{3,2,1,0:T(8,128)S(1)} %copy-done, f32[148,128]{1,0:T(8,128)S(1)} %collective-permute-done.north_ref, f32[148,128]{1,0:T(8,128)S(1)} %collective-permute-done.1.south_ref, f32[160,128]{1,0:T(8,128)S(1)} %collective-permute-done.2.west_ref, ...), custom_call_target="tpu_custom_call" | custom-call | flops 1509949440 | bytes 600000 | tf_op jit(solution)/shard_map/sample_step/pallas_call | solution.py:191
  22.8 0.1 collective-permute-start.5
  22.8 0.5 collective-permute-start.4
  23.4 0.1 maximum_maximum_fusion.past_ref
  23.4 4.3 %collective-permute-start.9 = (f32[148,128]{1,0:T(8,128)S(1)}, f32[148,128]{1,0:T(8,128)S(1)}, u32[]{:S(2)}, u32[]{:S(2)}) collective-permute-start(f32[148,128]{1,0:T(8,128)S(1)} %maximum_maximum_fusion.past_ref), channel_id=1, source_target_pairs={{0,4},{4,0},{1,5},{5,1},{2,6},{6,2},{3,7},{7,3},{8,12},{12,8},{9,1... | collective-permute-start | bytes 227336 | tf_op jit(solution)/shard_map/ppermute | solution.py:38
  27.7 0.5 collective-permute-start.7
  28.2 1.6 %collective-permute-start.6 = (f32[8,128]{1,0:T(8,128)S(1)}, f32[8,128]{1,0:T(8,128)S(1)}, u32[]{:S(2)}, u32[]{:S(2)}) collective-permute-start(f32[8,128]{1,0:T(8,128)S(1)} %select_select_fusion.lead_ref), channel_id=1, source_target_pairs={{0,1},{1,2},{2,3},{3,4},{4,5},{5,6},{6,7},{7,0},{8,9},{9,10},{10,1... | collective-permute-start | bytes 12296 | tf_op jit(solution)/shard_map/ppermute | solution.py:34
  29.8 1.2 %place_history.2 = (f32[16,72,128]{2,1,0:T(8,128)S(1)}, bf16[512,1024]{1,0:T(8,128)(2,1)S(1)}) custom-call(s32[1]{0:T(128)} %bitcast.half_ref, f32[1,512]{1,0:T(1,128)S(1)} %get-tuple-element.32.owner_ref, f32[568,128]{1,0:T(8,128)S(1)} %bitcast.32, f32[148,128]{1,0:T(8,128)S(1)} %maximum_maximum_fusion.past_ref), custom_call_target="tpu_custom_call" | custom-call | flops 301989888 | bytes 3000000 | tf_op jit(solution)/shard_map/place_history/pallas_call | solution.py:426
  31.0 0.4 collective-permute-done.7.east_ref
  31.4 3.1 %collective-permute-done.6.west_ref = f32[8,128]{1,0:T(8,128)S(1)} collective-permute-done((f32[8,128]{1,0:T(8,128)S(1)}, f32[8,128]{1,0:T(8,128)S(1)}, u32[]{:S(2)}, u32[]{:S(2)}) %collective-permute-start.6) | collective-permute-done | bytes 4128 | tf_op jit(solution)/shard_map/ppermute | solution.py:34
  34.6 0.7 %collective-permute-start.8 = (f32[4,512]{1,0:T(4,128)S(1)}, f32[4,512]{1,0:T(4,128)S(1)}, u32[]{:S(2)}, u32[]{:S(2)}) collective-permute-start(f32[4,512]{1,0:T(4,128)S(1)} %last_samples.1.samples_ref), channel_id=1, source_target_pairs={{0,4},{4,0},{1,5},{5,1},{2,6},{6,2},{3,7},{7,3},{8,12},{12,8},{9,1... | collective-permute-start | bytes 24584 | tf_op jit(solution)/shard_map/ppermute | solution.py:38
  35.3 1.2 %place_history.3 = (f32[16,72,128]{2,1,0:T(8,128)S(1)}, bf16[512,1024]{1,0:T(8,128)(2,1)S(1)}) custom-call(s32[1]{0:T(128)} %bitcast.half_ref, f32[1,512]{1,0:T(1,128)S(1)} %bitcast.33, f32[426,128]{1,0:T(8,128)S(1)} %collective-permute-done.10.history_ref, f32[148,128]{1,0:T(8,128)S(1)} %collective-permute-done.9.past_ref), custom_call_target="tpu_custom_call" | custom-call | flops 301989888 | bytes 3000000 | tf_op jit(solution)/shard_map/place_history/pallas_call | solution.py:426
  36.4 2.7 %collective-permute-done.8.far_samples_ref = f32[4,512]{1,0:T(4,128)S(1)} collective-permute-done((f32[4,512]{1,0:T(4,128)S(1)}, f32[4,512]{1,0:T(4,128)S(1)}, u32[]{:S(2)}, u32[]{:S(2)}) %collective-permute-start.8) | collective-permute-done | bytes 8224 | tf_op jit(solution)/shard_map/ppermute | solution.py:38
  39.2 0.6 place_samples.1
  39.8 0.0 copy-start.2
  39.8 20.5 %all_to_all.5.arrived_ref = f32[16,152,128]{2,1,0:T(8,128)S(1)} all-to-all(f32[16,152,128]{2,1,0:T(8,128)S(1)} %place_samples.1), channel_id=1, replica_groups=mesh['ty'=4,'half'=2,'within'=4] {'ty','within'}, dimensions={0} | all-to-all | bytes 2490368 | tf_op jit(solution)/shard_map/all_to_all | solution.py:460
  60.2 1.5 %filter_series.1 = f32[73,4,8,128]{3,2,1,0:T(8,128)} custom-call(f32[73,73]{1,0:T(8,128)S(1)} %copy-done.2, f32[16,152,128]{2,1,0:T(8,128)S(1)} %all_to_all.5.arrived_ref), custom_call_target="tpu_custom_call" | custom-call | flops 157286400 | bytes 3000000 | tf_op jit(solution)/shard_map/filter_series/pallas_call | solution.py:470
  (37 shorter events, 0.2 us)
Async XLA Ops:
  0.0 8.0 %copy-start = (f32[2,3,128,128]{3,2,1,0:T(8,128)S(1)}, f32[2,3,128,128]{3,2,1,0:T(8,128)}, u32[]{:S(2)}) copy-start(f32[2,3,128,128]{3,2,1,0:T(8,128)} %velocity_ref.1) | copy-start | bytes 1179652
  0.0 7.4 %copy-start.4 = (s32[1,8]{1,0:T(1,128)S(1)}, s32[1,8]{1,0:T(1,128)}, u32[]{:S(2)}) copy-start(s32[1,8]{1,0:T(1,128)} %leavers_ref.1) | copy-start | bytes 100
  2.0 6.4 %collective-permute-start.1 = (f32[148,128]{1,0:T(8,128)S(1)}, f32[148,128]{1,0:T(8,128)S(1)}, u32[]{:S(2)}, u32[]{:S(2)}) collective-permute-start(f32[148,128]{1,0:T(8,128)S(1)} %get-tuple-element.25), channel_id=1, source_target_pairs={{0,24},{8,0},{16,8},{24,16},{1,25},{9,1},{17,9},{25,17},{2,26},{10... | collective-permute-start | bytes 227336 | tf_op jit(solution)/shard_map/ppermute | solution.py:34
  4.5 8.5 %copy-start.6 = (s32[512,1]{0,1:T(1,128)S(1)}, s32[512,1]{0,1:T(1,128)}, u32[]{:S(2)}) copy-start(s32[512,1]{0,1:T(1,128)} %param.12) | copy-start | bytes 6148
  4.5 4.0 %collective-permute-start = (f32[148,128]{1,0:T(8,128)S(1)}, f32[148,128]{1,0:T(8,128)S(1)}, u32[]{:S(2)}, u32[]{:S(2)}) collective-permute-start(f32[148,128]{1,0:T(8,128)S(1)} %get-tuple-element.26), channel_id=1, source_target_pairs={{0,8},{8,16},{16,24},{24,0},{1,9},{9,17},{17,25},{25,1},{2,10},{10... | collective-permute-start | bytes 227336 | tf_op jit(solution)/shard_map/ppermute | solution.py:34
  4.5 15.7 %copy-start.3 = (s32[2,4,2,512]{3,2,1,0:T(2,128)S(1)}, s32[2,4,2,512]{3,2,1,0:T(2,128)}, u32[]{:S(2)}) copy-start(s32[2,4,2,512]{3,2,1,0:T(2,128)} %cells_ref.3) | copy-start | bytes 98308
  4.5 15.7 %copy-start.5 = (f32[2,512]{1,0:T(2,128)S(1)}, f32[2,512]{1,0:T(2,128)}, u32[]{:S(2)}) copy-start(f32[2,512]{1,0:T(2,128)} %point_ref.1) | copy-start | bytes 12292
  4.8 30.5 %collective-permute-start.10 = (f32[426,128]{1,0:T(8,128)S(1)}, f32[426,128]{1,0:T(8,128)S(1)}, u32[]{:S(2)}, u32[]{:S(2)}) collective-permute-start(f32[426,128]{1,0:T(8,128)S(1)} %reshape.69), channel_id=1, source_target_pairs={{0,4},{4,0},{1,5},{5,1},{2,6},{6,2},{3,7},{7,3},{8,12},{12,8},{9,1... | collective-permute-start | bytes 654344 | tf_op jit(solution)/shard_map/ppermute | solution.py:38
  8.5 6.5 %collective-permute-start.3 = (f32[160,128]{1,0:T(8,128)S(1)}, f32[160,128]{1,0:T(8,128)S(1)}, u32[]{:S(2)}, u32[]{:S(2)}) collective-permute-start(f32[160,128]{1,0:T(8,128)S(1)} %get-tuple-element.23), channel_id=1, source_target_pairs={{0,7},{1,0},{2,1},{3,2},{4,3},{5,4},{6,5},{7,6},{8,15},{9,8},{10,9... | collective-permute-start | bytes 245768 | tf_op jit(solution)/shard_map/ppermute | solution.py:34
  13.0 7.2 %collective-permute-start.2 = (f32[160,128]{1,0:T(8,128)S(1)}, f32[160,128]{1,0:T(8,128)S(1)}, u32[]{:S(2)}, u32[]{:S(2)}) collective-permute-start(f32[160,128]{1,0:T(8,128)S(1)} %get-tuple-element.24), channel_id=1, source_target_pairs={{0,1},{1,2},{2,3},{3,4},{4,5},{5,6},{6,7},{7,0},{8,9},{9,10},{10,1... | collective-permute-start | bytes 245768 | tf_op jit(solution)/shard_map/ppermute | solution.py:34
  13.1 16.7 %copy-start.1 = (f32[2,71,512]{2,0,1:T(2,128)S(1)}, f32[2,71,512]{2,0,1:T(2,128)}, u32[]{:S(2)}) copy-start(f32[2,71,512]{2,0,1:T(2,128)} %param.10) | copy-start | bytes 872452
  22.8 4.9 %collective-permute-start.5 = (f32[8,128]{1,0:T(8,128)S(1)}, f32[8,128]{1,0:T(8,128)S(1)}, u32[]{:S(2)}, u32[]{:S(2)}) collective-permute-start(f32[8,128]{1,0:T(8,128)S(1)} %get-tuple-element.13), channel_id=1, source_target_pairs={{0,24},{8,0},{16,8},{24,16},{1,25},{9,1},{17,9},{25,17},{2,26},{10... | collective-permute-start | bytes 12296 | tf_op jit(solution)/shard_map/ppermute | solution.py:34
  22.8 4.9 %collective-permute-start.4 = (f32[8,128]{1,0:T(8,128)S(1)}, f32[8,128]{1,0:T(8,128)S(1)}, u32[]{:S(2)}, u32[]{:S(2)}) collective-permute-start(f32[8,128]{1,0:T(8,128)S(1)} %get-tuple-element.13), channel_id=1, source_target_pairs={{0,8},{8,16},{16,24},{24,0},{1,9},{9,17},{17,25},{25,1},{2,10},{10... | collective-permute-start | bytes 12296 | tf_op jit(solution)/shard_map/ppermute | solution.py:34
  23.4 11.8 %collective-permute-start.9 = (f32[148,128]{1,0:T(8,128)S(1)}, f32[148,128]{1,0:T(8,128)S(1)}, u32[]{:S(2)}, u32[]{:S(2)}) collective-permute-start(f32[148,128]{1,0:T(8,128)S(1)} %maximum_maximum_fusion.past_ref), channel_id=1, source_target_pairs={{0,4},{4,0},{1,5},{5,1},{2,6},{6,2},{3,7},{7,3},{8,12},{12,8},{9,1... | collective-permute-start | bytes 227336 | tf_op jit(solution)/shard_map/ppermute | solution.py:38
  27.7 3.7 %collective-permute-start.7 = (f32[8,128]{1,0:T(8,128)S(1)}, f32[8,128]{1,0:T(8,128)S(1)}, u32[]{:S(2)}, u32[]{:S(2)}) collective-permute-start(f32[8,128]{1,0:T(8,128)S(1)} %select_select_fusion.lead_ref), channel_id=1, source_target_pairs={{0,7},{1,0},{2,1},{3,2},{4,3},{5,4},{6,5},{7,6},{8,15},{9,8},{10,9... | collective-permute-start | bytes 12296 | tf_op jit(solution)/shard_map/ppermute | solution.py:34
  28.2 6.3 %collective-permute-start.6 = (f32[8,128]{1,0:T(8,128)S(1)}, f32[8,128]{1,0:T(8,128)S(1)}, u32[]{:S(2)}, u32[]{:S(2)}) collective-permute-start(f32[8,128]{1,0:T(8,128)S(1)} %select_select_fusion.lead_ref), channel_id=1, source_target_pairs={{0,1},{1,2},{2,3},{3,4},{4,5},{5,6},{6,7},{7,0},{8,9},{9,10},{10,1... | collective-permute-start | bytes 12296 | tf_op jit(solution)/shard_map/ppermute | solution.py:34
  34.6 4.6 %collective-permute-start.8 = (f32[4,512]{1,0:T(4,128)S(1)}, f32[4,512]{1,0:T(4,128)S(1)}, u32[]{:S(2)}, u32[]{:S(2)}) collective-permute-start(f32[4,512]{1,0:T(4,128)S(1)} %last_samples.1.samples_ref), channel_id=1, source_target_pairs={{0,4},{4,0},{1,5},{5,1},{2,6},{6,2},{3,7},{7,3},{8,12},{12,8},{9,1... | collective-permute-start | bytes 24584 | tf_op jit(solution)/shard_map/ppermute | solution.py:38
  39.8 20.5 %copy-start.2 = (f32[73,73]{1,0:T(8,128)S(1)}, f32[73,73]{1,0:T(8,128)}, u32[]{:S(2)}) copy-start(f32[73,73]{1,0:T(8,128)} %matrix_ref.1) | copy-start | bytes 63952

commit v5 on v4

--- a/solution.py
+++ b/solution.py
@@ -29,9 +29,14 @@
 places = {"ty": "ty", "tx": ("half", "within")}
 
 
-def shifted(value, axis, by):
+def exchanged(up, down, axis):
     peers = lax.axis_size(places[axis])
-    return lax.ppermute(value, places[axis], [(i, (i + by) % peers) for i in range(peers)])
+    even = lax.axis_index(places[axis]) % 2 == 0
+    near = [(i, i ^ 1) for i in range(peers)]
+    far = [(i, (i - 1 if i % 2 == 0 else i + 1) % peers) for i in range(peers)]
+    first = lax.ppermute(up if up is down else jnp.where(even, up, down), places[axis], near)
+    second = lax.ppermute(up if up is down else jnp.where(even, down, up), places[axis], far)
+    return jnp.where(even, second, first), jnp.where(even, first, second)
 
 
 def swapped(value):
@@ -62,59 +67,51 @@
 grant = pltpu.CompilerParams(vmem_limit_bytes=16 * 1024 * 1024)
 
 
-def build_table(table_ref, number, snapshots, weight, velocity_ref, north_ref, south_ref, west_ref, east_ref, columns):
+def sections_of(step, following):
+    own = [(step, 0, 0)] if step == 0 else []
+    own += [(step, 1, 1), (step, 2, 1), (step, 3, 2)]
+    return own + ([(step + 1, 0, 2)] if following else [])
+
+
+def at_time(read, step, table):
+    if table == 1:
+        return 0.5 * (read(step) + read(step + 1))
+    return read(step + table // 2)
+
+
+def side_by_side(value):
+    return jnp.concatenate(halves(value), axis=1)
+
+
+def doubled(value):
+    return jnp.concatenate([value, value], axis=0)
+
+
+def inner_kernel(step, following, velocity_ref, cells_ref, part_ref, cols_ref, rows_ref, table_ref):
     rows, cols = velocity_ref.shape[2], velocity_ref.shape[3]
-    count = velocity_ref.shape[1]
-    base = 2 * HISTORY
-    block = up(rows + 2, 16)
-    lane = iota((16, cols), 1)
-    sub = iota((16, cols), 0)
-    for c in range(2):
-        inner = None
-        for a in snapshots:
-            k = c * count + a
-            body = velocity_ref[c, a]
-            side = pltpu.roll(columns, (cols - k) % cols, 1)
-            at = base + k
-            top, low = north_ref[at : at + 1], south_ref[at : at + 1]
-            edge = jnp.where(sub == 0, top, jnp.where(sub == 1, low, 0.0))
-            at += 2 * count
-            north_west, north_east = west_ref[at : at + 1, cols - 1 :], east_ref[at : at + 1, 0:1]
-            at += 2 * count
-            south_west, south_east = west_ref[at : at + 1, cols - 1 :], east_ref[at : at + 1, 0:1]
-            west = jnp.where(sub == 0, north_west, jnp.where(sub == 1, south_west, 0.0))
-            east = jnp.where(sub == 0, north_east, jnp.where(sub == 1, south_east, 0.0))
-            corner = jnp.where(lane == 0, west, jnp.where(lane == 8, east, 0.0))
-            parts = (body, side, edge, corner)
-            inner = parts if inner is None else tuple(p + q for p, q in zip(inner, parts))
-        body, side, edge, corner = (weight * p if weight != 1.0 else p for p in inner)
-        for split, (b, s, e, n) in enumerate(zip(halves(body), halves(side), halves(edge), halves(corner))):
-            at = (split * 2 + c) * block
-            table_ref[number, at : at + rows, 0:cols] = b
-            table_ref[number, at : at + rows, cols : 2 * cols] = s
-            table_ref[number, at + rows : at + block, 0:cols] = e
-            table_ref[number, at + rows : at + block, cols : 2 * cols] = n
-
-
-def read_corners(table_ref, number, cell, rows, cols):
-    block = up(rows + 2, 16)
-    slots = cell.shape[1]
-    cy, cx = cell[0:1], cell[1:2]
-    at = iota((2 * cols, slots), 0)
-    left = picked(at == jnp.where(cx < 0, cols, cx)).astype(bf16)
-    right = picked(at == jnp.where(cx + 1 >= cols, cols + 8, cx + 1)).astype(bf16)
-    row = iota((block, slots), 0)
-    upper = row == jnp.where(cy < 0, rows, cy)
-    lower = row == jnp.where(cy + 1 >= rows, rows + 1, cy + 1)
-    table = table_ref[number]
-    values = {}
-    for side, onehot in enumerate((left, right)):
-        product = jnp.dot(table, onehot, preferred_element_type=f32)
+    slots = cells_ref.shape[3]
+    for table in range(3):
         for c in range(2):
-            column = product[c * block : (c + 1) * block] + product[(2 + c) * block : (3 + c) * block]
-            values[0, side, c] = jnp.sum(jnp.where(upper, column, 0.0), axis=0, keepdims=True)
-            values[1, side, c] = jnp.sum(jnp.where(lower, column, 0.0), axis=0, keepdims=True)
-    return [[values[v, h, c] for c in range(2)] for v in range(2) for h in range(2)]
+            value = at_time(lambda a: velocity_ref[c, a], step, table)
+            table_ref[table, c * rows : (c + 1) * rows] = side_by_side(value)
+    col = iota((cols, slots), 0)
+    row = iota((rows, slots), 0)
+    for number, (k, section, table) in enumerate(sections_of(step, following)):
+        cy, cx = cells_ref[k, section, 0:1], cells_ref[k, section, 1:2]
+        across = [picked(row == cy), picked(row == cy + 1)]
+        for v in range(2):
+            rows_ref[number, v] = across[v].astype(bf16)
+        values = {}
+        for h in range(2):
+            onehot = picked(col == cx + h).astype(bf16)
+            cols_ref[number, h] = onehot
+            product = jnp.dot(table_ref[table], doubled(onehot), preferred_element_type=f32)
+            for c in range(2):
+                for v in range(2):
+                    kept = across[v] * product[c * rows : (c + 1) * rows]
+                    values[v, h, c] = jnp.sum(kept, axis=0, keepdims=True)
+        corners = [values[v, h, c] for v in range(2) for h in range(2) for c in range(2)]
+        part_ref[number] = jnp.concatenate(corners, axis=0)
 
 
 def bilinear(corners, point, cell):
@@ -131,40 +128,63 @@
     return [p + factor * s for p, s in zip(point, speed)]
 
 
-def halo_columns(west_ref, east_ref, count, cols):
-    zeros = jnp.zeros((8 - count, cols), f32)
-    base = 2 * HISTORY
-    west, east = west_ref[base : base + count], east_ref[base : base + count]
-    flat = jnp.concatenate([west, zeros, east, zeros, jnp.zeros((cols - 16, cols), f32)], axis=0)
-    return flat.T
-
-
-def step_kernel(step, following, velocity_ref, north_ref, south_ref, west_ref, east_ref, point_ref, cells_ref, *rest):
+def step_kernel(
+    step, following, velocity_shape, part_ref, cols_ref, rows_ref, north_ref, south_ref, west_ref, east_ref, point_ref, cells_ref, *rest
+):
     if step > 0:
         first_ref, rest = rest[0], rest[1:]
     if following:
-        record_ref, lead_ref, next_ref, table_ref = rest
+        record_ref, lead_ref, next_ref = rest
     else:
-        record_ref, lead_ref, table_ref = rest
-    rows, cols = velocity_ref.shape[2], velocity_ref.shape[3]
-    columns = halo_columns(west_ref, east_ref, 2 * velocity_ref.shape[1], cols)
-    fields = (velocity_ref, north_ref, south_ref, west_ref, east_ref, columns)
-    build_table(table_ref, 0, (step,), 1.0, *fields)
-    build_table(table_ref, 1, (step, step + 1), 0.5, *fields)
-    build_table(table_ref, 2, (step + 1,), 1.0, *fields)
+        record_ref, lead_ref = rest
+    count, rows, cols = velocity_shape
+    ends = ((north_ref, south_ref), (west_ref, east_ref))
+    tables = []
+    for pair in ends:
+        lines = []
+        for table in range(3):
+            for c in range(2):
+                for ref in pair:
+                    lines.append(at_time(lambda a: ref[c * count + a : c * count + a + 1], step, table))
+        lines.append(jnp.zeros((4, cols), f32))
+        tables.append(side_by_side(jnp.concatenate(lines, axis=0)))
+
+    def tip(table, c, v, h):
+        ref, at = ends[1][h], (1 + v) * 2 * count + c * count
+        lane = slice(cols - 1, cols) if h == 0 else slice(0, 1)
+        return at_time(lambda a: ref[at + a : at + a + 1, lane], step, table)
+
+    def corners_of(number):
+        k, section, table = sections_of(step, following)[number]
+        cy, cx = cells_ref[k, section, 0:1], cells_ref[k, section, 1:2]
+        outside = ((cy < 0, cy + 1 >= rows), (cx < 0, cx + 1 >= cols))
+        ends_of = [
+            jnp.dot(tables[0], doubled(cols_ref[number, i]), preferred_element_type=f32) for i in range(2)
+        ], [jnp.dot(tables[1], doubled(rows_ref[number, i]), preferred_element_type=f32) for i in range(2)]
+        result = []
+        for v in range(2):
+            for h in range(2):
+                pair = []
+                for c in range(2):
+                    value = part_ref[number, 4 * v + 2 * h + c : 4 * v + 2 * h + c + 1]
+                    at = 4 * table + 2 * c
+                    value += jnp.where(outside[0][v], ends_of[0][h][at + v : at + v + 1], 0.0)
+                    value += jnp.where(outside[1][h], ends_of[1][v][at + h : at + h + 1], 0.0)
+                    value += jnp.where(outside[0][v] & outside[1][h], tip(table, c, v, h), 0.0)
+                    pair.append(value)
+                result.append(pair)
+        return result
+
+    corners = [corners_of(number) for number in range(len(sections_of(step, following)))]
     sections = [cells_ref[step, s] for s in range(4)]
-    if step == 0:
-        first = read_corners(table_ref, 0, sections[0], rows, cols)
-    else:
-        first = [[first_ref[2 * i + c : 2 * i + c + 1] for c in range(2)] for i in range(4)]
-    second = read_corners(table_ref, 1, sections[1], rows, cols)
-    third = read_corners(table_ref, 1, sections[2], rows, cols)
-    fourth = read_corners(table_ref, 2, sections[3], rows, cols)
+    if step > 0:
+        given = [[first_ref[2 * i + c : 2 * i + c + 1] for c in range(2)] for i in range(4)]
+        corners = [given] + corners
     point = [point_ref[0:1], point_ref[1:2]]
-    k_one = bilinear(first, point, sections[0])
-    k_two = bilinear(second, along(point, 0.5 * drift, k_one), sections[1])
-    k_three = bilinear(third, along(point, 0.5 * drift, k_two), sections[2])
-    k_four = bilinear(fourth, along(point, drift, k_three), sections[3])
+    k_one = bilinear(corners[0], point, sections[0])
+    k_two = bilinear(corners[1], along(point, 0.5 * drift, k_one), sections[1])
+    k_three = bilinear(corners[2], along(point, 0.5 * drift, k_two), sections[2])
+    k_four = bilinear(corners[3], along(point, drift, k_three), sections[3])
     point = [
         p + drift / 6.0 * (a + 2.0 * b + 2.0 * c + d)
         for p, a, b, c, d in zip(point, k_one, k_two, k_three, k_four)
@@ -175,26 +195,38 @@
     band = step * 8 * MOST
     lead_ref[...] = record[:, band : band + 8 * MOST]
     if following:
-        ahead = read_corners(table_ref, 2, cells_ref[step + 1, 0], rows, cols)
-        next_ref[...] = jnp.concatenate([value for corner in ahead for value in corner], axis=0)
+        next_ref[...] = jnp.concatenate([value for corner in corners[4] for value in corner], axis=0)
 
 
 def run_step(step, halo, point, first, cells):
-    velocity = halo[0]
+    velocity, *ends = halo
     slots = point.shape[1]
     following = step + 1 < STEPS
-    cols = velocity.shape[3]
-    block = up(velocity.shape[2] + 2, 16)
-    operands = (*halo, point, cells) + ((first,) if step > 0 else ())
+    rows, cols = velocity.shape[2:]
+    number = len(sections_of(step, following))
+    inner = pl.pallas_call(
+        functools.partial(inner_kernel, step, following),
+        out_shape=[
+            jax.ShapeDtypeStruct((number, 8, slots), f32),
+            jax.ShapeDtypeStruct((number, 2, cols, slots), bf16),
+            jax.ShapeDtypeStruct((number, 2, rows, slots), bf16),
+        ],
+        in_specs=whole(2),
+        out_specs=whole(3),
+        scratch_shapes=[pltpu.VMEM((3, 2 * rows, 2 * cols), bf16)],
+        cost_estimate=cost(number * 2 * 2 * rows * 2 * cols * slots * 2, 600000),
+        compiler_params=grant,
+        name="sample_inner",
+    )(velocity, cells)
+    operands = (*inner, *ends, point, cells) + ((first,) if step > 0 else ())
     shape = jax.ShapeDtypeStruct((8, slots), f32)
     shapes = [shape, jax.ShapeDtypeStruct((8, 8 * MOST), f32)] + ([shape] if following else [])
     return pl.pallas_call(
-        functools.partial(step_kernel, step, following),
+        functools.partial(step_kernel, step, following, velocity.shape[1:]),
         out_shape=shapes,
         in_specs=whole(len(operands)),
         out_specs=whole(len(shapes)),
-        scratch_shapes=[pltpu.VMEM((3, 4 * block, 2 * cols), bf16)],
-        cost_estimate=cost(10 * 4 * block * 2 * cols * slots * 2, 600000),
+        cost_estimate=cost(number * 2 * 4 * 16 * 2 * cols * slots, 600000),
         compiler_params=grant,
         name="sample_step",
     )(*operands)
@@ -281,7 +313,7 @@
             out_ref[1, :, start : start + chunk] = placed[rows:]
 
 
-def last_samples_kernel(tile, record_ref, lead_ref, west_ref, east_ref, sides_ref, next_ref, cells_ref, out_ref):
+def last_samples_kernel(tile, record_ref, lead_ref, west_ref, east_ref, sides_ref, next_ref, cells_ref, out_ref, point_ref):
     moved = lead_ref.shape[1]
     sides = sides_ref[0]
     lead = chosen(sides[1:2], lead_ref[...], west_ref[...], east_ref[...])
@@ -291,6 +323,7 @@
     corners = [[next_ref[2 * i + c : 2 * i + c + 1] for c in range(2)] for i in range(4)]
     last = bilinear(corners, [record[0:1], record[1:2]], cells_ref[STEPS - 1, 0])
     out_ref[...] = jnp.concatenate([record[2:3], last[0], record[3:4], last[1]], axis=0)
+    point_ref[...] = record[0:2]
 
 
 def place_samples_kernel(
@@ -391,21 +424,21 @@
     per_owner = 4 * slots // tile_count
     paired = 2 * per_owner == LANES
     groups = slots // LANES
+
+    def joined(*parts):
+        return jnp.concatenate([part.reshape(-1, LANES) for part in parts], axis=0)
+
     lines = 2 * HISTORY
+    north, south = exchanged(joined(velocity[:, :, tile_rows - 1]), joined(velocity[:, :, 0]), "ty")
+    west, east = exchanged(
+        joined(velocity[:, :, :, tile_cols - 1], north, south), joined(velocity[:, :, :, 0], north, south), "tx"
+    )
     by_rows = history.reshape(2, HISTORY, groups, LANES).transpose(1, 2, 0, 3)
     raw = by_rows.reshape(2 * groups * HISTORY, LANES)
+    sides = find_sides(leavers)
     past = by_rows[:, 0].reshape(lines, LANES)
-    sides = find_sides(leavers)
-
-    def joined(*parts):
-        return jnp.concatenate([part.reshape(-1, LANES) for part in parts], axis=0)
-
-    north = shifted(joined(past, velocity[:, :, tile_rows - 1]), "ty", 1)
-    south = shifted(joined(past, velocity[:, :, 0]), "ty", -1)
-    past = chosen(sides[0, 0:1], past, north[:lines], south[:lines])
-    west = shifted(joined(past, velocity[:, :, :, tile_cols - 1], north[lines:], south[lines:]), "tx", 1)
-    east = shifted(joined(past, velocity[:, :, :, 0], north[lines:], south[lines:]), "tx", -1)
-    past = chosen(sides[0, 1:2], past, west[:lines], east[:lines])
+    past = chosen(sides[0, 0:1], past, *exchanged(past, past, "ty"))
+    past = chosen(sides[0, 1:2], past, *exchanged(past, past, "tx"))
     halo = (velocity, north, south, west, east)
     owner = owner.astype(f32)
     past = joined(past, owner, jnp.zeros((2, LANES), f32))
@@ -415,8 +448,8 @@
     far_owner = far_past[lines : lines + groups].reshape(1, slots)
     half = lax.axis_index("half").reshape(1)
     record, lead, first = run_step(0, halo, start_position, None, cells)
-    lead = chosen(sides[0, 0:1], lead, shifted(lead, "ty", 1), shifted(lead, "ty", -1))
-    lead_west, lead_east = shifted(lead, "tx", 1), shifted(lead, "tx", -1)
+    lead = chosen(sides[0, 0:1], lead, *exchanged(lead, lead, "ty"))
+    lead_west, lead_east = exchanged(lead, lead, "tx")
     rows = up(HISTORY, 8)
     scalar = [pl.BlockSpec(memory_space=pltpu.SMEM)]
     span = members * per_owner
@@ -435,15 +468,16 @@
 
     placed, onehot = place(owner.reshape(1, slots), raw, past, 0)
     far_placed, far_onehot = place(far_owner, far_raw, far_past, moving)
-    samples = pl.pallas_call(
+    samples, point = pl.pallas_call(
         functools.partial(last_samples_kernel, (float(tile_rows), float(tile_cols))),
-        out_shape=jax.ShapeDtypeStruct((2 * STEPS, slots), f32),
+        out_shape=[jax.ShapeDtypeStruct((2 * STEPS, slots), f32), jax.ShapeDtypeStruct((2, slots), f32)],
         in_specs=whole(7),
-        out_specs=whole(1)[0],
+        out_specs=whole(2),
         cost_estimate=cost(1000000, 100000),
         compiler_params=grant,
         name="last_samples",
     )(record, lead, lead_west, lead_east, sides, first, cells)
+    run_step(STEPS - 1, halo, point, first, cells)
     far_samples = swapped(samples)
     depth = 2 * rows + 8
     outgoing = pl.pallas_call(

time: 62 us -> 61.5 us (level)
  waiting for transfers between devices: 13.4 us -> 4.16 us
  starting transfers between devices: 17.1 us -> 23.9 us
  blocking collectives: 20.5 us -> 21.6 us
  local copies, waits for them, and re-layouts: 2.77 us -> 1.98 us
  other arithmetic: 0.16 us -> 0.95 us
  Pallas kernels: 7.59 us -> 8.31 us
    ppermute x8 -> x12, starting transfers between devices: 9.52 us -> 18.1 us  [the longest x6 11.8 us: exchanged(): lax.ppermute(up if up is down else jnp.where(even, down, up), places[axis...]
    ppermute x8 -> x12, waiting for transfers between devices: 10.7 us -> 2.98 us  [the longest x6 2.97 us: exchanged(): lax.ppermute(up if up is down else jnp.where(even, down, up), places[axis...]
    ppermute x3, starting transfers between devices: 7.59 us -> 5.8 us  [swapped(): return lax.ppermute(value, 'half', [(0, 1), (1, 0)])]
    ppermute x3, waiting for transfers between devices: 2.75 us -> 1.18 us  [swapped(): return lax.ppermute(value, 'half', [(0, 1), (1, 0)])]
    all_to_all x1, blocking collectives: 20.5 us -> 21.6 us  [run(): lax.all_to_all(outgoing, ('ty', 'within'), split_axis=0, concat_axis=0, t...]
    slice x4 -> x1, local copies, waits for them, and re-layouts: 1.26 us -> 0.42 us  [run(): velocity[:, :, :, tile_cols - 1]]
    select_n x0 -> x5, other arithmetic: none -> 0.81 us  [the longest x2 0.79 us: exchanged(): jnp.where(even, up, down)]
    pallas_call x1 -> x2, Pallas kernels: 2.55 us -> 2.71 us  [the longest x1 1.9 us: run_step(): pl.pallas_call(functools.partial(inner_kernel, step, following), out_shap...]
  transfers between devices with their start and end apart: 11 -> 15, of which waited for: 5 -> 5; matrix products, arithmetic and copies ran while one was open for 1% -> 3% of each run, Pallas kernels for 9% -> 10%
where the time goes in v5:
time: 61.5 us; the launch traced here: 61.2 us
  starting transfers between devices  23.9 us (39%)
  blocking collectives  21.6 us (35%)
  Pallas kernels  8.31 us (14%)
  waiting for transfers between devices  4.16 us (7%)
  local copies, waits for them, and re-layouts  1.98 us (3%)
  other arithmetic  0.95 us (2%)
    all_to_all x1, blocking collectives, run(): lax.all_to_all(outgoing, ('ty', 'within'), split_axis=0, concat_axis=0, t...  21.6 us
    ppermute x6, starting transfers between devices, exchanged(): lax.ppermute(up if up is down else jnp.where(even, down, up), places[axis...  11.8 us
    ppermute x6, starting transfers between devices, exchanged(): lax.ppermute(up if up is down else jnp.where(even, up, down), places[axis...  6.27 us
    ppermute x3, starting transfers between devices, swapped(): return lax.ppermute(value, 'half', [(0, 1), (1, 0)])  5.8 us
    ppermute x6, waiting for transfers between devices, exchanged(): lax.ppermute(up if up is down else jnp.where(even, down, up), places[axis...  2.97 us
    pallas_call x2, Pallas kernels, place(): pl.pallas_call(functools.partial(place_history_kernel, per_owner, paired,...  2.35 us
    pallas_call x1, Pallas kernels, run_step(): pl.pallas_call(functools.partial(inner_kernel, step, following), out_shap...  1.9 us
    pallas_call x1, Pallas kernels, run(): pl.pallas_call(functools.partial(filter_kernel, per_owner, paired, 2 * wi...  1.53 us
  transfers between devices with their start and end apart: 15, of which 5 were waited for; matrix products, arithmetic and copies ran while one was open for 3% of the time, Pallas kernels for 10%

profile of v5, /device:TPU:0, one launch (start us, length us, event | category | flops | bytes accessed | tf_op | source)
XLA Modules:
  0.0 61.2 jit_solution(18150708343517648308)
XLA Ops:
  0.0 1.1 %bitcast_bitcast_fusion = f32[71,4,2,128]{3,2,0,1:T(2,128)S(1)} fusion(f32[2,71,512]{2,0,1:T(2,128)} %param.10), kind=kLoop, calls=%fused_computation.2 | loop fusion | bytes 581632 | tf_op jit(solution)/shard_map/transpose | solution.py:436
  1.2 0.6 collective-permute-start.10
  1.8 2.6 %collective-permute-start.9 = (f32[142,128]{1,0:T(8,128)S(1)}, f32[142,128]{1,0:T(8,128)S(1)}, u32[]{:S(2)}, u32[]{:S(2)}) collective-permute-start(f32[142,128]{1,0:T(8,128)S(1)} %reshape_squeeze.13), channel_id=1, source_target_pairs={{0,24},{8,16},{16,8},{24,0},{1,25},{9,17},{17,9},{25,1},{2,26},{10... | collective-permute-start | bytes 218120 | tf_op jit(solution)/shard_map/ppermute | solution.py:38
  4.4 0.8 %fusion.3 = (f32[2,3,128]{2,1,0:T(4,128)S(1)}, f32[2,3,128]{2,1,0:T(4,128)S(1)}) fusion(pred[]{:T(512)S(6)} %eq.17, f32[2,3,128,128]{3,2,1,0:T(8,128)} %velocity_ref.1), kind=kLoop, calls=%fused_computation.18 | loop fusion | flops 1536 | bytes 12289 | tf_op jit(solution)/shard_map/jit(_where)/select_n | solution.py:37
  5.2 0.1 collective-permute-start.1
  5.4 0.1 copy.14
  5.4 0.2 reshape.73
  5.6 3.2 %collective-permute-start.14 = (f32[426,128]{1,0:T(8,128)S(1)}, f32[426,128]{1,0:T(8,128)S(1)}, u32[]{:S(2)}, u32[]{:S(2)}) collective-permute-start(f32[426,128]{1,0:T(8,128)S(1)} %reshape.73), channel_id=1, source_target_pairs={{0,4},{4,0},{1,5},{5,1},{2,6},{6,2},{3,7},{7,3},{8,12},{12,8},{9,1... | collective-permute-start | bytes 654344 | tf_op jit(solution)/shard_map/ppermute | solution.py:43
  8.8 0.6 find_sides.1.sides_ref
  9.4 0.4 slice_reduce_fusion
  9.9 1.6 %collective-permute-start.3 = (f32[18,128]{1,0:T(8,128)S(1)}, f32[18,128]{1,0:T(8,128)S(1)}, u32[]{:S(2)}, u32[]{:S(2)}) collective-permute-start(f32[18,128]{1,0:T(8,128)S(1)} %get-tuple-element.33), channel_id=1, source_target_pairs={{0,1},{1,0},{2,3},{3,2},{4,5},{5,4},{6,7},{7,6},{8,9},{9,8},{10,11... | collective-permute-start | bytes 27656 | tf_op jit(solution)/shard_map/ppermute | solution.py:37
  11.5 2.0 %collective-permute-start.2 = (f32[18,128]{1,0:T(8,128)S(1)}, f32[18,128]{1,0:T(8,128)S(1)}, u32[]{:S(2)}, u32[]{:S(2)}) collective-permute-start(f32[18,128]{1,0:T(8,128)S(1)} %get-tuple-element.34), channel_id=1, source_target_pairs={{0,7},{1,2},{2,1},{3,4},{4,3},{5,6},{6,5},{7,0},{8,15},{9,10},{10,... | collective-permute-start | bytes 27656 | tf_op jit(solution)/shard_map/ppermute | solution.py:38
  13.5 1.9 %sample_inner.1 = (f32[5,8,512]{2,1,0:T(8,128)S(1)}, bf16[5,2,128,512]{3,2,1,0:T(8,128)(2,1)S(1)}, bf16[5,2,128,512]{3,2,1,0:T(8,128)(2,1)S(1)}) custom-call(f32[2,3,128,128]{3,2,1,0:T(8,128)S(1)} %copy-done, s32[2,4,2,512]{3,2,1,0:T(2,128)S(1)} %copy-done.2), custom_call_target="tpu_custom_call" | custom-call | flops 671088640 | bytes 600000 | tf_op jit(solution)/shard_map/sample_inner/pallas_call | solution.py:207
  15.4 0.1 pad.2.clone
  15.5 2.5 %collective-permute-done.2 = f32[18,128]{1,0:T(8,128)S(1)} collective-permute-done((f32[18,128]{1,0:T(8,128)S(1)}, f32[18,128]{1,0:T(8,128)S(1)}, u32[]{:S(2)}, u32[]{:S(2)}) %collective-permute-start.2) | collective-permute-done | bytes 9248 | tf_op jit(solution)/shard_map/ppermute | solution.py:38
  18.0 0.8 %sample_step.1 = (f32[8,512]{1,0:T(8,128)S(1)}, f32[8,128]{1,0:T(8,128)S(1)}, f32[8,512]{1,0:T(8,128)S(1)}) custom-call(f32[5,8,512]{2,1,0:T(8,128)S(1)} %get-tuple-element.16.part_ref, bf16[5,2,128,512]{3,2,1,0:T(8,128)(2,1)S(1)} %get-tuple-element.17.cols_ref, bf16[5,2,128,512]{3,2,1,0:T(8,128)(2,1)S(1)} %get-tuple-element.18.rows_ref, ...), custom_call_target="tpu_custom_call" | custom-call | flops 83886080 | bytes 600000 | tf_op jit(solution)/shard_map/sample_step/pallas_call | solution.py:224
  18.9 1.6 %collective-permute-start.4 = (f32[8,128]{1,0:T(8,128)S(1)}, f32[8,128]{1,0:T(8,128)S(1)}, u32[]{:S(2)}, u32[]{:S(2)}) collective-permute-start(f32[8,128]{1,0:T(8,128)S(1)} %get-tuple-element.20), channel_id=1, source_target_pairs={{0,24},{8,16},{16,8},{24,0},{1,25},{9,17},{17,9},{25,1},{2,26},{10... | collective-permute-start | bytes 12296 | tf_op jit(solution)/shard_map/ppermute | solution.py:38
  20.6 1.3 %collective-permute-start.11 = (f32[142,128]{1,0:T(8,128)S(1)}, f32[142,128]{1,0:T(8,128)S(1)}, u32[]{:S(2)}, u32[]{:S(2)}) collective-permute-start(f32[142,128]{1,0:T(8,128)S(1)} %select_select_fusion.1), channel_id=1, source_target_pairs={{0,7},{1,2},{2,1},{3,4},{4,3},{5,6},{6,5},{7,0},{8,15},{9,10},{10,... | collective-permute-start | bytes 218120 | tf_op jit(solution)/shard_map/ppermute | solution.py:38
  22.0 3.8 %collective-permute-start.7 = (f32[8,128]{1,0:T(8,128)S(1)}, f32[8,128]{1,0:T(8,128)S(1)}, u32[]{:S(2)}, u32[]{:S(2)}) collective-permute-start(f32[8,128]{1,0:T(8,128)S(1)} %select_select_fusion.2.lead_ref), channel_id=1, source_target_pairs={{0,1},{1,0},{2,3},{3,2},{4,5},{5,4},{6,7},{7,6},{8,9},{9,8},{10,11... | collective-permute-start | bytes 12296 | tf_op jit(solution)/shard_map/ppermute | solution.py:37
  25.9 4.3 %collective-permute-start.6 = (f32[8,128]{1,0:T(8,128)S(1)}, f32[8,128]{1,0:T(8,128)S(1)}, u32[]{:S(2)}, u32[]{:S(2)}) collective-permute-start(f32[8,128]{1,0:T(8,128)S(1)} %select_select_fusion.2.lead_ref), channel_id=1, source_target_pairs={{0,7},{1,2},{2,1},{3,4},{4,3},{5,6},{6,5},{7,0},{8,15},{9,10},{10,... | collective-permute-start | bytes 12296 | tf_op jit(solution)/shard_map/ppermute | solution.py:38
  30.2 0.1 maximum_maximum_fusion.past_ref
  30.3 1.6 %collective-permute-start.13 = (f32[148,128]{1,0:T(8,128)S(1)}, f32[148,128]{1,0:T(8,128)S(1)}, u32[]{:S(2)}, u32[]{:S(2)}) collective-permute-start(f32[148,128]{1,0:T(8,128)S(1)} %maximum_maximum_fusion.past_ref), channel_id=1, source_target_pairs={{0,4},{4,0},{1,5},{5,1},{2,6},{6,2},{3,7},{7,3},{8,12},{12,8},{9,1... | collective-permute-start | bytes 227336 | tf_op jit(solution)/shard_map/ppermute | solution.py:43
  31.9 0.4 collective-permute-done.6
  32.3 0.6 last_samples.1
  32.9 1.0 %collective-permute-start.8 = (f32[4,512]{1,0:T(4,128)S(1)}, f32[4,512]{1,0:T(4,128)S(1)}, u32[]{:S(2)}, u32[]{:S(2)}) collective-permute-start(f32[4,512]{1,0:T(4,128)S(1)} %get-tuple-element.22.samples_ref), channel_id=1, source_target_pairs={{0,4},{4,0},{1,5},{5,1},{2,6},{6,2},{3,7},{7,3},{8,12},{12,8},{9,1... | collective-permute-start | bytes 24584 | tf_op jit(solution)/shard_map/ppermute | solution.py:43
  33.9 1.2 %place_history.2 = (f32[16,72,128]{2,1,0:T(8,128)S(1)}, bf16[512,1024]{1,0:T(8,128)(2,1)S(1)}) custom-call(s32[1]{0:T(128)} %bitcast.half_ref, f32[1,512]{1,0:T(1,128)S(1)} %get-tuple-element.44.owner_ref, f32[568,128]{1,0:T(8,128)S(1)} %bitcast.32, f32[148,128]{1,0:T(8,128)S(1)} %maximum_maximum_fusion.past_ref), custom_call_target="tpu_custom_call" | custom-call | flops 301989888 | bytes 3000000 | tf_op jit(solution)/shard_map/place_history/pallas_call | solution.py:459
  35.1 0.6 collective-permute-done.13.past_ref
  35.6 1.2 %place_history.3 = (f32[16,72,128]{2,1,0:T(8,128)S(1)}, bf16[512,1024]{1,0:T(8,128)(2,1)S(1)}) custom-call(s32[1]{0:T(128)} %bitcast.half_ref, f32[1,512]{1,0:T(1,128)S(1)} %bitcast.33, f32[426,128]{1,0:T(8,128)S(1)} %collective-permute-done.14.history_ref, f32[148,128]{1,0:T(8,128)S(1)} %collective-permute-done.13.past_ref), custom_call_target="tpu_custom_call" | custom-call | flops 301989888 | bytes 3000000 | tf_op jit(solution)/shard_map/place_history/pallas_call | solution.py:459
  36.8 0.6 %collective-permute-done.8.far_samples_ref = f32[4,512]{1,0:T(4,128)S(1)} collective-permute-done((f32[4,512]{1,0:T(4,128)S(1)}, f32[4,512]{1,0:T(4,128)S(1)}, u32[]{:S(2)}, u32[]{:S(2)}) %collective-permute-start.8) | collective-permute-done | bytes 8224 | tf_op jit(solution)/shard_map/ppermute | solution.py:43
  37.4 0.6 place_samples.1
  38.0 21.6 %all_to_all.5.arrived_ref = f32[16,152,128]{2,1,0:T(8,128)S(1)} all-to-all(f32[16,152,128]{2,1,0:T(8,128)S(1)} %place_samples.1), channel_id=1, replica_groups=mesh['ty'=4,'half'=2,'within'=4] {'ty','within'}, dimensions={0} | all-to-all | bytes 2490368 | tf_op jit(solution)/shard_map/all_to_all | solution.py:494
  59.7 1.5 %filter_series.1 = f32[73,4,8,128]{3,2,1,0:T(8,128)} custom-call(f32[73,73]{1,0:T(8,128)S(1)} %copy-done.3, f32[16,152,128]{2,1,0:T(8,128)S(1)} %all_to_all.5.arrived_ref), custom_call_target="tpu_custom_call" | custom-call | flops 157286400 | bytes 3000000 | tf_op jit(solution)/shard_map/filter_series/pallas_call | solution.py:504
  (46 shorter events, 0.5 us)
Async XLA Ops:
  0.0 9.4 %copy-start = (f32[2,3,128,128]{3,2,1,0:T(8,128)S(1)}, f32[2,3,128,128]{3,2,1,0:T(8,128)}, u32[]{:S(2)}) copy-start(f32[2,3,128,128]{3,2,1,0:T(8,128)} %velocity_ref.1) | copy-start | bytes 1179652
  0.0 8.8 %copy-start.5 = (s32[1,8]{1,0:T(1,128)S(1)}, s32[1,8]{1,0:T(1,128)}, u32[]{:S(2)}) copy-start(s32[1,8]{1,0:T(1,128)} %leavers_ref.1) | copy-start | bytes 100
  0.0 9.4 %copy-start.6 = (s32[512,1]{0,1:T(1,128)S(1)}, s32[512,1]{0,1:T(1,128)}, u32[]{:S(2)}) copy-start(s32[512,1]{0,1:T(1,128)} %param.12) | copy-start | bytes 6148
  1.1 12.4 %copy-start.2 = (s32[2,4,2,512]{3,2,1,0:T(2,128)S(1)}, s32[2,4,2,512]{3,2,1,0:T(2,128)}, u32[]{:S(2)}) copy-start(s32[2,4,2,512]{3,2,1,0:T(2,128)} %cells_ref.5) | copy-start | bytes 98308
  1.2 19.3 %collective-permute-start.10 = (f32[142,128]{1,0:T(8,128)S(1)}, f32[142,128]{1,0:T(8,128)S(1)}, u32[]{:S(2)}, u32[]{:S(2)}) collective-permute-start(f32[142,128]{1,0:T(8,128)S(1)} %reshape_squeeze.13), channel_id=1, source_target_pairs={{0,8},{8,0},{16,24},{24,16},{1,9},{9,1},{17,25},{25,17},{2,10},{10... | collective-permute-start | bytes 218120 | tf_op jit(solution)/shard_map/ppermute | solution.py:37
  1.8 18.7 %collective-permute-start.9 = (f32[142,128]{1,0:T(8,128)S(1)}, f32[142,128]{1,0:T(8,128)S(1)}, u32[]{:S(2)}, u32[]{:S(2)}) collective-permute-start(f32[142,128]{1,0:T(8,128)S(1)} %reshape_squeeze.13), channel_id=1, source_target_pairs={{0,24},{8,16},{16,8},{24,0},{1,25},{9,17},{17,9},{25,1},{2,26},{10... | collective-permute-start | bytes 218120 | tf_op jit(solution)/shard_map/ppermute | solution.py:38
  5.2 4.7 %collective-permute-start.1 = (f32[6,128]{1,0:T(8,128)S(1)}, f32[6,128]{1,0:T(8,128)S(1)}, u32[]{:S(2)}, u32[]{:S(2)}) collective-permute-start(f32[6,128]{1,0:T(8,128)S(1)} %select_n.137), channel_id=1, source_target_pairs={{0,8},{8,0},{16,24},{24,16},{1,9},{9,1},{17,25},{25,17},{2,10},{10... | collective-permute-start | bytes 9224 | tf_op jit(solution)/shard_map/ppermute | solution.py:37
  5.3 4.6 %collective-permute-start = (f32[6,128]{1,0:T(8,128)S(1)}, f32[6,128]{1,0:T(8,128)S(1)}, u32[]{:S(2)}, u32[]{:S(2)}) collective-permute-start(f32[6,128]{1,0:T(8,128)S(1)} %select_n.135), channel_id=1, source_target_pairs={{0,24},{8,16},{16,8},{24,0},{1,25},{9,17},{17,9},{25,1},{2,26},{10... | collective-permute-start | bytes 9224 | tf_op jit(solution)/shard_map/ppermute | solution.py:38
  5.6 30.0 %collective-permute-start.14 = (f32[426,128]{1,0:T(8,128)S(1)}, f32[426,128]{1,0:T(8,128)S(1)}, u32[]{:S(2)}, u32[]{:S(2)}) collective-permute-start(f32[426,128]{1,0:T(8,128)S(1)} %reshape.73), channel_id=1, source_target_pairs={{0,4},{4,0},{1,5},{5,1},{2,6},{6,2},{3,7},{7,3},{8,12},{12,8},{9,1... | collective-permute-start | bytes 654344 | tf_op jit(solution)/shard_map/ppermute | solution.py:43
  9.9 5.6 %collective-permute-start.3 = (f32[18,128]{1,0:T(8,128)S(1)}, f32[18,128]{1,0:T(8,128)S(1)}, u32[]{:S(2)}, u32[]{:S(2)}) collective-permute-start(f32[18,128]{1,0:T(8,128)S(1)} %get-tuple-element.33), channel_id=1, source_target_pairs={{0,1},{1,0},{2,3},{3,2},{4,5},{5,4},{6,7},{7,6},{8,9},{9,8},{10,11... | collective-permute-start | bytes 27656 | tf_op jit(solution)/shard_map/ppermute | solution.py:37
  11.5 6.5 %copy-start.4 = (f32[2,512]{1,0:T(2,128)S(1)}, f32[2,512]{1,0:T(2,128)}, u32[]{:S(2)}) copy-start(f32[2,512]{1,0:T(2,128)} %point_ref.1) | copy-start | bytes 12292
  11.5 6.5 %collective-permute-start.2 = (f32[18,128]{1,0:T(8,128)S(1)}, f32[18,128]{1,0:T(8,128)S(1)}, u32[]{:S(2)}, u32[]{:S(2)}) collective-permute-start(f32[18,128]{1,0:T(8,128)S(1)} %get-tuple-element.34), channel_id=1, source_target_pairs={{0,7},{1,2},{2,1},{3,4},{4,3},{5,6},{6,5},{7,0},{8,15},{9,10},{10,... | collective-permute-start | bytes 27656 | tf_op jit(solution)/shard_map/ppermute | solution.py:38
  18.0 15.9 %copy-start.1 = (f32[2,71,512]{2,0,1:T(2,128)S(1)}, f32[2,71,512]{2,0,1:T(2,128)}, u32[]{:S(2)}) copy-start(f32[2,71,512]{2,0,1:T(2,128)} %param.10) | copy-start | bytes 872452
  18.8 3.1 %collective-permute-start.5 = (f32[8,128]{1,0:T(8,128)S(1)}, f32[8,128]{1,0:T(8,128)S(1)}, u32[]{:S(2)}, u32[]{:S(2)}) collective-permute-start(f32[8,128]{1,0:T(8,128)S(1)} %get-tuple-element.20), channel_id=1, source_target_pairs={{0,8},{8,0},{16,24},{24,16},{1,9},{9,1},{17,25},{25,17},{2,10},{10... | collective-permute-start | bytes 12296 | tf_op jit(solution)/shard_map/ppermute | solution.py:37
  18.9 3.1 %collective-permute-start.4 = (f32[8,128]{1,0:T(8,128)S(1)}, f32[8,128]{1,0:T(8,128)S(1)}, u32[]{:S(2)}, u32[]{:S(2)}) collective-permute-start(f32[8,128]{1,0:T(8,128)S(1)} %get-tuple-element.20), channel_id=1, source_target_pairs={{0,24},{8,16},{16,8},{24,0},{1,25},{9,17},{17,9},{25,1},{2,26},{10... | collective-permute-start | bytes 12296 | tf_op jit(solution)/shard_map/ppermute | solution.py:38
  20.5 9.6 %collective-permute-start.12 = (f32[142,128]{1,0:T(8,128)S(1)}, f32[142,128]{1,0:T(8,128)S(1)}, u32[]{:S(2)}, u32[]{:S(2)}) collective-permute-start(f32[142,128]{1,0:T(8,128)S(1)} %select_select_fusion.1), channel_id=1, source_target_pairs={{0,1},{1,0},{2,3},{3,2},{4,5},{5,4},{6,7},{7,6},{8,9},{9,8},{10,11... | collective-permute-start | bytes 218120 | tf_op jit(solution)/shard_map/ppermute | solution.py:37
  20.6 9.5 %collective-permute-start.11 = (f32[142,128]{1,0:T(8,128)S(1)}, f32[142,128]{1,0:T(8,128)S(1)}, u32[]{:S(2)}, u32[]{:S(2)}) collective-permute-start(f32[142,128]{1,0:T(8,128)S(1)} %select_select_fusion.1), channel_id=1, source_target_pairs={{0,7},{1,2},{2,1},{3,4},{4,3},{5,6},{6,5},{7,0},{8,15},{9,10},{10,... | collective-permute-start | bytes 218120 | tf_op jit(solution)/shard_map/ppermute | solution.py:38
  22.0 9.9 %collective-permute-start.7 = (f32[8,128]{1,0:T(8,128)S(1)}, f32[8,128]{1,0:T(8,128)S(1)}, u32[]{:S(2)}, u32[]{:S(2)}) collective-permute-start(f32[8,128]{1,0:T(8,128)S(1)} %select_select_fusion.2.lead_ref), channel_id=1, source_target_pairs={{0,1},{1,0},{2,3},{3,2},{4,5},{5,4},{6,7},{7,6},{8,9},{9,8},{10,11... | collective-permute-start | bytes 12296 | tf_op jit(solution)/shard_map/ppermute | solution.py:37
  25.9 6.4 %collective-permute-start.6 = (f32[8,128]{1,0:T(8,128)S(1)}, f32[8,128]{1,0:T(8,128)S(1)}, u32[]{:S(2)}, u32[]{:S(2)}) collective-permute-start(f32[8,128]{1,0:T(8,128)S(1)} %select_select_fusion.2.lead_ref), channel_id=1, source_target_pairs={{0,7},{1,2},{2,1},{3,4},{4,3},{5,6},{6,5},{7,0},{8,15},{9,10},{10,... | collective-permute-start | bytes 12296 | tf_op jit(solution)/shard_map/ppermute | solution.py:38
  30.3 5.4 %collective-permute-start.13 = (f32[148,128]{1,0:T(8,128)S(1)}, f32[148,128]{1,0:T(8,128)S(1)}, u32[]{:S(2)}, u32[]{:S(2)}) collective-permute-start(f32[148,128]{1,0:T(8,128)S(1)} %maximum_maximum_fusion.past_ref), channel_id=1, source_target_pairs={{0,4},{4,0},{1,5},{5,1},{2,6},{6,2},{3,7},{7,3},{8,12},{12,8},{9,1... | collective-permute-start | bytes 227336 | tf_op jit(solution)/shard_map/ppermute | solution.py:43
  32.9 4.5 %collective-permute-start.8 = (f32[4,512]{1,0:T(4,128)S(1)}, f32[4,512]{1,0:T(4,128)S(1)}, u32[]{:S(2)}, u32[]{:S(2)}) collective-permute-start(f32[4,512]{1,0:T(4,128)S(1)} %get-tuple-element.22.samples_ref), channel_id=1, source_target_pairs={{0,4},{4,0},{1,5},{5,1},{2,6},{6,2},{3,7},{7,3},{8,12},{12,8},{9,1... | collective-permute-start | bytes 24584 | tf_op jit(solution)/shard_map/ppermute | solution.py:43
  38.0 21.7 %copy-start.3 = (f32[73,73]{1,0:T(8,128)S(1)}, f32[73,73]{1,0:T(8,128)}, u32[]{:S(2)}) copy-start(f32[73,73]{1,0:T(8,128)} %matrix_ref.1) | copy-start | bytes 63952

commit v6 on v5

--- a/solution.py
+++ b/solution.py
@@ -138,6 +138,7 @@
     else:
         record_ref, lead_ref = rest
     count, rows, cols = velocity_shape
+    base = 2 * HISTORY
     ends = ((north_ref, south_ref), (west_ref, east_ref))
     tables = []
     for pair in ends:
@@ -145,12 +146,12 @@
         for table in range(3):
             for c in range(2):
                 for ref in pair:
-                    lines.append(at_time(lambda a: ref[c * count + a : c * count + a + 1], step, table))
+                    lines.append(at_time(lambda a: ref[base + c * count + a : base + c * count + a + 1], step, table))
         lines.append(jnp.zeros((4, cols), f32))
         tables.append(side_by_side(jnp.concatenate(lines, axis=0)))
 
     def tip(table, c, v, h):
-        ref, at = ends[1][h], (1 + v) * 2 * count + c * count
+        ref, at = ends[1][h], base + (1 + v) * 2 * count + c * count
         lane = slice(cols - 1, cols) if h == 0 else slice(0, 1)
         return at_time(lambda a: ref[at + a : at + a + 1, lane], step, table)
 
@@ -311,19 +312,6 @@
         else:
             out_ref[0, :, start : start + chunk] = placed[:rows]
             out_ref[1, :, start : start + chunk] = placed[rows:]
-
-
-def last_samples_kernel(tile, record_ref, lead_ref, west_ref, east_ref, sides_ref, next_ref, cells_ref, out_ref, point_ref):
-    moved = lead_ref.shape[1]
-    sides = sides_ref[0]
-    lead = chosen(sides[1:2], lead_ref[...], west_ref[...], east_ref[...])
-    sub = iota(lead.shape, 0)
-    lowered = jnp.where(sub == 0, sides[0:1] * tile[0], jnp.where(sub == 1, sides[1:2] * tile[1], 0.0))
-    record = jnp.concatenate([lead - lowered, record_ref[:, moved:]], axis=1)
-    corners = [[next_ref[2 * i + c : 2 * i + c + 1] for c in range(2)] for i in range(4)]
-    last = bilinear(corners, [record[0:1], record[1:2]], cells_ref[STEPS - 1, 0])
-    out_ref[...] = jnp.concatenate([record[2:3], last[0], record[3:4], last[1]], axis=0)
-    point_ref[...] = record[0:2]
 
 
 def place_samples_kernel(
@@ -424,21 +412,23 @@
     per_owner = 4 * slots // tile_count
     paired = 2 * per_owner == LANES
     groups = slots // LANES
+    lines = 2 * HISTORY
+    by_rows = history.reshape(2, HISTORY, groups, LANES).transpose(1, 2, 0, 3)
+    raw = by_rows.reshape(2 * groups * HISTORY, LANES)
+    past = by_rows[:, 0].reshape(lines, LANES)
+    sides = find_sides(leavers)
 
     def joined(*parts):
         return jnp.concatenate([part.reshape(-1, LANES) for part in parts], axis=0)
 
-    lines = 2 * HISTORY
-    north, south = exchanged(joined(velocity[:, :, tile_rows - 1]), joined(velocity[:, :, 0]), "ty")
+    north, south = exchanged(joined(past, velocity[:, :, tile_rows - 1]), joined(past, velocity[:, :, 0]), "ty")
+    past = chosen(sides[0, 0:1], past, north[:lines], south[:lines])
     west, east = exchanged(
-        joined(velocity[:, :, :, tile_cols - 1], north, south), joined(velocity[:, :, :, 0], north, south), "tx"
+        joined(past, velocity[:, :, :, tile_cols - 1], north[lines:], south[lines:]),
+        joined(past, velocity[:, :, :, 0], north[lines:], south[lines:]),
+        "tx",
     )
-    by_rows = history.reshape(2, HISTORY, groups, LANES).transpose(1, 2, 0, 3)
-    raw = by_rows.reshape(2 * groups * HISTORY, LANES)
-    sides = find_sides(leavers)
-    past = by_rows[:, 0].reshape(lines, LANES)
-    past = chosen(sides[0, 0:1], past, *exchanged(past, past, "ty"))
-    past = chosen(sides[0, 1:2], past, *exchanged(past, past, "tx"))
+    past = chosen(sides[0, 1:2], past, west[:lines], east[:lines])
     halo = (velocity, north, south, west, east)
     owner = owner.astype(f32)
     past = joined(past, owner, jnp.zeros((2, LANES), f32))
@@ -468,15 +458,13 @@
 
     placed, onehot = place(owner.reshape(1, slots), raw, past, 0)
     far_placed, far_onehot = place(far_owner, far_raw, far_past, moving)
-    samples, point = pl.pallas_call(
-        functools.partial(last_samples_kernel, (float(tile_rows), float(tile_cols))),
-        out_shape=[jax.ShapeDtypeStruct((2 * STEPS, slots), f32), jax.ShapeDtypeStruct((2, slots), f32)],
-        in_specs=whole(7),
-        out_specs=whole(2),
-        cost_estimate=cost(1000000, 100000),
-        compiler_params=grant,
-        name="last_samples",
-    )(record, lead, lead_west, lead_east, sides, first, cells)
+    lead = chosen(sides[0, 1:2], lead, lead_west, lead_east)
+    lowered = [sides[0, 0:1] * tile_rows, sides[0, 1:2] * tile_cols, jnp.zeros((6, 8 * MOST), f32)]
+    record = jnp.concatenate([lead - jnp.concatenate(lowered, axis=0), record[:, 8 * MOST :]], axis=1)
+    point = record[0:2]
+    corners = [[first[2 * i + c : 2 * i + c + 1] for c in range(2)] for i in range(4)]
+    last = bilinear(corners, [record[0:1], record[1:2]], cells[STEPS - 1, 0])
+    samples = jnp.concatenate([record[2:3], last[0], record[3:4], last[1]], axis=0)
     run_step(STEPS - 1, halo, point, first, cells)
     far_samples = swapped(samples)
     depth = 2 * rows + 8

time: 61.5 us -> 59.8 us (0.972)
  starting transfers between devices: 23.9 us -> 19.2 us
  waiting for transfers between devices: 4.16 us -> 8.63 us
  blocking collectives: 21.6 us -> 20.5 us
  local copies, waits for them, and re-layouts: 1.98 us -> 2.87 us
  other arithmetic: 0.95 us -> 0.33 us
    ppermute x6 -> x4, starting transfers between devices: 6.27 us -> 2.28 us  [exchanged(): lax.ppermute(up if up is down else jnp.where(even, up, down), places[axis...]
    ppermute x6 -> x4, starting transfers between devices: 11.8 us -> 7.82 us  [exchanged(): lax.ppermute(up if up is down else jnp.where(even, down, up), places[axis...]
    ppermute x3, starting transfers between devices: 5.8 us -> 9.05 us  [swapped(): return lax.ppermute(value, 'half', [(0, 1), (1, 0)])]
    ppermute x6 -> x4, waiting for transfers between devices: 2.97 us -> 5.63 us  [exchanged(): lax.ppermute(up if up is down else jnp.where(even, down, up), places[axis...]
    ppermute x3, waiting for transfers between devices: 1.18 us -> 2.99 us  [swapped(): return lax.ppermute(value, 'half', [(0, 1), (1, 0)])]
    all_to_all x1, blocking collectives: 21.6 us -> 20.5 us  [run(): lax.all_to_all(outgoing, ('ty', 'within'), split_axis=0, concat_axis=0, t...]
    slice x0 -> x4, local copies, waits for them, and re-layouts: none -> 0.79 us  [the longest x1 0.78 us: run(): velocity[:, :, 0]]
    select_n x2, other arithmetic: 0.79 us -> 0.03 us  [exchanged(): jnp.where(even, up, down)]
  transfers between devices with their start and end apart: 15 -> 11, of which waited for: 5 -> 3; matrix products, arithmetic and copies ran while one was open for 3% -> 2% of each run, Pallas kernels for 10% -> 9%
where the time goes in v6:
time: 59.8 us; the launch traced here: 59.5 us
  blocking collectives  20.5 us (34%)
  starting transfers between devices  19.2 us (32%)
  waiting for transfers between devices  8.63 us (14%)
  Pallas kernels  7.7 us (13%)
  local copies, waits for them, and re-layouts  2.87 us (5%)
    all_to_all x1, blocking collectives, run(): lax.all_to_all(outgoing, ('ty', 'within'), split_axis=0, concat_axis=0, t...  20.5 us
    ppermute x3, starting transfers between devices, swapped(): return lax.ppermute(value, 'half', [(0, 1), (1, 0)])  9.05 us
    ppermute x4, starting transfers between devices, exchanged(): lax.ppermute(up if up is down else jnp.where(even, down, up), places[axis...  7.82 us
    ppermute x4, waiting for transfers between devices, exchanged(): lax.ppermute(up if up is down else jnp.where(even, down, up), places[axis...  5.63 us
    ppermute x3, waiting for transfers between devices, swapped(): return lax.ppermute(value, 'half', [(0, 1), (1, 0)])  2.99 us
    pallas_call x2, Pallas kernels, place(): pl.pallas_call(functools.partial(place_history_kernel, per_owner, paired,...  2.36 us
    ppermute x4, starting transfers between devices, exchanged(): lax.ppermute(up if up is down else jnp.where(even, up, down), places[axis...  2.28 us
    pallas_call x1, Pallas kernels, run_step(): pl.pallas_call(functools.partial(inner_kernel, step, following), out_shap...  1.89 us
  transfers between devices with their start and end apart: 11, of which 3 were waited for; matrix products, arithmetic and copies ran while one was open for 2% of the time, Pallas kernels for 9%

profile of v6, /device:TPU:0, one launch (start us, length us, event | category | flops | bytes accessed | tf_op | source)
XLA Modules:
  0.0 59.5 jit_solution(1905368026654108151)
XLA Ops:
  0.0 0.8 %slice_reduce_fusion.3 = (f32[2,3,128]{2,1,0:T(4,128)S(1)}, f32[2,3,128]{2,1,0:T(4,128)S(1)}) fusion(f32[2,3,128,128]{3,2,1,0:T(8,128)} %velocity_ref.1), kind=kLoop, calls=%fused_computation.34 | loop fusion | bytes 12288 | tf_op jit(solution)/shard_map/slice | solution.py:424
  0.8 1.1 %bitcast_bitcast_fusion = f32[71,4,2,128]{3,2,0,1:T(2,128)S(1)} fusion(f32[2,71,512]{2,0,1:T(2,128)} %param.10), kind=kLoop, calls=%fused_computation.2 | loop fusion | bytes 581632 | tf_op jit(solution)/shard_map/transpose | solution.py:416
  2.0 0.1 reshape_squeeze.15
  2.1 0.6 collective-permute-start.1
  2.6 2.6 %collective-permute-start = (f32[148,128]{1,0:T(8,128)S(1)}, f32[148,128]{1,0:T(8,128)S(1)}, u32[]{:S(2)}, u32[]{:S(2)}) collective-permute-start(f32[148,128]{1,0:T(8,128)S(1)} %get-tuple-element.39), channel_id=1, source_target_pairs={{0,24},{8,16},{16,8},{24,0},{1,25},{9,17},{17,9},{25,1},{2,26},{10... | collective-permute-start | bytes 227336 | tf_op jit(solution)/shard_map/ppermute | solution.py:38
  5.2 0.1 copy.14
  5.3 0.2 reshape.125
  5.5 2.7 %collective-permute-start.10 = (f32[426,128]{1,0:T(8,128)S(1)}, f32[426,128]{1,0:T(8,128)S(1)}, u32[]{:S(2)}, u32[]{:S(2)}) collective-permute-start(f32[426,128]{1,0:T(8,128)S(1)} %reshape.125), channel_id=1, source_target_pairs={{0,4},{4,0},{1,5},{5,1},{2,6},{6,2},{3,7},{7,3},{8,12},{12,8},{9,1... | collective-permute-start | bytes 654344 | tf_op jit(solution)/shard_map/ppermute | solution.py:43
  8.1 0.6 find_sides.1
  8.8 0.4 slice_reduce_fusion
  9.3 1.6 %collective-permute-start.3 = (f32[160,128]{1,0:T(8,128)S(1)}, f32[160,128]{1,0:T(8,128)S(1)}, u32[]{:S(2)}, u32[]{:S(2)}) collective-permute-start(f32[160,128]{1,0:T(8,128)S(1)} %get-tuple-element.36), channel_id=1, source_target_pairs={{0,1},{1,0},{2,3},{3,2},{4,5},{5,4},{6,7},{7,6},{8,9},{9,8},{10,11... | collective-permute-start | bytes 245768 | tf_op jit(solution)/shard_map/ppermute | solution.py:37
  10.9 2.0 %collective-permute-start.2 = (f32[160,128]{1,0:T(8,128)S(1)}, f32[160,128]{1,0:T(8,128)S(1)}, u32[]{:S(2)}, u32[]{:S(2)}) collective-permute-start(f32[160,128]{1,0:T(8,128)S(1)} %get-tuple-element.37), channel_id=1, source_target_pairs={{0,7},{1,2},{2,1},{3,4},{4,3},{5,6},{6,5},{7,0},{8,15},{9,10},{10,... | collective-permute-start | bytes 245768 | tf_op jit(solution)/shard_map/ppermute | solution.py:38
  13.0 0.1 pad.11.clone
  13.0 0.1 pad.2.clone
  13.1 1.9 %sample_inner.1 = (f32[5,8,512]{2,1,0:T(8,128)S(1)}, bf16[5,2,128,512]{3,2,1,0:T(8,128)(2,1)S(1)}, bf16[5,2,128,512]{3,2,1,0:T(8,128)(2,1)S(1)}) custom-call(f32[2,3,128,128]{3,2,1,0:T(8,128)S(1)} %copy-done, s32[2,4,2,512]{3,2,1,0:T(2,128)S(1)} %copy-done.2), custom_call_target="tpu_custom_call" | custom-call | flops 671088640 | bytes 600000 | tf_op jit(solution)/shard_map/sample_inner/pallas_call | solution.py:208
  15.0 3.0 %collective-permute-done.2 = f32[160,128]{1,0:T(8,128)S(1)} collective-permute-done((f32[160,128]{1,0:T(8,128)S(1)}, f32[160,128]{1,0:T(8,128)S(1)}, u32[]{:S(2)}, u32[]{:S(2)}) %collective-permute-start.2) | collective-permute-done | bytes 81952 | tf_op jit(solution)/shard_map/ppermute | solution.py:38
  18.1 0.8 %sample_step.1 = (f32[8,512]{1,0:T(8,128)S(1)}, f32[8,128]{1,0:T(8,128)S(1)}, f32[8,512]{1,0:T(8,128)S(1)}) custom-call(f32[5,8,512]{2,1,0:T(8,128)S(1)} %get-tuple-element.15.part_ref, bf16[5,2,128,512]{3,2,1,0:T(8,128)(2,1)S(1)} %get-tuple-element.16.cols_ref, bf16[5,2,128,512]{3,2,1,0:T(8,128)(2,1)S(1)} %get-tuple-element.17.rows_ref, ...), custom_call_target="tpu_custom_call" | custom-call | flops 83886080 | bytes 600000 | tf_op jit(solution)/shard_map/sample_step/pallas_call | solution.py:225
  18.9 0.1 collective-permute-start.5
  19.0 0.6 %collective-permute-start.4 = (f32[8,128]{1,0:T(8,128)S(1)}, f32[8,128]{1,0:T(8,128)S(1)}, u32[]{:S(2)}, u32[]{:S(2)}) collective-permute-start(f32[8,128]{1,0:T(8,128)S(1)} %get-tuple-element.18), channel_id=1, source_target_pairs={{0,24},{8,16},{16,8},{24,0},{1,25},{9,17},{17,9},{25,1},{2,26},{10... | collective-permute-start | bytes 12296 | tf_op jit(solution)/shard_map/ppermute | solution.py:38
  19.6 0.1 maximum_maximum_fusion.past_ref
  19.7 6.0 %collective-permute-start.9 = (f32[148,128]{1,0:T(8,128)S(1)}, f32[148,128]{1,0:T(8,128)S(1)}, u32[]{:S(2)}, u32[]{:S(2)}) collective-permute-start(f32[148,128]{1,0:T(8,128)S(1)} %maximum_maximum_fusion.past_ref), channel_id=1, source_target_pairs={{0,4},{4,0},{1,5},{5,1},{2,6},{6,2},{3,7},{7,3},{8,12},{12,8},{9,1... | collective-permute-start | bytes 227336 | tf_op jit(solution)/shard_map/ppermute | solution.py:43
  25.7 0.1 collective-permute-start.7
  25.8 2.6 %collective-permute-start.6 = (f32[8,128]{1,0:T(8,128)S(1)}, f32[8,128]{1,0:T(8,128)S(1)}, u32[]{:S(2)}, u32[]{:S(2)}) collective-permute-start(f32[8,128]{1,0:T(8,128)S(1)} %select_select_fusion), channel_id=1, source_target_pairs={{0,7},{1,2},{2,1},{3,4},{4,3},{5,6},{6,5},{7,0},{8,15},{9,10},{10,... | collective-permute-start | bytes 12296 | tf_op jit(solution)/shard_map/ppermute | solution.py:38
  28.4 1.2 %place_history.2 = (f32[16,72,128]{2,1,0:T(8,128)S(1)}, bf16[512,1024]{1,0:T(8,128)(2,1)S(1)}) custom-call(s32[1]{0:T(128)} %bitcast.half_ref, f32[1,512]{1,0:T(1,128)S(1)} %get-tuple-element.47.owner_ref, f32[568,128]{1,0:T(8,128)S(1)} %bitcast.42, f32[148,128]{1,0:T(8,128)S(1)} %maximum_maximum_fusion.past_ref), custom_call_target="tpu_custom_call" | custom-call | flops 301989888 | bytes 3000000 | tf_op jit(solution)/shard_map/place_history/pallas_call | solution.py:449
  29.6 2.6 %collective-permute-done.6 = f32[8,128]{1,0:T(8,128)S(1)} collective-permute-done((f32[8,128]{1,0:T(8,128)S(1)}, f32[8,128]{1,0:T(8,128)S(1)}, u32[]{:S(2)}, u32[]{:S(2)}) %collective-permute-start.6) | collective-permute-done | bytes 4128 | tf_op jit(solution)/shard_map/ppermute | solution.py:38
  32.2 0.1 maximum_subtract_fusion
  32.3 0.4 collective-permute-start.8
  32.7 1.2 %place_history.3 = (f32[16,72,128]{2,1,0:T(8,128)S(1)}, bf16[512,1024]{1,0:T(8,128)(2,1)S(1)}) custom-call(s32[1]{0:T(128)} %bitcast.half_ref, f32[1,512]{1,0:T(1,128)S(1)} %bitcast.43, f32[426,128]{1,0:T(8,128)S(1)} %collective-permute-done.10.history_ref, f32[148,128]{1,0:T(8,128)S(1)} %collective-permute-done.9.past_ref), custom_call_target="tpu_custom_call" | custom-call | flops 301989888 | bytes 3000000 | tf_op jit(solution)/shard_map/place_history/pallas_call | solution.py:449
  33.9 3.0 %collective-permute-done.8.far_samples_ref = f32[4,512]{1,0:T(4,128)S(1)} collective-permute-done((f32[4,512]{1,0:T(4,128)S(1)}, f32[4,512]{1,0:T(4,128)S(1)}, u32[]{:S(2)}, u32[]{:S(2)}) %collective-permute-start.8) | collective-permute-done | bytes 8224 | tf_op jit(solution)/shard_map/ppermute | solution.py:43
  36.9 0.6 place_samples.1
  37.5 20.5 %all_to_all.5.arrived_ref = f32[16,152,128]{2,1,0:T(8,128)S(1)} all-to-all(f32[16,152,128]{2,1,0:T(8,128)S(1)} %place_samples.1), channel_id=1, replica_groups=mesh['ty'=4,'half'=2,'within'=4] {'ty','within'}, dimensions={0} | all-to-all | bytes 2490368 | tf_op jit(solution)/shard_map/all_to_all | solution.py:482
  58.0 1.5 %filter_series.1 = f32[73,4,8,128]{3,2,1,0:T(8,128)} custom-call(f32[73,73]{1,0:T(8,128)S(1)} %copy-done.3, f32[16,152,128]{2,1,0:T(8,128)S(1)} %all_to_all.5.arrived_ref), custom_call_target="tpu_custom_call" | custom-call | flops 157286400 | bytes 3000000 | tf_op jit(solution)/shard_map/filter_series/pallas_call | solution.py:492
  (47 shorter events, 0.3 us)
Async XLA Ops:
  0.8 7.4 %copy-start.5 = (s32[1,8]{1,0:T(1,128)S(1)}, s32[1,8]{1,0:T(1,128)}, u32[]{:S(2)}) copy-start(s32[1,8]{1,0:T(1,128)} %leavers_ref.1) | copy-start | bytes 100
  0.8 7.9 %copy-start.6 = (s32[512,1]{0,1:T(1,128)S(1)}, s32[512,1]{0,1:T(1,128)}, u32[]{:S(2)}) copy-start(s32[512,1]{0,1:T(1,128)} %param.12) | copy-start | bytes 6148
  0.8 7.9 %copy-start = (f32[2,3,128,128]{3,2,1,0:T(8,128)S(1)}, f32[2,3,128,128]{3,2,1,0:T(8,128)}, u32[]{:S(2)}) copy-start(f32[2,3,128,128]{3,2,1,0:T(8,128)} %velocity_ref.1) | copy-start | bytes 1179652
  2.1 7.1 %collective-permute-start.1 = (f32[148,128]{1,0:T(8,128)S(1)}, f32[148,128]{1,0:T(8,128)S(1)}, u32[]{:S(2)}, u32[]{:S(2)}) collective-permute-start(f32[148,128]{1,0:T(8,128)S(1)} %get-tuple-element.38), channel_id=1, source_target_pairs={{0,8},{8,0},{16,24},{24,16},{1,9},{9,1},{17,25},{25,17},{2,10},{10... | collective-permute-start | bytes 227336 | tf_op jit(solution)/shard_map/ppermute | solution.py:37
  2.6 6.6 %collective-permute-start = (f32[148,128]{1,0:T(8,128)S(1)}, f32[148,128]{1,0:T(8,128)S(1)}, u32[]{:S(2)}, u32[]{:S(2)}) collective-permute-start(f32[148,128]{1,0:T(8,128)S(1)} %get-tuple-element.39), channel_id=1, source_target_pairs={{0,24},{8,16},{16,8},{24,0},{1,25},{9,17},{17,9},{25,1},{2,26},{10... | collective-permute-start | bytes 227336 | tf_op jit(solution)/shard_map/ppermute | solution.py:38
  5.2 7.9 %copy-start.2 = (s32[2,4,2,512]{3,2,1,0:T(2,128)S(1)}, s32[2,4,2,512]{3,2,1,0:T(2,128)}, u32[]{:S(2)}) copy-start(s32[2,4,2,512]{3,2,1,0:T(2,128)} %cells_ref.3) | copy-start | bytes 98308
  5.5 27.3 %collective-permute-start.10 = (f32[426,128]{1,0:T(8,128)S(1)}, f32[426,128]{1,0:T(8,128)S(1)}, u32[]{:S(2)}, u32[]{:S(2)}) collective-permute-start(f32[426,128]{1,0:T(8,128)S(1)} %reshape.125), channel_id=1, source_target_pairs={{0,4},{4,0},{1,5},{5,1},{2,6},{6,2},{3,7},{7,3},{8,12},{12,8},{9,1... | collective-permute-start | bytes 654344 | tf_op jit(solution)/shard_map/ppermute | solution.py:43
  9.3 5.7 %collective-permute-start.3 = (f32[160,128]{1,0:T(8,128)S(1)}, f32[160,128]{1,0:T(8,128)S(1)}, u32[]{:S(2)}, u32[]{:S(2)}) collective-permute-start(f32[160,128]{1,0:T(8,128)S(1)} %get-tuple-element.36), channel_id=1, source_target_pairs={{0,1},{1,0},{2,3},{3,2},{4,5},{5,4},{6,7},{7,6},{8,9},{9,8},{10,11... | collective-permute-start | bytes 245768 | tf_op jit(solution)/shard_map/ppermute | solution.py:37
  10.9 7.1 %collective-permute-start.2 = (f32[160,128]{1,0:T(8,128)S(1)}, f32[160,128]{1,0:T(8,128)S(1)}, u32[]{:S(2)}, u32[]{:S(2)}) collective-permute-start(f32[160,128]{1,0:T(8,128)S(1)} %get-tuple-element.37), channel_id=1, source_target_pairs={{0,7},{1,2},{2,1},{3,4},{4,3},{5,6},{6,5},{7,0},{8,15},{9,10},{10,... | collective-permute-start | bytes 245768 | tf_op jit(solution)/shard_map/ppermute | solution.py:38
  13.1 5.0 %copy-start.4 = (f32[2,512]{1,0:T(2,128)S(1)}, f32[2,512]{1,0:T(2,128)}, u32[]{:S(2)}) copy-start(f32[2,512]{1,0:T(2,128)} %point_ref.1) | copy-start | bytes 12292
  18.1 10.3 %copy-start.1 = (f32[2,71,512]{2,0,1:T(2,128)S(1)}, f32[2,71,512]{2,0,1:T(2,128)}, u32[]{:S(2)}) copy-start(f32[2,71,512]{2,0,1:T(2,128)} %param.10) | copy-start | bytes 872452
  18.9 6.8 %collective-permute-start.5 = (f32[8,128]{1,0:T(8,128)S(1)}, f32[8,128]{1,0:T(8,128)S(1)}, u32[]{:S(2)}, u32[]{:S(2)}) collective-permute-start(f32[8,128]{1,0:T(8,128)S(1)} %get-tuple-element.18), channel_id=1, source_target_pairs={{0,8},{8,0},{16,24},{24,16},{1,9},{9,1},{17,25},{25,17},{2,10},{10... | collective-permute-start | bytes 12296 | tf_op jit(solution)/shard_map/ppermute | solution.py:37
  19.0 6.7 %collective-permute-start.4 = (f32[8,128]{1,0:T(8,128)S(1)}, f32[8,128]{1,0:T(8,128)S(1)}, u32[]{:S(2)}, u32[]{:S(2)}) collective-permute-start(f32[8,128]{1,0:T(8,128)S(1)} %get-tuple-element.18), channel_id=1, source_target_pairs={{0,24},{8,16},{16,8},{24,0},{1,25},{9,17},{17,9},{25,1},{2,26},{10... | collective-permute-start | bytes 12296 | tf_op jit(solution)/shard_map/ppermute | solution.py:38
  19.7 13.0 %collective-permute-start.9 = (f32[148,128]{1,0:T(8,128)S(1)}, f32[148,128]{1,0:T(8,128)S(1)}, u32[]{:S(2)}, u32[]{:S(2)}) collective-permute-start(f32[148,128]{1,0:T(8,128)S(1)} %maximum_maximum_fusion.past_ref), channel_id=1, source_target_pairs={{0,4},{4,0},{1,5},{5,1},{2,6},{6,2},{3,7},{7,3},{8,12},{12,8},{9,1... | collective-permute-start | bytes 227336 | tf_op jit(solution)/shard_map/ppermute | solution.py:43
  25.7 3.8 %collective-permute-start.7 = (f32[8,128]{1,0:T(8,128)S(1)}, f32[8,128]{1,0:T(8,128)S(1)}, u32[]{:S(2)}, u32[]{:S(2)}) collective-permute-start(f32[8,128]{1,0:T(8,128)S(1)} %select_select_fusion), channel_id=1, source_target_pairs={{0,1},{1,0},{2,3},{3,2},{4,5},{5,4},{6,7},{7,6},{8,9},{9,8},{10,11... | collective-permute-start | bytes 12296 | tf_op jit(solution)/shard_map/ppermute | solution.py:37
  25.8 6.4 %collective-permute-start.6 = (f32[8,128]{1,0:T(8,128)S(1)}, f32[8,128]{1,0:T(8,128)S(1)}, u32[]{:S(2)}, u32[]{:S(2)}) collective-permute-start(f32[8,128]{1,0:T(8,128)S(1)} %select_select_fusion), channel_id=1, source_target_pairs={{0,7},{1,2},{2,1},{3,4},{4,3},{5,6},{6,5},{7,0},{8,15},{9,10},{10,... | collective-permute-start | bytes 12296 | tf_op jit(solution)/shard_map/ppermute | solution.py:38
  32.3 4.6 %collective-permute-start.8 = (f32[4,512]{1,0:T(4,128)S(1)}, f32[4,512]{1,0:T(4,128)S(1)}, u32[]{:S(2)}, u32[]{:S(2)}) collective-permute-start(f32[4,512]{1,0:T(4,128)S(1)} %fusion.7.samples_ref), channel_id=1, source_target_pairs={{0,4},{4,0},{1,5},{5,1},{2,6},{6,2},{3,7},{7,3},{8,12},{12,8},{9,1... | collective-permute-start | bytes 24584 | tf_op jit(solution)/shard_map/ppermute | solution.py:43
  37.5 20.5 %copy-start.3 = (f32[73,73]{1,0:T(8,128)S(1)}, f32[73,73]{1,0:T(8,128)}, u32[]{:S(2)}) copy-start(f32[73,73]{1,0:T(8,128)} %matrix_ref.1) | copy-start | bytes 63952

commit v7 on v6

--- a/solution.py
+++ b/solution.py
@@ -269,19 +269,24 @@
     return left, right
 
 
-def targets_of(owner_row, half, within, width):
+def columns_kernel(width, owner_ref, out_ref):
+    owner_row = owner_ref[...]
     slots = owner_row.shape[1]
+    owner = jnp.broadcast_to(owner_row, (LANES, slots)).T[:, 0:1]
+    before = iota((slots, slots), 0) < iota((slots, slots), 1)
+    rank = jnp.sum(picked((owner == owner_row) & before), axis=0, keepdims=True)
+    out_ref[...] = owner_row * width + rank
+
+
+def targets_of(columns, half, within, width):
+    slots = columns.shape[1]
     half = half.astype(f32)
-    column = jnp.floor((owner_row + 0.5) / within)
+    owner = jnp.floor((columns + 0.5) / width)
+    column = jnp.floor((owner + 0.5) / within)
     line = jnp.floor((column + 0.5) * 0.5)
-    block = line * within + (owner_row - column * within)
-    base = jnp.where(column - 2.0 * line == half, block * width, -1.0e6)
-    row = iota((LANES, slots), 0)
-    turned = jnp.where(row == 0, owner_row, base).T
-    owner, base = turned[:, 0:1], turned[:, 1:2]
-    before = iota((slots, slots), 1) < iota((slots, slots), 0)
-    rank = jnp.sum(picked((owner == owner_row) & before), axis=1, keepdims=True)
-    return (base + rank).astype(jnp.int32)
+    block = line * within + (owner - column * within)
+    target = jnp.where(column - 2.0 * line == half, block * width + (columns - owner * width), -1.0)
+    return jnp.broadcast_to(target, (LANES, slots)).T[:, 0:1].astype(jnp.int32)
 
 
 def place_history_kernel(width, paired, within, skipped, half_ref, owner_ref, history_ref, past_ref, out_ref, onehot_ref):
@@ -430,7 +435,15 @@
     )
     past = chosen(sides[0, 1:2], past, west[:lines], east[:lines])
     halo = (velocity, north, south, west, east)
-    owner = owner.astype(f32)
+    owner = pl.pallas_call(
+        functools.partial(columns_kernel, per_owner),
+        out_shape=jax.ShapeDtypeStruct((1, slots), f32),
+        in_specs=whole(1),
+        out_specs=whole(1)[0],
+        cost_estimate=cost(1000000, 10000),
+        compiler_params=grant,
+        name="find_columns",
+    )(owner.astype(f32).reshape(1, slots))
     past = joined(past, owner, jnp.zeros((2, LANES), f32))
     moving = 8 * MOST // LANES
     far_raw = swapped(by_rows[:, moving:].reshape(2 * (groups - moving) * HISTORY, LANES))

time: 59.8 us -> 59.8 us (level)
  transfers between devices with their start and end apart: 11 -> 11, of which waited for: 3 -> 4; matrix products, arithmetic and copies ran while one was open for 2% -> 2% of each run, Pallas kernels for 9% -> 9%
where the time goes in v7:
time: 59.8 us; the launch traced here: 59.5 us
  blocking collectives  20.5 us (34%)
  starting transfers between devices  19.2 us (32%)
  waiting for transfers between devices  8.85 us (15%)
  Pallas kernels  7.47 us (12%)
  local copies, waits for them, and re-layouts  2.87 us (5%)
    all_to_all x1, blocking collectives, run(): lax.all_to_all(outgoing, ('ty', 'within'), split_axis=0, concat_axis=0, t...  20.5 us
    ppermute x3, starting transfers between devices, swapped(): return lax.ppermute(value, 'half', [(0, 1), (1, 0)])  9.06 us
    ppermute x4, starting transfers between devices, exchanged(): lax.ppermute(up if up is down else jnp.where(even, down, up), places[axis...  7.82 us
    ppermute x4, waiting for transfers between devices, exchanged(): lax.ppermute(up if up is down else jnp.where(even, down, up), places[axis...  5.54 us
    ppermute x3, waiting for transfers between devices, swapped(): return lax.ppermute(value, 'half', [(0, 1), (1, 0)])  3.23 us
    ppermute x4, starting transfers between devices, exchanged(): lax.ppermute(up if up is down else jnp.where(even, up, down), places[axis...  2.28 us
    pallas_call x1, Pallas kernels, run_step(): pl.pallas_call(functools.partial(inner_kernel, step, following), out_shap...  1.9 us
    pallas_call x2, Pallas kernels, place(): pl.pallas_call(functools.partial(place_history_kernel, per_owner, paired,...  1.89 us
  transfers between devices with their start and end apart: 11, of which 4 were waited for; matrix products, arithmetic and copies ran while one was open for 2% of the time, Pallas kernels for 9%

profile of v7, /device:TPU:0, one launch (start us, length us, event | category | flops | bytes accessed | tf_op | source)
XLA Modules:
  0.0 59.5 jit_solution(2982231099895112133)
XLA Ops:
  0.0 0.8 %slice_reduce_fusion.3 = (f32[2,3,128]{2,1,0:T(4,128)S(1)}, f32[2,3,128]{2,1,0:T(4,128)S(1)}) fusion(f32[2,3,128,128]{3,2,1,0:T(8,128)} %velocity_ref.1), kind=kLoop, calls=%fused_computation.34 | loop fusion | bytes 12288 | tf_op jit(solution)/shard_map/slice | solution.py:429
  0.8 1.1 %bitcast_bitcast_fusion = f32[71,4,2,128]{3,2,0,1:T(2,128)S(1)} fusion(f32[2,71,512]{2,0,1:T(2,128)} %param.10), kind=kLoop, calls=%fused_computation.2 | loop fusion | bytes 581632 | tf_op jit(solution)/shard_map/transpose | solution.py:421
  2.1 0.6 collective-permute-start.1
  2.6 2.6 %collective-permute-start = (f32[148,128]{1,0:T(8,128)S(1)}, f32[148,128]{1,0:T(8,128)S(1)}, u32[]{:S(2)}, u32[]{:S(2)}) collective-permute-start(f32[148,128]{1,0:T(8,128)S(1)} %get-tuple-element.39), channel_id=1, source_target_pairs={{0,24},{8,16},{16,8},{24,0},{1,25},{9,17},{17,9},{25,1},{2,26},{10... | collective-permute-start | bytes 227336 | tf_op jit(solution)/shard_map/ppermute | solution.py:38
  5.2 0.1 copy.14
  5.3 0.2 reshape.125
  5.5 2.7 %collective-permute-start.10 = (f32[426,128]{1,0:T(8,128)S(1)}, f32[426,128]{1,0:T(8,128)S(1)}, u32[]{:S(2)}, u32[]{:S(2)}) collective-permute-start(f32[426,128]{1,0:T(8,128)S(1)} %reshape.125), channel_id=1, source_target_pairs={{0,4},{4,0},{1,5},{5,1},{2,6},{6,2},{3,7},{7,3},{8,12},{12,8},{9,1... | collective-permute-start | bytes 654344 | tf_op jit(solution)/shard_map/ppermute | solution.py:43
  8.1 0.6 find_sides.1
  8.7 0.4 slice_reduce_fusion
  9.3 1.6 %collective-permute-start.3 = (f32[160,128]{1,0:T(8,128)S(1)}, f32[160,128]{1,0:T(8,128)S(1)}, u32[]{:S(2)}, u32[]{:S(2)}) collective-permute-start(f32[160,128]{1,0:T(8,128)S(1)} %get-tuple-element.36), channel_id=1, source_target_pairs={{0,1},{1,0},{2,3},{3,2},{4,5},{5,4},{6,7},{7,6},{8,9},{9,8},{10,11... | collective-permute-start | bytes 245768 | tf_op jit(solution)/shard_map/ppermute | solution.py:37
  10.9 2.0 %collective-permute-start.2 = (f32[160,128]{1,0:T(8,128)S(1)}, f32[160,128]{1,0:T(8,128)S(1)}, u32[]{:S(2)}, u32[]{:S(2)}) collective-permute-start(f32[160,128]{1,0:T(8,128)S(1)} %get-tuple-element.37), channel_id=1, source_target_pairs={{0,7},{1,2},{2,1},{3,4},{4,3},{5,6},{6,5},{7,0},{8,15},{9,10},{10,... | collective-permute-start | bytes 245768 | tf_op jit(solution)/shard_map/ppermute | solution.py:38
  12.9 0.1 pad.11.clone
  13.0 0.1 pad.2.clone
  13.1 0.2 find_columns.1.owner_ref
  13.4 1.9 %sample_inner.1 = (f32[5,8,512]{2,1,0:T(8,128)S(1)}, bf16[5,2,128,512]{3,2,1,0:T(8,128)(2,1)S(1)}, bf16[5,2,128,512]{3,2,1,0:T(8,128)(2,1)S(1)}) custom-call(f32[2,3,128,128]{3,2,1,0:T(8,128)S(1)} %copy-done, s32[2,4,2,512]{3,2,1,0:T(2,128)S(1)} %copy-done.2), custom_call_target="tpu_custom_call" | custom-call | flops 671088640 | bytes 600000 | tf_op jit(solution)/shard_map/sample_inner/pallas_call | solution.py:208
  15.3 2.8 %collective-permute-done.2 = f32[160,128]{1,0:T(8,128)S(1)} collective-permute-done((f32[160,128]{1,0:T(8,128)S(1)}, f32[160,128]{1,0:T(8,128)S(1)}, u32[]{:S(2)}, u32[]{:S(2)}) %collective-permute-start.2) | collective-permute-done | bytes 81952 | tf_op jit(solution)/shard_map/ppermute | solution.py:38
  18.1 0.8 %sample_step.1 = (f32[8,512]{1,0:T(8,128)S(1)}, f32[8,128]{1,0:T(8,128)S(1)}, f32[8,512]{1,0:T(8,128)S(1)}) custom-call(f32[5,8,512]{2,1,0:T(8,128)S(1)} %get-tuple-element.15.part_ref, bf16[5,2,128,512]{3,2,1,0:T(8,128)(2,1)S(1)} %get-tuple-element.16.cols_ref, bf16[5,2,128,512]{3,2,1,0:T(8,128)(2,1)S(1)} %get-tuple-element.17.rows_ref, ...), custom_call_target="tpu_custom_call" | custom-call | flops 83886080 | bytes 600000 | tf_op jit(solution)/shard_map/sample_step/pallas_call | solution.py:225
  18.9 0.1 collective-permute-start.5
  19.0 0.6 %collective-permute-start.4 = (f32[8,128]{1,0:T(8,128)S(1)}, f32[8,128]{1,0:T(8,128)S(1)}, u32[]{:S(2)}, u32[]{:S(2)}) collective-permute-start(f32[8,128]{1,0:T(8,128)S(1)} %get-tuple-element.18), channel_id=1, source_target_pairs={{0,24},{8,16},{16,8},{24,0},{1,25},{9,17},{17,9},{25,1},{2,26},{10... | collective-permute-start | bytes 12296 | tf_op jit(solution)/shard_map/ppermute | solution.py:38
  19.6 0.1 maximum_maximum_fusion.past_ref
  19.7 6.0 %collective-permute-start.9 = (f32[148,128]{1,0:T(8,128)S(1)}, f32[148,128]{1,0:T(8,128)S(1)}, u32[]{:S(2)}, u32[]{:S(2)}) collective-permute-start(f32[148,128]{1,0:T(8,128)S(1)} %maximum_maximum_fusion.past_ref), channel_id=1, source_target_pairs={{0,4},{4,0},{1,5},{5,1},{2,6},{6,2},{3,7},{7,3},{8,12},{12,8},{9,1... | collective-permute-start | bytes 227336 | tf_op jit(solution)/shard_map/ppermute | solution.py:43
  25.7 0.1 collective-permute-start.7
  25.8 2.6 %collective-permute-start.6 = (f32[8,128]{1,0:T(8,128)S(1)}, f32[8,128]{1,0:T(8,128)S(1)}, u32[]{:S(2)}, u32[]{:S(2)}) collective-permute-start(f32[8,128]{1,0:T(8,128)S(1)} %select_select_fusion), channel_id=1, source_target_pairs={{0,7},{1,2},{2,1},{3,4},{4,3},{5,6},{6,5},{7,0},{8,15},{9,10},{10,... | collective-permute-start | bytes 12296 | tf_op jit(solution)/shard_map/ppermute | solution.py:38
  28.3 0.9 %place_history.2 = (f32[16,72,128]{2,1,0:T(8,128)S(1)}, bf16[512,1024]{1,0:T(8,128)(2,1)S(1)}) custom-call(s32[1]{0:T(128)} %bitcast.half_ref, f32[1,512]{1,0:T(1,128)S(1)} %find_columns.1.owner_ref, f32[568,128]{1,0:T(8,128)S(1)} %bitcast.42, f32[148,128]{1,0:T(8,128)S(1)} %maximum_maximum_fusion.past_ref), custom_call_target="tpu_custom_call" | custom-call | flops 301989888 | bytes 3000000 | tf_op jit(solution)/shard_map/place_history/pallas_call | solution.py:462
  29.4 2.8 %collective-permute-done.6 = f32[8,128]{1,0:T(8,128)S(1)} collective-permute-done((f32[8,128]{1,0:T(8,128)S(1)}, f32[8,128]{1,0:T(8,128)S(1)}, u32[]{:S(2)}, u32[]{:S(2)}) %collective-permute-start.6) | collective-permute-done | bytes 4128 | tf_op jit(solution)/shard_map/ppermute | solution.py:38
  32.2 0.1 maximum_subtract_fusion
  32.3 0.4 collective-permute-start.8
  32.7 0.9 %place_history.3 = (f32[16,72,128]{2,1,0:T(8,128)S(1)}, bf16[512,1024]{1,0:T(8,128)(2,1)S(1)}) custom-call(s32[1]{0:T(128)} %bitcast.half_ref, f32[1,512]{1,0:T(1,128)S(1)} %bitcast.44, f32[426,128]{1,0:T(8,128)S(1)} %collective-permute-done.10.history_ref, f32[148,128]{1,0:T(8,128)S(1)} %collective-permute-done.9.past_ref), custom_call_target="tpu_custom_call" | custom-call | flops 301989888 | bytes 3000000 | tf_op jit(solution)/shard_map/place_history/pallas_call | solution.py:462
  33.7 3.2 %collective-permute-done.8.far_samples_ref = f32[4,512]{1,0:T(4,128)S(1)} collective-permute-done((f32[4,512]{1,0:T(4,128)S(1)}, f32[4,512]{1,0:T(4,128)S(1)}, u32[]{:S(2)}, u32[]{:S(2)}) %collective-permute-start.8) | collective-permute-done | bytes 8224 | tf_op jit(solution)/shard_map/ppermute | solution.py:43
  36.9 0.6 place_samples.1
  37.5 20.5 %all_to_all.5.arrived_ref = f32[16,152,128]{2,1,0:T(8,128)S(1)} all-to-all(f32[16,152,128]{2,1,0:T(8,128)S(1)} %place_samples.1), channel_id=1, replica_groups=mesh['ty'=4,'half'=2,'within'=4] {'ty','within'}, dimensions={0} | all-to-all | bytes 2490368 | tf_op jit(solution)/shard_map/all_to_all | solution.py:495
  58.0 1.5 %filter_series.1 = f32[73,4,8,128]{3,2,1,0:T(8,128)} custom-call(f32[73,73]{1,0:T(8,128)S(1)} %copy-done.3, f32[16,152,128]{2,1,0:T(8,128)S(1)} %all_to_all.5.arrived_ref), custom_call_target="tpu_custom_call" | custom-call | flops 157286400 | bytes 3000000 | tf_op jit(solution)/shard_map/filter_series/pallas_call | solution.py:505
  (48 shorter events, 0.4 us)
Async XLA Ops:
  0.8 7.4 %copy-start.5 = (s32[1,8]{1,0:T(1,128)S(1)}, s32[1,8]{1,0:T(1,128)}, u32[]{:S(2)}) copy-start(s32[1,8]{1,0:T(1,128)} %leavers_ref.1) | copy-start | bytes 100
  0.8 7.9 %copy-start = (f32[2,3,128,128]{3,2,1,0:T(8,128)S(1)}, f32[2,3,128,128]{3,2,1,0:T(8,128)}, u32[]{:S(2)}) copy-start(f32[2,3,128,128]{3,2,1,0:T(8,128)} %velocity_ref.1) | copy-start | bytes 1179652
  2.1 7.1 %collective-permute-start.1 = (f32[148,128]{1,0:T(8,128)S(1)}, f32[148,128]{1,0:T(8,128)S(1)}, u32[]{:S(2)}, u32[]{:S(2)}) collective-permute-start(f32[148,128]{1,0:T(8,128)S(1)} %get-tuple-element.38), channel_id=1, source_target_pairs={{0,8},{8,0},{16,24},{24,16},{1,9},{9,1},{17,25},{25,17},{2,10},{10... | collective-permute-start | bytes 227336 | tf_op jit(solution)/shard_map/ppermute | solution.py:37
  2.6 6.6 %collective-permute-start = (f32[148,128]{1,0:T(8,128)S(1)}, f32[148,128]{1,0:T(8,128)S(1)}, u32[]{:S(2)}, u32[]{:S(2)}) collective-permute-start(f32[148,128]{1,0:T(8,128)S(1)} %get-tuple-element.39), channel_id=1, source_target_pairs={{0,24},{8,16},{16,8},{24,0},{1,25},{9,17},{17,9},{25,1},{2,26},{10... | collective-permute-start | bytes 227336 | tf_op jit(solution)/shard_map/ppermute | solution.py:38
  5.2 7.7 %copy-start.6 = (s32[512,1]{0,1:T(1,128)S(1)}, s32[512,1]{0,1:T(1,128)}, u32[]{:S(2)}) copy-start(s32[512,1]{0,1:T(1,128)} %param.12) | copy-start | bytes 6148
  5.2 8.1 %copy-start.2 = (s32[2,4,2,512]{3,2,1,0:T(2,128)S(1)}, s32[2,4,2,512]{3,2,1,0:T(2,128)}, u32[]{:S(2)}) copy-start(s32[2,4,2,512]{3,2,1,0:T(2,128)} %cells_ref.3) | copy-start | bytes 98308
  5.5 27.3 %collective-permute-start.10 = (f32[426,128]{1,0:T(8,128)S(1)}, f32[426,128]{1,0:T(8,128)S(1)}, u32[]{:S(2)}, u32[]{:S(2)}) collective-permute-start(f32[426,128]{1,0:T(8,128)S(1)} %reshape.125), channel_id=1, source_target_pairs={{0,4},{4,0},{1,5},{5,1},{2,6},{6,2},{3,7},{7,3},{8,12},{12,8},{9,1... | collective-permute-start | bytes 654344 | tf_op jit(solution)/shard_map/ppermute | solution.py:43
  9.3 6.0 %collective-permute-start.3 = (f32[160,128]{1,0:T(8,128)S(1)}, f32[160,128]{1,0:T(8,128)S(1)}, u32[]{:S(2)}, u32[]{:S(2)}) collective-permute-start(f32[160,128]{1,0:T(8,128)S(1)} %get-tuple-element.36), channel_id=1, source_target_pairs={{0,1},{1,0},{2,3},{3,2},{4,5},{5,4},{6,7},{7,6},{8,9},{9,8},{10,11... | collective-permute-start | bytes 245768 | tf_op jit(solution)/shard_map/ppermute | solution.py:37
  10.9 7.1 %collective-permute-start.2 = (f32[160,128]{1,0:T(8,128)S(1)}, f32[160,128]{1,0:T(8,128)S(1)}, u32[]{:S(2)}, u32[]{:S(2)}) collective-permute-start(f32[160,128]{1,0:T(8,128)S(1)} %get-tuple-element.37), channel_id=1, source_target_pairs={{0,7},{1,2},{2,1},{3,4},{4,3},{5,6},{6,5},{7,0},{8,15},{9,10},{10,... | collective-permute-start | bytes 245768 | tf_op jit(solution)/shard_map/ppermute | solution.py:38
  13.3 4.7 %copy-start.4 = (f32[2,512]{1,0:T(2,128)S(1)}, f32[2,512]{1,0:T(2,128)}, u32[]{:S(2)}) copy-start(f32[2,512]{1,0:T(2,128)} %point_ref.1) | copy-start | bytes 12292
  18.1 10.3 %copy-start.1 = (f32[2,71,512]{2,0,1:T(2,128)S(1)}, f32[2,71,512]{2,0,1:T(2,128)}, u32[]{:S(2)}) copy-start(f32[2,71,512]{2,0,1:T(2,128)} %param.10) | copy-start | bytes 872452
  18.9 6.8 %collective-permute-start.5 = (f32[8,128]{1,0:T(8,128)S(1)}, f32[8,128]{1,0:T(8,128)S(1)}, u32[]{:S(2)}, u32[]{:S(2)}) collective-permute-start(f32[8,128]{1,0:T(8,128)S(1)} %get-tuple-element.18), channel_id=1, source_target_pairs={{0,8},{8,0},{16,24},{24,16},{1,9},{9,1},{17,25},{25,17},{2,10},{10... | collective-permute-start | bytes 12296 | tf_op jit(solution)/shard_map/ppermute | solution.py:37
  19.0 6.7 %collective-permute-start.4 = (f32[8,128]{1,0:T(8,128)S(1)}, f32[8,128]{1,0:T(8,128)S(1)}, u32[]{:S(2)}, u32[]{:S(2)}) collective-permute-start(f32[8,128]{1,0:T(8,128)S(1)} %get-tuple-element.18), channel_id=1, source_target_pairs={{0,24},{8,16},{16,8},{24,0},{1,25},{9,17},{17,9},{25,1},{2,26},{10... | collective-permute-start | bytes 12296 | tf_op jit(solution)/shard_map/ppermute | solution.py:38
  19.7 13.0 %collective-permute-start.9 = (f32[148,128]{1,0:T(8,128)S(1)}, f32[148,128]{1,0:T(8,128)S(1)}, u32[]{:S(2)}, u32[]{:S(2)}) collective-permute-start(f32[148,128]{1,0:T(8,128)S(1)} %maximum_maximum_fusion.past_ref), channel_id=1, source_target_pairs={{0,4},{4,0},{1,5},{5,1},{2,6},{6,2},{3,7},{7,3},{8,12},{12,8},{9,1... | collective-permute-start | bytes 227336 | tf_op jit(solution)/shard_map/ppermute | solution.py:43
  25.7 3.7 %collective-permute-start.7 = (f32[8,128]{1,0:T(8,128)S(1)}, f32[8,128]{1,0:T(8,128)S(1)}, u32[]{:S(2)}, u32[]{:S(2)}) collective-permute-start(f32[8,128]{1,0:T(8,128)S(1)} %select_select_fusion), channel_id=1, source_target_pairs={{0,1},{1,0},{2,3},{3,2},{4,5},{5,4},{6,7},{7,6},{8,9},{9,8},{10,11... | collective-permute-start | bytes 12296 | tf_op jit(solution)/shard_map/ppermute | solution.py:37
  25.8 6.4 %collective-permute-start.6 = (f32[8,128]{1,0:T(8,128)S(1)}, f32[8,128]{1,0:T(8,128)S(1)}, u32[]{:S(2)}, u32[]{:S(2)}) collective-permute-start(f32[8,128]{1,0:T(8,128)S(1)} %select_select_fusion), channel_id=1, source_target_pairs={{0,7},{1,2},{2,1},{3,4},{4,3},{5,6},{6,5},{7,0},{8,15},{9,10},{10,... | collective-permute-start | bytes 12296 | tf_op jit(solution)/shard_map/ppermute | solution.py:38
  32.3 4.6 %collective-permute-start.8 = (f32[4,512]{1,0:T(4,128)S(1)}, f32[4,512]{1,0:T(4,128)S(1)}, u32[]{:S(2)}, u32[]{:S(2)}) collective-permute-start(f32[4,512]{1,0:T(4,128)S(1)} %fusion.7.samples_ref), channel_id=1, source_target_pairs={{0,4},{4,0},{1,5},{5,1},{2,6},{6,2},{3,7},{7,3},{8,12},{12,8},{9,1... | collective-permute-start | bytes 24584 | tf_op jit(solution)/shard_map/ppermute | solution.py:43
  37.5 20.5 %copy-start.3 = (f32[73,73]{1,0:T(8,128)S(1)}, f32[73,73]{1,0:T(8,128)}, u32[]{:S(2)}) copy-start(f32[73,73]{1,0:T(8,128)} %matrix_ref.1) | copy-start | bytes 63952

commit v8 on v7

--- a/solution.py
+++ b/solution.py
@@ -362,20 +362,24 @@
                 out_ref[c, 2 * rows : 2 * rows + 8, span] = values[8 * c : 8 * c + 8]
 
 
-def filter_kernel(width, paired, across, matrix_ref, arrived_ref, out_ref, wide_ref, ready_ref, sems):
-    depth = wide_ref.shape[0]
-    rows = depth - 8
+def split_matrix_kernel(rows, matrix_ref, out_ref, wide_ref):
     samples = matrix_ref.shape[0]
-    groups = out_ref.shape[2] // 2
-    row = iota((8, LANES), 0)
     wide_ref[...] = jnp.zeros_like(wide_ref)
     wide_ref[0:samples, 0:HISTORY] = matrix_ref[:, 0:HISTORY]
     for late in range(STEPS):
         for number in range(2):
             at = rows + 2 * late + number
             wide_ref[0:samples, at : at + 1] = matrix_ref[:, HISTORY + late : HISTORY + late + 1]
-    high, low = halves(wide_ref[:, 0:depth])
-    left = jnp.concatenate([high, low, high], axis=1)
+    high, low = halves(wide_ref[:, 0 : rows + 8])
+    out_ref[...] = jnp.concatenate([high, low, high], axis=1)
+
+
+def filter_kernel(width, paired, across, matrix_ref, arrived_ref, out_ref, ready_ref, sems):
+    rows = matrix_ref.shape[0] - 8
+    samples = out_ref.shape[0]
+    groups = out_ref.shape[2] // 2
+    row = iota((8, LANES), 0)
+    left = matrix_ref[...]
 
     def block_of(tile):
         line, column = tile // across, tile % across
@@ -490,6 +494,17 @@
         compiler_params=grant,
         name="place_samples",
     )(half, samples, far_samples, onehot, far_onehot, placed, far_placed)
+    matrix = pl.pallas_call(
+        functools.partial(split_matrix_kernel, rows),
+        out_shape=jax.ShapeDtypeStruct((rows + 8, 3 * (rows + 8)), bf16),
+        in_specs=whole(1),
+        out_specs=whole(1)[0],
+        scratch_shapes=[pltpu.VMEM((rows + 8, LANES), f32)],
+        cost_estimate=cost(1000000, 60000),
+        compiler_params=grant,
+        name="split_matrix",
+    )(filter_matrix)
+    matrix, outgoing = lax.optimization_barrier((matrix, outgoing))
     if not paired:
         outgoing = outgoing.reshape(2, depth, members, per_owner).transpose(2, 1, 0, 3)
     arrived = lax.all_to_all(outgoing, ("ty", "within"), split_axis=0, concat_axis=0, tiled=True)
@@ -508,14 +523,13 @@
         in_specs=whole(2),
         out_specs=pl.BlockSpec(memory_space=pltpu.HBM),
         scratch_shapes=[
-            pltpu.VMEM((rows + 8, LANES), f32),
             pltpu.VMEM((runs, SAMPLES * 8, LANES), f32),
             pltpu.SemaphoreType.DMA((runs,)),
         ],
         cost_estimate=cost(2 * 3 * 80 * 80 * 8 * slots, 3000000),
         compiler_params=grant,
         name="filter_series",
-    )(filter_matrix, arrived)
+    )(matrix, arrived)
     filtered = filtered.reshape(SAMPLES, 4 * groups, 2, LANES)
     return filtered.transpose(2, 0, 1, 3).reshape(2, SAMPLES, 4 * slots)
 

time: 59.8 us -> 59.7 us (level)
  no operation moved by 1% of the time
where the time goes in v8:
time: 59.7 us; the launch traced here: 59.4 us
  blocking collectives  20.5 us (34%)
  starting transfers between devices  19.1 us (32%)
  waiting for transfers between devices  8.66 us (15%)
  Pallas kernels  7.59 us (13%)
  local copies, waits for them, and re-layouts  2.87 us (5%)
    all_to_all x1, blocking collectives, run(): lax.all_to_all(outgoing, ('ty', 'within'), split_axis=0, concat_axis=0, t...  20.5 us
    ppermute x3, starting transfers between devices, swapped(): return lax.ppermute(value, 'half', [(0, 1), (1, 0)])  9.06 us
    ppermute x4, starting transfers between devices, exchanged(): lax.ppermute(up if up is down else jnp.where(even, down, up), places[axis...  7.8 us
    ppermute x4, waiting for transfers between devices, exchanged(): lax.ppermute(up if up is down else jnp.where(even, down, up), places[axis...  5.35 us
    ppermute x3, waiting for transfers between devices, swapped(): return lax.ppermute(value, 'half', [(0, 1), (1, 0)])  3.22 us
    ppermute x4, starting transfers between devices, exchanged(): lax.ppermute(up if up is down else jnp.where(even, up, down), places[axis...  2.28 us
    pallas_call x1, Pallas kernels, run_step(): pl.pallas_call(functools.partial(inner_kernel, step, following), out_shap...  1.9 us
    pallas_call x2, Pallas kernels, place(): pl.pallas_call(functools.partial(place_history_kernel, per_owner, paired,...  1.89 us
  transfers between devices with their start and end apart: 11, of which 4 were waited for; matrix products, arithmetic and copies ran while one was open for 2% of the time, Pallas kernels for 9%

profile of v8, /device:TPU:0, one launch (start us, length us, event | category | flops | bytes accessed | tf_op | source)
XLA Modules:
  0.0 59.4 jit_solution(3747942424610215816)
XLA Ops:
  0.0 0.8 %slice_reduce_fusion.3 = (f32[2,3,128]{2,1,0:T(4,128)S(1)}, f32[2,3,128]{2,1,0:T(4,128)S(1)}) fusion(f32[2,3,128,128]{3,2,1,0:T(8,128)} %velocity_ref.1), kind=kLoop, calls=%fused_computation.34 | loop fusion | bytes 12288 | tf_op jit(solution)/shard_map/slice | solution.py:433
  0.8 1.1 %bitcast_bitcast_fusion = f32[71,4,2,128]{3,2,0,1:T(2,128)S(1)} fusion(f32[2,71,512]{2,0,1:T(2,128)} %param.10), kind=kLoop, calls=%fused_computation.2 | loop fusion | bytes 581632 | tf_op jit(solution)/shard_map/transpose | solution.py:425
  2.1 0.6 collective-permute-start.1
  2.6 2.6 %collective-permute-start = (f32[148,128]{1,0:T(8,128)S(1)}, f32[148,128]{1,0:T(8,128)S(1)}, u32[]{:S(2)}, u32[]{:S(2)}) collective-permute-start(f32[148,128]{1,0:T(8,128)S(1)} %get-tuple-element.43), channel_id=1, source_target_pairs={{0,24},{8,16},{16,8},{24,0},{1,25},{9,17},{17,9},{25,1},{2,26},{10... | collective-permute-start | bytes 227336 | tf_op jit(solution)/shard_map/ppermute | solution.py:38
  5.2 0.1 copy.14
  5.3 0.2 reshape.125
  5.5 2.7 %collective-permute-start.10 = (f32[426,128]{1,0:T(8,128)S(1)}, f32[426,128]{1,0:T(8,128)S(1)}, u32[]{:S(2)}, u32[]{:S(2)}) collective-permute-start(f32[426,128]{1,0:T(8,128)S(1)} %reshape.125), channel_id=1, source_target_pairs={{0,4},{4,0},{1,5},{5,1},{2,6},{6,2},{3,7},{7,3},{8,12},{12,8},{9,1... | collective-permute-start | bytes 654344 | tf_op jit(solution)/shard_map/ppermute | solution.py:43
  8.2 0.6 find_sides.1
  8.8 0.4 slice_reduce_fusion
  9.3 1.6 %collective-permute-start.3 = (f32[160,128]{1,0:T(8,128)S(1)}, f32[160,128]{1,0:T(8,128)S(1)}, u32[]{:S(2)}, u32[]{:S(2)}) collective-permute-start(f32[160,128]{1,0:T(8,128)S(1)} %get-tuple-element.40), channel_id=1, source_target_pairs={{0,1},{1,0},{2,3},{3,2},{4,5},{5,4},{6,7},{7,6},{8,9},{9,8},{10,11... | collective-permute-start | bytes 245768 | tf_op jit(solution)/shard_map/ppermute | solution.py:37
  10.9 2.0 %collective-permute-start.2 = (f32[160,128]{1,0:T(8,128)S(1)}, f32[160,128]{1,0:T(8,128)S(1)}, u32[]{:S(2)}, u32[]{:S(2)}) collective-permute-start(f32[160,128]{1,0:T(8,128)S(1)} %get-tuple-element.41), channel_id=1, source_target_pairs={{0,7},{1,2},{2,1},{3,4},{4,3},{5,6},{6,5},{7,0},{8,15},{9,10},{10,... | collective-permute-start | bytes 245768 | tf_op jit(solution)/shard_map/ppermute | solution.py:38
  12.9 0.1 pad.11.clone
  13.0 0.1 pad.2.clone
  13.1 0.2 split_matrix.1.matrix_ref
  13.3 0.2 find_columns.1.owner_ref
  13.6 1.9 %sample_inner.1 = (f32[5,8,512]{2,1,0:T(8,128)S(1)}, bf16[5,2,128,512]{3,2,1,0:T(8,128)(2,1)S(1)}, bf16[5,2,128,512]{3,2,1,0:T(8,128)(2,1)S(1)}) custom-call(f32[2,3,128,128]{3,2,1,0:T(8,128)S(1)} %copy-done, s32[2,4,2,512]{3,2,1,0:T(2,128)S(1)} %copy-done.2), custom_call_target="tpu_custom_call" | custom-call | flops 671088640 | bytes 600000 | tf_op jit(solution)/shard_map/sample_inner/pallas_call | solution.py:208
  15.5 2.6 %collective-permute-done.2 = f32[160,128]{1,0:T(8,128)S(1)} collective-permute-done((f32[160,128]{1,0:T(8,128)S(1)}, f32[160,128]{1,0:T(8,128)S(1)}, u32[]{:S(2)}, u32[]{:S(2)}) %collective-permute-start.2) | collective-permute-done | bytes 81952 | tf_op jit(solution)/shard_map/ppermute | solution.py:38
  18.1 0.8 %sample_step.1 = (f32[8,512]{1,0:T(8,128)S(1)}, f32[8,128]{1,0:T(8,128)S(1)}, f32[8,512]{1,0:T(8,128)S(1)}) custom-call(f32[5,8,512]{2,1,0:T(8,128)S(1)} %get-tuple-element.17.part_ref, bf16[5,2,128,512]{3,2,1,0:T(8,128)(2,1)S(1)} %get-tuple-element.18.cols_ref, bf16[5,2,128,512]{3,2,1,0:T(8,128)(2,1)S(1)} %get-tuple-element.19.rows_ref, ...), custom_call_target="tpu_custom_call" | custom-call | flops 83886080 | bytes 600000 | tf_op jit(solution)/shard_map/sample_step/pallas_call | solution.py:225
  19.0 0.6 %collective-permute-start.4 = (f32[8,128]{1,0:T(8,128)S(1)}, f32[8,128]{1,0:T(8,128)S(1)}, u32[]{:S(2)}, u32[]{:S(2)}) collective-permute-start(f32[8,128]{1,0:T(8,128)S(1)} %get-tuple-element.20), channel_id=1, source_target_pairs={{0,24},{8,16},{16,8},{24,0},{1,25},{9,17},{17,9},{25,1},{2,26},{10... | collective-permute-start | bytes 12296 | tf_op jit(solution)/shard_map/ppermute | solution.py:38
  19.6 0.1 maximum_maximum_fusion.past_ref
  19.7 6.0 %collective-permute-start.9 = (f32[148,128]{1,0:T(8,128)S(1)}, f32[148,128]{1,0:T(8,128)S(1)}, u32[]{:S(2)}, u32[]{:S(2)}) collective-permute-start(f32[148,128]{1,0:T(8,128)S(1)} %maximum_maximum_fusion.past_ref), channel_id=1, source_target_pairs={{0,4},{4,0},{1,5},{5,1},{2,6},{6,2},{3,7},{7,3},{8,12},{12,8},{9,1... | collective-permute-start | bytes 227336 | tf_op jit(solution)/shard_map/ppermute | solution.py:43
  25.8 2.5 %collective-permute-start.6 = (f32[8,128]{1,0:T(8,128)S(1)}, f32[8,128]{1,0:T(8,128)S(1)}, u32[]{:S(2)}, u32[]{:S(2)}) collective-permute-start(f32[8,128]{1,0:T(8,128)S(1)} %select_select_fusion), channel_id=1, source_target_pairs={{0,7},{1,2},{2,1},{3,4},{4,3},{5,6},{6,5},{7,0},{8,15},{9,10},{10,... | collective-permute-start | bytes 12296 | tf_op jit(solution)/shard_map/ppermute | solution.py:38
  28.4 0.9 %place_history.2 = (f32[16,72,128]{2,1,0:T(8,128)S(1)}, bf16[512,1024]{1,0:T(8,128)(2,1)S(1)}) custom-call(s32[1]{0:T(128)} %bitcast.half_ref, f32[1,512]{1,0:T(1,128)S(1)} %find_columns.1.owner_ref, f32[568,128]{1,0:T(8,128)S(1)} %bitcast.42, f32[148,128]{1,0:T(8,128)S(1)} %maximum_maximum_fusion.past_ref), custom_call_target="tpu_custom_call" | custom-call | flops 301989888 | bytes 3000000 | tf_op jit(solution)/shard_map/place_history/pallas_call | solution.py:466
  29.3 0.1 collective-permute-done.7
  29.4 2.8 %collective-permute-done.6 = f32[8,128]{1,0:T(8,128)S(1)} collective-permute-done((f32[8,128]{1,0:T(8,128)S(1)}, f32[8,128]{1,0:T(8,128)S(1)}, u32[]{:S(2)}, u32[]{:S(2)}) %collective-permute-start.6) | collective-permute-done | bytes 4128 | tf_op jit(solution)/shard_map/ppermute | solution.py:38
  32.2 0.1 maximum_subtract_fusion
  32.3 0.4 collective-permute-start.8
  32.8 0.9 %place_history.3 = (f32[16,72,128]{2,1,0:T(8,128)S(1)}, bf16[512,1024]{1,0:T(8,128)(2,1)S(1)}) custom-call(s32[1]{0:T(128)} %bitcast.half_ref, f32[1,512]{1,0:T(1,128)S(1)} %bitcast.44, f32[426,128]{1,0:T(8,128)S(1)} %collective-permute-done.10.history_ref, f32[148,128]{1,0:T(8,128)S(1)} %collective-permute-done.9.past_ref), custom_call_target="tpu_custom_call" | custom-call | flops 301989888 | bytes 3000000 | tf_op jit(solution)/shard_map/place_history/pallas_call | solution.py:466
  33.7 3.2 %collective-permute-done.8.far_samples_ref = f32[4,512]{1,0:T(4,128)S(1)} collective-permute-done((f32[4,512]{1,0:T(4,128)S(1)}, f32[4,512]{1,0:T(4,128)S(1)}, u32[]{:S(2)}, u32[]{:S(2)}) %collective-permute-start.8) | collective-permute-done | bytes 8224 | tf_op jit(solution)/shard_map/ppermute | solution.py:43
  36.9 0.6 place_samples.1
  37.5 20.5 %all_to_all.5.arrived_ref = f32[16,152,128]{2,1,0:T(8,128)S(1)} all-to-all(f32[16,152,128]{2,1,0:T(8,128)S(1)} %place_samples.1), channel_id=1, replica_groups=mesh['ty'=4,'half'=2,'within'=4] {'ty','within'}, dimensions={0} | all-to-all | bytes 2490368 | tf_op jit(solution)/shard_map/all_to_all | solution.py:510
  58.0 1.5 %filter_series.1 = f32[73,4,8,128]{3,2,1,0:T(8,128)} custom-call(bf16[80,240]{1,0:T(8,128)(2,1)S(1)} %split_matrix.1.matrix_ref, f32[16,152,128]{2,1,0:T(8,128)S(1)} %all_to_all.5.arrived_ref), custom_call_target="tpu_custom_call" | custom-call | flops 157286400 | bytes 3000000 | tf_op jit(solution)/shard_map/filter_series/pallas_call | solution.py:520
  (49 shorter events, 0.5 us)
Async XLA Ops:
  0.8 7.4 %copy-start.5 = (s32[1,8]{1,0:T(1,128)S(1)}, s32[1,8]{1,0:T(1,128)}, u32[]{:S(2)}) copy-start(s32[1,8]{1,0:T(1,128)} %leavers_ref.1) | copy-start | bytes 100
  0.8 8.0 %copy-start = (f32[2,3,128,128]{3,2,1,0:T(8,128)S(1)}, f32[2,3,128,128]{3,2,1,0:T(8,128)}, u32[]{:S(2)}) copy-start(f32[2,3,128,128]{3,2,1,0:T(8,128)} %velocity_ref.1) | copy-start | bytes 1179652
  2.1 7.2 %collective-permute-start.1 = (f32[148,128]{1,0:T(8,128)S(1)}, f32[148,128]{1,0:T(8,128)S(1)}, u32[]{:S(2)}, u32[]{:S(2)}) collective-permute-start(f32[148,128]{1,0:T(8,128)S(1)} %get-tuple-element.42), channel_id=1, source_target_pairs={{0,8},{8,0},{16,24},{24,16},{1,9},{9,1},{17,25},{25,17},{2,10},{10... | collective-permute-start | bytes 227336 | tf_op jit(solution)/shard_map/ppermute | solution.py:37
  2.6 6.6 %collective-permute-start = (f32[148,128]{1,0:T(8,128)S(1)}, f32[148,128]{1,0:T(8,128)S(1)}, u32[]{:S(2)}, u32[]{:S(2)}) collective-permute-start(f32[148,128]{1,0:T(8,128)S(1)} %get-tuple-element.43), channel_id=1, source_target_pairs={{0,24},{8,16},{16,8},{24,0},{1,25},{9,17},{17,9},{25,1},{2,26},{10... | collective-permute-start | bytes 227336 | tf_op jit(solution)/shard_map/ppermute | solution.py:38
  5.2 7.7 %copy-start.6 = (s32[512,1]{0,1:T(1,128)S(1)}, s32[512,1]{0,1:T(1,128)}, u32[]{:S(2)}) copy-start(s32[512,1]{0,1:T(1,128)} %param.12) | copy-start | bytes 6148
  5.2 7.9 %copy-start.3 = (f32[73,73]{1,0:T(8,128)S(1)}, f32[73,73]{1,0:T(8,128)}, u32[]{:S(2)}) copy-start(f32[73,73]{1,0:T(8,128)} %matrix_ref.1) | copy-start | bytes 63952
  5.3 8.2 %copy-start.2 = (s32[2,4,2,512]{3,2,1,0:T(2,128)S(1)}, s32[2,4,2,512]{3,2,1,0:T(2,128)}, u32[]{:S(2)}) copy-start(s32[2,4,2,512]{3,2,1,0:T(2,128)} %cells_ref.3) | copy-start | bytes 98308
  5.5 27.3 %collective-permute-start.10 = (f32[426,128]{1,0:T(8,128)S(1)}, f32[426,128]{1,0:T(8,128)S(1)}, u32[]{:S(2)}, u32[]{:S(2)}) collective-permute-start(f32[426,128]{1,0:T(8,128)S(1)} %reshape.125), channel_id=1, source_target_pairs={{0,4},{4,0},{1,5},{5,1},{2,6},{6,2},{3,7},{7,3},{8,12},{12,8},{9,1... | collective-permute-start | bytes 654344 | tf_op jit(solution)/shard_map/ppermute | solution.py:43
  9.3 6.1 %collective-permute-start.3 = (f32[160,128]{1,0:T(8,128)S(1)}, f32[160,128]{1,0:T(8,128)S(1)}, u32[]{:S(2)}, u32[]{:S(2)}) collective-permute-start(f32[160,128]{1,0:T(8,128)S(1)} %get-tuple-element.40), channel_id=1, source_target_pairs={{0,1},{1,0},{2,3},{3,2},{4,5},{5,4},{6,7},{7,6},{8,9},{9,8},{10,11... | collective-permute-start | bytes 245768 | tf_op jit(solution)/shard_map/ppermute | solution.py:37
  10.9 7.1 %collective-permute-start.2 = (f32[160,128]{1,0:T(8,128)S(1)}, f32[160,128]{1,0:T(8,128)S(1)}, u32[]{:S(2)}, u32[]{:S(2)}) collective-permute-start(f32[160,128]{1,0:T(8,128)S(1)} %get-tuple-element.41), channel_id=1, source_target_pairs={{0,7},{1,2},{2,1},{3,4},{4,3},{5,6},{6,5},{7,0},{8,15},{9,10},{10,... | collective-permute-start | bytes 245768 | tf_op jit(solution)/shard_map/ppermute | solution.py:38
  13.5 4.5 %copy-start.4 = (f32[2,512]{1,0:T(2,128)S(1)}, f32[2,512]{1,0:T(2,128)}, u32[]{:S(2)}) copy-start(f32[2,512]{1,0:T(2,128)} %point_ref.1) | copy-start | bytes 12292
  18.1 10.3 %copy-start.1 = (f32[2,71,512]{2,0,1:T(2,128)S(1)}, f32[2,71,512]{2,0,1:T(2,128)}, u32[]{:S(2)}) copy-start(f32[2,71,512]{2,0,1:T(2,128)} %param.10) | copy-start | bytes 872452
  18.9 6.8 %collective-permute-start.5 = (f32[8,128]{1,0:T(8,128)S(1)}, f32[8,128]{1,0:T(8,128)S(1)}, u32[]{:S(2)}, u32[]{:S(2)}) collective-permute-start(f32[8,128]{1,0:T(8,128)S(1)} %get-tuple-element.20), channel_id=1, source_target_pairs={{0,8},{8,0},{16,24},{24,16},{1,9},{9,1},{17,25},{25,17},{2,10},{10... | collective-permute-start | bytes 12296 | tf_op jit(solution)/shard_map/ppermute | solution.py:37
  19.0 6.7 %collective-permute-start.4 = (f32[8,128]{1,0:T(8,128)S(1)}, f32[8,128]{1,0:T(8,128)S(1)}, u32[]{:S(2)}, u32[]{:S(2)}) collective-permute-start(f32[8,128]{1,0:T(8,128)S(1)} %get-tuple-element.20), channel_id=1, source_target_pairs={{0,24},{8,16},{16,8},{24,0},{1,25},{9,17},{17,9},{25,1},{2,26},{10... | collective-permute-start | bytes 12296 | tf_op jit(solution)/shard_map/ppermute | solution.py:38
  19.7 13.0 %collective-permute-start.9 = (f32[148,128]{1,0:T(8,128)S(1)}, f32[148,128]{1,0:T(8,128)S(1)}, u32[]{:S(2)}, u32[]{:S(2)}) collective-permute-start(f32[148,128]{1,0:T(8,128)S(1)} %maximum_maximum_fusion.past_ref), channel_id=1, source_target_pairs={{0,4},{4,0},{1,5},{5,1},{2,6},{6,2},{3,7},{7,3},{8,12},{12,8},{9,1... | collective-permute-start | bytes 227336 | tf_op jit(solution)/shard_map/ppermute | solution.py:43
  25.7 3.7 %collective-permute-start.7 = (f32[8,128]{1,0:T(8,128)S(1)}, f32[8,128]{1,0:T(8,128)S(1)}, u32[]{:S(2)}, u32[]{:S(2)}) collective-permute-start(f32[8,128]{1,0:T(8,128)S(1)} %select_select_fusion), channel_id=1, source_target_pairs={{0,1},{1,0},{2,3},{3,2},{4,5},{5,4},{6,7},{7,6},{8,9},{9,8},{10,11... | collective-permute-start | bytes 12296 | tf_op jit(solution)/shard_map/ppermute | solution.py:37
  25.8 6.4 %collective-permute-start.6 = (f32[8,128]{1,0:T(8,128)S(1)}, f32[8,128]{1,0:T(8,128)S(1)}, u32[]{:S(2)}, u32[]{:S(2)}) collective-permute-start(f32[8,128]{1,0:T(8,128)S(1)} %select_select_fusion), channel_id=1, source_target_pairs={{0,7},{1,2},{2,1},{3,4},{4,3},{5,6},{6,5},{7,0},{8,15},{9,10},{10,... | collective-permute-start | bytes 12296 | tf_op jit(solution)/shard_map/ppermute | solution.py:38
  32.3 4.6 %collective-permute-start.8 = (f32[4,512]{1,0:T(4,128)S(1)}, f32[4,512]{1,0:T(4,128)S(1)}, u32[]{:S(2)}, u32[]{:S(2)}) collective-permute-start(f32[4,512]{1,0:T(4,128)S(1)} %fusion.7.samples_ref), channel_id=1, source_target_pairs={{0,4},{4,0},{1,5},{5,1},{2,6},{6,2},{3,7},{7,3},{8,12},{12,8},{9,1... | collective-permute-start | bytes 24584 | tf_op jit(solution)/shard_map/ppermute | solution.py:43

commit v9 on v8

--- a/solution.py
+++ b/solution.py
@@ -194,7 +194,7 @@
     record = jnp.concatenate(point + k_one + blank, axis=0)
     record_ref[...] = record
     band = step * 8 * MOST
-    lead_ref[...] = record[:, band : band + 8 * MOST]
+    lead_ref[...] = record[0:4, band : band + 8 * MOST]
     if following:
         next_ref[...] = jnp.concatenate([value for corner in corners[4] for value in corner], axis=0)
 
@@ -221,7 +221,7 @@
     )(velocity, cells)
     operands = (*inner, *ends, point, cells) + ((first,) if step > 0 else ())
     shape = jax.ShapeDtypeStruct((8, slots), f32)
-    shapes = [shape, jax.ShapeDtypeStruct((8, 8 * MOST), f32)] + ([shape] if following else [])
+    shapes = [shape, jax.ShapeDtypeStruct((4, 8 * MOST), f32)] + ([shape] if following else [])
     return pl.pallas_call(
         functools.partial(step_kernel, step, following, velocity.shape[1:]),
         out_shape=shapes,
@@ -476,8 +476,8 @@
     placed, onehot = place(owner.reshape(1, slots), raw, past, 0)
     far_placed, far_onehot = place(far_owner, far_raw, far_past, moving)
     lead = chosen(sides[0, 1:2], lead, lead_west, lead_east)
-    lowered = [sides[0, 0:1] * tile_rows, sides[0, 1:2] * tile_cols, jnp.zeros((6, 8 * MOST), f32)]
-    record = jnp.concatenate([lead - jnp.concatenate(lowered, axis=0), record[:, 8 * MOST :]], axis=1)
+    lowered = [sides[0, 0:1] * tile_rows, sides[0, 1:2] * tile_cols, jnp.zeros((2, 8 * MOST), f32)]
+    record = jnp.concatenate([lead - jnp.concatenate(lowered, axis=0), record[0:4, 8 * MOST :]], axis=1)
     point = record[0:2]
     corners = [[first[2 * i + c : 2 * i + c + 1] for c in range(2)] for i in range(4)]
     last = bilinear(corners, [record[0:1], record[1:2]], cells[STEPS - 1, 0])

time: 59.7 us -> 59.5 us (level)
  transfers between devices with their start and end apart: 11 -> 11, of which waited for: 4 -> 3; matrix products, arithmetic and copies ran while one was open for 2% -> 1% of each run, Pallas kernels for 9% -> 9%
where the time goes in v9:
time: 59.5 us; the launch traced here: 59.3 us
  blocking collectives  20.5 us (34%)
  starting transfers between devices  19.2 us (32%)
  waiting for transfers between devices  8.72 us (15%)
  Pallas kernels  7.58 us (13%)
  local copies, waits for them, and re-layouts  2.71 us (5%)
    all_to_all x1, blocking collectives, run(): lax.all_to_all(outgoing, ('ty', 'within'), split_axis=0, concat_axis=0, t...  20.5 us
    ppermute x3, starting transfers between devices, swapped(): return lax.ppermute(value, 'half', [(0, 1), (1, 0)])  9.11 us
    ppermute x4, starting transfers between devices, exchanged(): lax.ppermute(up if up is down else jnp.where(even, down, up), places[axis...  7.84 us
    ppermute x4, waiting for transfers between devices, exchanged(): lax.ppermute(up if up is down else jnp.where(even, down, up), places[axis...  5.51 us
    ppermute x3, waiting for transfers between devices, swapped(): return lax.ppermute(value, 'half', [(0, 1), (1, 0)])  3.2 us
    ppermute x4, starting transfers between devices, exchanged(): lax.ppermute(up if up is down else jnp.where(even, up, down), places[axis...  2.28 us
    pallas_call x1, Pallas kernels, run_step(): pl.pallas_call(functools.partial(inner_kernel, step, following), out_shap...  1.9 us
    pallas_call x2, Pallas kernels, place(): pl.pallas_call(functools.partial(place_history_kernel, per_owner, paired,...  1.87 us
  transfers between devices with their start and end apart: 11, of which 3 were waited for; matrix products, arithmetic and copies ran while one was open for 1% of the time, Pallas kernels for 9%

profile of v9, /device:TPU:0, one launch (start us, length us, event | category | flops | bytes accessed | tf_op | source)
XLA Modules:
  0.0 59.3 jit_solution(15039128415879007192)
XLA Ops:
  0.0 0.8 %slice_reduce_fusion.3 = (f32[2,3,128]{2,1,0:T(4,128)S(1)}, f32[2,3,128]{2,1,0:T(4,128)S(1)}) fusion(f32[2,3,128,128]{3,2,1,0:T(8,128)} %velocity_ref.1), kind=kLoop, calls=%fused_computation.35 | loop fusion | bytes 12288 | tf_op jit(solution)/shard_map/slice | solution.py:433
  0.8 0.0 copy-start.5
  0.8 1.1 %bitcast_bitcast_fusion = f32[71,4,2,128]{3,2,0,1:T(2,128)S(1)} fusion(f32[2,71,512]{2,0,1:T(2,128)} %param.10), kind=kLoop, calls=%fused_computation.2 | loop fusion | bytes 581632 | tf_op jit(solution)/shard_map/transpose | solution.py:425
  1.9 0.1 reshape_squeeze.15
  2.1 0.6 collective-permute-start.1
  2.6 2.6 %collective-permute-start = (f32[148,128]{1,0:T(8,128)S(1)}, f32[148,128]{1,0:T(8,128)S(1)}, u32[]{:S(2)}, u32[]{:S(2)}) collective-permute-start(f32[148,128]{1,0:T(8,128)S(1)} %get-tuple-element.40), channel_id=1, source_target_pairs={{0,24},{8,16},{16,8},{24,0},{1,25},{9,17},{17,9},{25,1},{2,26},{10... | collective-permute-start | bytes 227336 | tf_op jit(solution)/shard_map/ppermute | solution.py:38
  5.2 0.1 copy.14
  5.3 0.2 reshape.125
  5.5 2.7 %collective-permute-start.10 = (f32[426,128]{1,0:T(8,128)S(1)}, f32[426,128]{1,0:T(8,128)S(1)}, u32[]{:S(2)}, u32[]{:S(2)}) collective-permute-start(f32[426,128]{1,0:T(8,128)S(1)} %reshape.125), channel_id=1, source_target_pairs={{0,4},{4,0},{1,5},{5,1},{2,6},{6,2},{3,7},{7,3},{8,12},{12,8},{9,1... | collective-permute-start | bytes 654344 | tf_op jit(solution)/shard_map/ppermute | solution.py:43
  8.2 0.6 find_sides.1
  8.8 0.4 slice_reduce_fusion
  9.3 1.6 %collective-permute-start.3 = (f32[160,128]{1,0:T(8,128)S(1)}, f32[160,128]{1,0:T(8,128)S(1)}, u32[]{:S(2)}, u32[]{:S(2)}) collective-permute-start(f32[160,128]{1,0:T(8,128)S(1)} %get-tuple-element.37), channel_id=1, source_target_pairs={{0,1},{1,0},{2,3},{3,2},{4,5},{5,4},{6,7},{7,6},{8,9},{9,8},{10,11... | collective-permute-start | bytes 245768 | tf_op jit(solution)/shard_map/ppermute | solution.py:37
  10.9 2.0 %collective-permute-start.2 = (f32[160,128]{1,0:T(8,128)S(1)}, f32[160,128]{1,0:T(8,128)S(1)}, u32[]{:S(2)}, u32[]{:S(2)}) collective-permute-start(f32[160,128]{1,0:T(8,128)S(1)} %get-tuple-element.38), channel_id=1, source_target_pairs={{0,7},{1,2},{2,1},{3,4},{4,3},{5,6},{6,5},{7,0},{8,15},{9,10},{10,... | collective-permute-start | bytes 245768 | tf_op jit(solution)/shard_map/ppermute | solution.py:38
  12.9 0.2 split_matrix.1.matrix_ref
  13.1 0.2 find_columns.1.owner_ref
  13.4 1.9 %sample_inner.1 = (f32[5,8,512]{2,1,0:T(8,128)S(1)}, bf16[5,2,128,512]{3,2,1,0:T(8,128)(2,1)S(1)}, bf16[5,2,128,512]{3,2,1,0:T(8,128)(2,1)S(1)}) custom-call(f32[2,3,128,128]{3,2,1,0:T(8,128)S(1)} %copy-done, s32[2,4,2,512]{3,2,1,0:T(2,128)S(1)} %copy-done.2), custom_call_target="tpu_custom_call" | custom-call | flops 671088640 | bytes 600000 | tf_op jit(solution)/shard_map/sample_inner/pallas_call | solution.py:208
  15.3 2.7 %collective-permute-done.2 = f32[160,128]{1,0:T(8,128)S(1)} collective-permute-done((f32[160,128]{1,0:T(8,128)S(1)}, f32[160,128]{1,0:T(8,128)S(1)}, u32[]{:S(2)}, u32[]{:S(2)}) %collective-permute-start.2) | collective-permute-done | bytes 81952 | tf_op jit(solution)/shard_map/ppermute | solution.py:38
  18.1 0.8 %sample_step.1 = (f32[8,512]{1,0:T(8,128)S(1)}, f32[4,128]{1,0:T(4,128)S(1)}, f32[8,512]{1,0:T(8,128)S(1)}) custom-call(f32[5,8,512]{2,1,0:T(8,128)S(1)} %get-tuple-element.17.part_ref, bf16[5,2,128,512]{3,2,1,0:T(8,128)(2,1)S(1)} %get-tuple-element.18.cols_ref, bf16[5,2,128,512]{3,2,1,0:T(8,128)(2,1)S(1)} %get-tuple-element.19.rows_ref, ...), custom_call_target="tpu_custom_call" | custom-call | flops 83886080 | bytes 600000 | tf_op jit(solution)/shard_map/sample_step/pallas_call | solution.py:225
  18.9 0.1 collective-permute-start.5
  19.0 0.6 %collective-permute-start.4 = (f32[4,128]{1,0:T(4,128)S(1)}, f32[4,128]{1,0:T(4,128)S(1)}, u32[]{:S(2)}, u32[]{:S(2)}) collective-permute-start(f32[4,128]{1,0:T(4,128)S(1)} %get-tuple-element.20), channel_id=1, source_target_pairs={{0,24},{8,16},{16,8},{24,0},{1,25},{9,17},{17,9},{25,1},{2,26},{10... | collective-permute-start | bytes 6152 | tf_op jit(solution)/shard_map/ppermute | solution.py:38
  19.7 6.0 %collective-permute-start.9 = (f32[148,128]{1,0:T(8,128)S(1)}, f32[148,128]{1,0:T(8,128)S(1)}, u32[]{:S(2)}, u32[]{:S(2)}) collective-permute-start(f32[148,128]{1,0:T(8,128)S(1)} %pad_maximum_fusion.6.past_ref), channel_id=1, source_target_pairs={{0,4},{4,0},{1,5},{5,1},{2,6},{6,2},{3,7},{7,3},{8,12},{12,8},{9,1... | collective-permute-start | bytes 227336 | tf_op jit(solution)/shard_map/ppermute | solution.py:43
  25.7 0.1 collective-permute-start.7
  25.7 2.6 %collective-permute-start.6 = (f32[4,128]{1,0:T(4,128)S(1)}, f32[4,128]{1,0:T(4,128)S(1)}, u32[]{:S(2)}, u32[]{:S(2)}) collective-permute-start(f32[4,128]{1,0:T(4,128)S(1)} %select_select_fusion), channel_id=1, source_target_pairs={{0,7},{1,2},{2,1},{3,4},{4,3},{5,6},{6,5},{7,0},{8,15},{9,10},{10,... | collective-permute-start | bytes 6152 | tf_op jit(solution)/shard_map/ppermute | solution.py:38
  28.3 0.9 %place_history.2 = (f32[16,72,128]{2,1,0:T(8,128)S(1)}, bf16[512,1024]{1,0:T(8,128)(2,1)S(1)}) custom-call(s32[1]{0:T(128)} %bitcast.half_ref, f32[1,512]{1,0:T(1,128)S(1)} %find_columns.1.owner_ref, f32[568,128]{1,0:T(8,128)S(1)} %bitcast.48, f32[148,128]{1,0:T(8,128)S(1)} %pad_maximum_fusion.6.past_ref), custom_call_target="tpu_custom_call" | custom-call | flops 301989888 | bytes 3000000 | tf_op jit(solution)/shard_map/place_history/pallas_call | solution.py:466
  29.3 0.0 collective-permute-done.7
  29.3 2.8 %collective-permute-done.6 = f32[4,128]{1,0:T(4,128)S(1)} collective-permute-done((f32[4,128]{1,0:T(4,128)S(1)}, f32[4,128]{1,0:T(4,128)S(1)}, u32[]{:S(2)}, u32[]{:S(2)}) %collective-permute-start.6) | collective-permute-done | bytes 2080 | tf_op jit(solution)/shard_map/ppermute | solution.py:38
  32.2 0.5 collective-permute-start.8
  32.6 0.9 %place_history.3 = (f32[16,72,128]{2,1,0:T(8,128)S(1)}, bf16[512,1024]{1,0:T(8,128)(2,1)S(1)}) custom-call(s32[1]{0:T(128)} %bitcast.half_ref, f32[1,512]{1,0:T(1,128)S(1)} %bitcast.50, f32[426,128]{1,0:T(8,128)S(1)} %collective-permute-done.10.history_ref, f32[148,128]{1,0:T(8,128)S(1)} %collective-permute-done.9.past_ref), custom_call_target="tpu_custom_call" | custom-call | flops 301989888 | bytes 3000000 | tf_op jit(solution)/shard_map/place_history/pallas_call | solution.py:466
  33.6 3.2 %collective-permute-done.8.far_samples_ref = f32[4,512]{1,0:T(4,128)S(1)} collective-permute-done((f32[4,512]{1,0:T(4,128)S(1)}, f32[4,512]{1,0:T(4,128)S(1)}, u32[]{:S(2)}, u32[]{:S(2)}) %collective-permute-start.8) | collective-permute-done | bytes 8224 | tf_op jit(solution)/shard_map/ppermute | solution.py:43
  36.8 0.6 place_samples.1
  37.3 20.5 %all_to_all.5.arrived_ref = f32[16,152,128]{2,1,0:T(8,128)S(1)} all-to-all(f32[16,152,128]{2,1,0:T(8,128)S(1)} %place_samples.1), channel_id=1, replica_groups=mesh['ty'=4,'half'=2,'within'=4] {'ty','within'}, dimensions={0} | all-to-all | bytes 2490368 | tf_op jit(solution)/shard_map/all_to_all | solution.py:510
  57.8 1.5 %filter_series.1 = f32[73,4,8,128]{3,2,1,0:T(8,128)} custom-call(bf16[80,240]{1,0:T(8,128)(2,1)S(1)} %split_matrix.1.matrix_ref, f32[16,152,128]{2,1,0:T(8,128)S(1)} %all_to_all.5.arrived_ref), custom_call_target="tpu_custom_call" | custom-call | flops 157286400 | bytes 3000000 | tf_op jit(solution)/shard_map/filter_series/pallas_call | solution.py:520
  (45 shorter events, 0.3 us)
Async XLA Ops:
  0.8 7.4 %copy-start.5 = (s32[1,8]{1,0:T(1,128)S(1)}, s32[1,8]{1,0:T(1,128)}, u32[]{:S(2)}) copy-start(s32[1,8]{1,0:T(1,128)} %leavers_ref.1) | copy-start | bytes 100
  0.8 8.0 %copy-start = (f32[2,3,128,128]{3,2,1,0:T(8,128)S(1)}, f32[2,3,128,128]{3,2,1,0:T(8,128)}, u32[]{:S(2)}) copy-start(f32[2,3,128,128]{3,2,1,0:T(8,128)} %velocity_ref.1) | copy-start | bytes 1179652
  2.1 7.2 %collective-permute-start.1 = (f32[148,128]{1,0:T(8,128)S(1)}, f32[148,128]{1,0:T(8,128)S(1)}, u32[]{:S(2)}, u32[]{:S(2)}) collective-permute-start(f32[148,128]{1,0:T(8,128)S(1)} %get-tuple-element.39), channel_id=1, source_target_pairs={{0,8},{8,0},{16,24},{24,16},{1,9},{9,1},{17,25},{25,17},{2,10},{10... | collective-permute-start | bytes 227336 | tf_op jit(solution)/shard_map/ppermute | solution.py:37
  2.6 6.6 %collective-permute-start = (f32[148,128]{1,0:T(8,128)S(1)}, f32[148,128]{1,0:T(8,128)S(1)}, u32[]{:S(2)}, u32[]{:S(2)}) collective-permute-start(f32[148,128]{1,0:T(8,128)S(1)} %get-tuple-element.40), channel_id=1, source_target_pairs={{0,24},{8,16},{16,8},{24,0},{1,25},{9,17},{17,9},{25,1},{2,26},{10... | collective-permute-start | bytes 227336 | tf_op jit(solution)/shard_map/ppermute | solution.py:38
  5.2 7.7 %copy-start.6 = (s32[512,1]{0,1:T(1,128)S(1)}, s32[512,1]{0,1:T(1,128)}, u32[]{:S(2)}) copy-start(s32[512,1]{0,1:T(1,128)} %param.12) | copy-start | bytes 6148
  5.2 7.7 %copy-start.3 = (f32[73,73]{1,0:T(8,128)S(1)}, f32[73,73]{1,0:T(8,128)}, u32[]{:S(2)}) copy-start(f32[73,73]{1,0:T(8,128)} %matrix_ref.1) | copy-start | bytes 63952
  5.3 8.1 %copy-start.2 = (s32[2,4,2,512]{3,2,1,0:T(2,128)S(1)}, s32[2,4,2,512]{3,2,1,0:T(2,128)}, u32[]{:S(2)}) copy-start(s32[2,4,2,512]{3,2,1,0:T(2,128)} %cells_ref.3) | copy-start | bytes 98308
  5.5 27.1 %collective-permute-start.10 = (f32[426,128]{1,0:T(8,128)S(1)}, f32[426,128]{1,0:T(8,128)S(1)}, u32[]{:S(2)}, u32[]{:S(2)}) collective-permute-start(f32[426,128]{1,0:T(8,128)S(1)} %reshape.125), channel_id=1, source_target_pairs={{0,4},{4,0},{1,5},{5,1},{2,6},{6,2},{3,7},{7,3},{8,12},{12,8},{9,1... | collective-permute-start | bytes 654344 | tf_op jit(solution)/shard_map/ppermute | solution.py:43
  9.3 6.0 %collective-permute-start.3 = (f32[160,128]{1,0:T(8,128)S(1)}, f32[160,128]{1,0:T(8,128)S(1)}, u32[]{:S(2)}, u32[]{:S(2)}) collective-permute-start(f32[160,128]{1,0:T(8,128)S(1)} %get-tuple-element.37), channel_id=1, source_target_pairs={{0,1},{1,0},{2,3},{3,2},{4,5},{5,4},{6,7},{7,6},{8,9},{9,8},{10,11... | collective-permute-start | bytes 245768 | tf_op jit(solution)/shard_map/ppermute | solution.py:37
  10.9 7.1 %collective-permute-start.2 = (f32[160,128]{1,0:T(8,128)S(1)}, f32[160,128]{1,0:T(8,128)S(1)}, u32[]{:S(2)}, u32[]{:S(2)}) collective-permute-start(f32[160,128]{1,0:T(8,128)S(1)} %get-tuple-element.38), channel_id=1, source_target_pairs={{0,7},{1,2},{2,1},{3,4},{4,3},{5,6},{6,5},{7,0},{8,15},{9,10},{10,... | collective-permute-start | bytes 245768 | tf_op jit(solution)/shard_map/ppermute | solution.py:38
  13.4 4.7 %copy-start.4 = (f32[2,512]{1,0:T(2,128)S(1)}, f32[2,512]{1,0:T(2,128)}, u32[]{:S(2)}) copy-start(f32[2,512]{1,0:T(2,128)} %point_ref.1) | copy-start | bytes 12292
  18.1 10.3 %copy-start.1 = (f32[2,71,512]{2,0,1:T(2,128)S(1)}, f32[2,71,512]{2,0,1:T(2,128)}, u32[]{:S(2)}) copy-start(f32[2,71,512]{2,0,1:T(2,128)} %param.10) | copy-start | bytes 872452
  18.9 6.7 %collective-permute-start.5 = (f32[4,128]{1,0:T(4,128)S(1)}, f32[4,128]{1,0:T(4,128)S(1)}, u32[]{:S(2)}, u32[]{:S(2)}) collective-permute-start(f32[4,128]{1,0:T(4,128)S(1)} %get-tuple-element.20), channel_id=1, source_target_pairs={{0,8},{8,0},{16,24},{24,16},{1,9},{9,1},{17,25},{25,17},{2,10},{10... | collective-permute-start | bytes 6152 | tf_op jit(solution)/shard_map/ppermute | solution.py:37
  19.0 6.7 %collective-permute-start.4 = (f32[4,128]{1,0:T(4,128)S(1)}, f32[4,128]{1,0:T(4,128)S(1)}, u32[]{:S(2)}, u32[]{:S(2)}) collective-permute-start(f32[4,128]{1,0:T(4,128)S(1)} %get-tuple-element.20), channel_id=1, source_target_pairs={{0,24},{8,16},{16,8},{24,0},{1,25},{9,17},{17,9},{25,1},{2,26},{10... | collective-permute-start | bytes 6152 | tf_op jit(solution)/shard_map/ppermute | solution.py:38
  19.7 13.0 %collective-permute-start.9 = (f32[148,128]{1,0:T(8,128)S(1)}, f32[148,128]{1,0:T(8,128)S(1)}, u32[]{:S(2)}, u32[]{:S(2)}) collective-permute-start(f32[148,128]{1,0:T(8,128)S(1)} %pad_maximum_fusion.6.past_ref), channel_id=1, source_target_pairs={{0,4},{4,0},{1,5},{5,1},{2,6},{6,2},{3,7},{7,3},{8,12},{12,8},{9,1... | collective-permute-start | bytes 227336 | tf_op jit(solution)/shard_map/ppermute | solution.py:43
  25.7 3.7 %collective-permute-start.7 = (f32[4,128]{1,0:T(4,128)S(1)}, f32[4,128]{1,0:T(4,128)S(1)}, u32[]{:S(2)}, u32[]{:S(2)}) collective-permute-start(f32[4,128]{1,0:T(4,128)S(1)} %select_select_fusion), channel_id=1, source_target_pairs={{0,1},{1,0},{2,3},{3,2},{4,5},{5,4},{6,7},{7,6},{8,9},{9,8},{10,11... | collective-permute-start | bytes 6152 | tf_op jit(solution)/shard_map/ppermute | solution.py:37
  25.7 6.3 %collective-permute-start.6 = (f32[4,128]{1,0:T(4,128)S(1)}, f32[4,128]{1,0:T(4,128)S(1)}, u32[]{:S(2)}, u32[]{:S(2)}) collective-permute-start(f32[4,128]{1,0:T(4,128)S(1)} %select_select_fusion), channel_id=1, source_target_pairs={{0,7},{1,2},{2,1},{3,4},{4,3},{5,6},{6,5},{7,0},{8,15},{9,10},{10,... | collective-permute-start | bytes 6152 | tf_op jit(solution)/shard_map/ppermute | solution.py:38
  32.2 4.6 %collective-permute-start.8 = (f32[4,512]{1,0:T(4,128)S(1)}, f32[4,512]{1,0:T(4,128)S(1)}, u32[]{:S(2)}, u32[]{:S(2)}) collective-permute-start(f32[4,512]{1,0:T(4,128)S(1)} %fusion.7.samples_ref), channel_id=1, source_target_pairs={{0,4},{4,0},{1,5},{5,1},{2,6},{6,2},{3,7},{7,3},{8,12},{12,8},{9,1... | collective-permute-start | bytes 24584 | tf_op jit(solution)/shard_map/ppermute | solution.py:43
